TPU v7x, 256 devices: a whole 4x4x8 slice. The times are simulated.
256 devices in a mesh: tm: 8 (over x, y_lo), space: 32 (over z, y_hi, core).
Axes of the slice: x: 4, y: 4 (y_hi: 2, y_lo: 2; y = y_hi * 2 + y_lo), z: 8, core: 2. Of those that a mesh axis runs over, the one named last changes fastest.
Arguments:
- source: float32 [16, 4096, 5, 128], P('tm', 'space'), may hold values from -6 to 6
- terminal: float32 [4096, 5, 128], P('space'), may hold values from -6 to 6
- jacobian: float32 [8, 4096, 5, 5, 128], P('tm', 'space')
- face_coef: float32 [4096, 6, 128], P('space'), may hold values from 0.1 to 0.5
- cell_coef: float32 [4096, 128], P('space'), may hold values from 0.1 to 0.5
- neighbours: int32 [4096, 6], P('space'), may hold values from 0 to 160, as said below
- send_blocks: int32 [32, 2, 16], P('space'), may hold values from 0 to 127, as said below
- live_count: int32 [32], P('space'), may hold values from 64 to 128, as said below
- volume: float32 [4096, 128], P('space'), may hold values from 0.5 to 2
- shape_field: float32 [4096, 5, 128], P('space'), may hold values from -6 to 6
- weights: float32 [16], P('tm'), may hold values from 0.25 to 4
Outputs:
- adjoint: float32 [16, 4096, 5, 128], P('tm', 'space')
- sensitivity: float32 [4096], P('space')
Inputs may be any that keep to these rules, and one draw needn't show every extreme that they name: `live_count`: some device has 128 live blocks in every draw. `send_blocks`: each index names a live block of its own device. `neighbours`: a slot below 128 names a live block of the same device; 128 to 159 name received blocks, those of the lower device first; 160 is an empty slot.
All inputs are finite; a program needn't handle non-finite values.
Results may differ from a plain program's by a relative error of at most 0.00016.
Values sent between devices are 32-bit elements; how exact they have to be, the bound alone decides.
No kernel may reach another device: no remote copies, remote signals or barrier semaphores. Data moves between devices by JAX's collectives and lax.ppermute only.
A program may use at most 64 MiB of HBM per device.

v0:
```python
import jax
import jax.numpy as jnp
from jax import lax
from jax.sharding import PartitionSpec as P

ITERS = 3


inverse_step = 6.0


def from_behind(value, axis, steps):
    count = lax.axis_size(axis)
    first, last = (max(0, -steps), min(count, count - steps))
    return lax.ppermute(value, axis, [(source, source + steps) for source in range(first, last)])


def copy_for_each(x, axis):
    copies = jnp.broadcast_to(x, (lax.axis_size(axis), *x.shape))
    return lax.all_to_all(copies, axis, split_axis=0, concat_axis=0, tiled=True)


def taken_together(x, axis):
    return copy_for_each(x, axis).sum(axis=0)


def pad_local(field):
    return jnp.pad(field, ((0, 0), (0, 0), (1, 1)))


def make_operator(face_coef, cell_coef, neighbours, mass, to_lower, to_higher, sides):
    highest = lax.Precision.HIGHEST
    along_coef = cell_coef[:, None, :]

    def operate(field, jac):
        from_lower = from_behind(field[to_higher], "space", 1)
        from_higher = from_behind(field[to_lower], "space", -1)
        blank = jnp.zeros((1,) + field.shape[1:], jnp.float32)
        extended = jnp.concatenate([field, from_lower, from_higher, blank], axis=0)
        gathered = extended[neighbours]
        coupled = jnp.einsum("bnc,bnkc->bkc", face_coef, gathered, precision=highest)
        own = jnp.einsum("bijc,bic->bjc", jac, field, precision=highest)
        widened = sides(field)
        beside = widened[:, :, :-2] + widened[:, :, 2:]
        return mass * field + own - coupled - along_coef * beside

    return operate


def make_precond(jac, mass, face_coef, cell_coef):
    diagonal = jnp.stack([jac[:, k, k, :] for k in range(jac.shape[1])], axis=1)
    return 1.0 / (
        mass + diagonal + jnp.sum(face_coef, axis=1)[:, None, :] + 2.0 * cell_coef[:, None, :]
    )


def sweep_levels(incoming, sources, jac, precond, mass, live, operate):

    def level_step(later, level_source):
        rhs = level_source + mass * later
        field = later
        for sweep in range(ITERS):
            field = live * (field + precond * (rhs - operate(field, jac)))
        return (field, field)

    return lax.scan(level_step, incoming, sources, reverse=True)


def per_device(
    source,
    terminal,
    jacobian,
    face_coef,
    cell_coef,
    neighbours,
    send_blocks,
    live_count,
    volume,
    shape_field,
    weights,
):
    nblocks = terminal.shape[0]
    live = (lax.iota(jnp.int32, nblocks) < live_count[0]).astype(jnp.float32)[:, None, None]
    mass = (inverse_step * volume)[:, None, :]
    to_lower = send_blocks[0, 0]
    to_higher = send_blocks[0, 1]
    rounds = lax.axis_size("tm")
    jac = jacobian[0]
    precond = make_precond(jac, mass, face_coef, cell_coef)
    operate = make_operator(face_coef, cell_coef, neighbours, mass, to_lower, to_higher, pad_local)

    def slab(incoming):
        return sweep_levels(incoming, source, jac, precond, mass, live, operate)

    is_last = lax.axis_index("tm") == rounds - 1
    start = live * terminal

    def turn(step_index, incoming):
        first, fields = slab(incoming)
        moved = from_behind(first, "tm", -1)
        return jnp.where(is_last, start, moved)

    incoming = lax.fori_loop(0, rounds - 1, turn, start)
    first, fields = slab(incoming)
    sensitivity = taken_together(
        jnp.sum(weights[:, None] * jnp.sum(fields * shape_field[None], axis=(2, 3)), axis=0), "tm"
    )
    return (fields, sensitivity)


def solution(mesh):
    return jax.shard_map(
        per_device,
        mesh=mesh,
        in_specs=(
            P("tm", "space", None, None),
            P("space", None, None),
            P("tm", "space", None, None, None),
            P("space", None, None),
            P("space", None),
            P("space", None),
            P("space", None, None),
            P("space"),
            P("space", None),
            P("space", None, None),
            P("tm"),
        ),
        out_specs=(P("tm", "space", None, None), P("space")),
        check_vma=False,
    )
```

profile of v0, /device:TPU:113, one launch (start us, length us, event | category | flops | bytes accessed | tf_op | source)
XLA Modules:
  0.0 1305.5 jit_solution(17971713993202420043)
XLA Ops:
  16.2 1117.3 %while.60 = (s32[]{:T(128)}, f32[128,5,128]{2,1,0:T(8,128)S(1)}, pred[]{:T(512)}, f32[2,128,5,128]{3,2,1,0:T(8,128)}, f32[128,1,128]{2,0,1:T(8,128)S(1)}, /*inde...) while((s32[]{:T(128)}, f32[128,5,128]{2,1,0:T(8,128)S(1)}, ...), condition=%wide.region_4.5_spmd.clone, body=%wide.region_1.4_spmd.clone.sunk | while | flops 8797413 | bytes 66983056 | solution.py:103
  17.5 145.3 %while.62 = (s32[]{:T(128)}, f32[128,5,128]{2,1,0:T(8,128)S(1)}, f32[128,1,1]{0,2,1:T(1,128)}, f32[2,128,5,128]{3,2,1,0:T(8,128)}, f32[128,1,128]{2,0,1:T(8,128)...) while((s32[]{:T(128)}, f32[128,5,128]{2,1,0:T(8,128)S(1)}, ...), condition=%wide.region_3.3_spmd, body=%wide.region_2.2_spmd.sunk | while | flops 8715235 | bytes 64688432 | solution.py:66
  21.9 6.6 collective-permute-start.7
  93.9 7.2 collective-permute-start.7
  164.1 10.0 collective-permute-done.12
  176.4 145.3 %while.62 = (s32[]{:T(128)}, f32[128,5,128]{2,1,0:T(8,128)S(1)}, f32[128,1,1]{0,2,1:T(1,128)}, f32[2,128,5,128]{3,2,1,0:T(8,128)}, f32[128,1,128]{2,0,1:T(8,128)...) while((s32[]{:T(128)}, f32[128,5,128]{2,1,0:T(8,128)S(1)}, ...), condition=%wide.region_3.3_spmd, body=%wide.region_2.2_spmd.sunk | while | flops 8715235 | bytes 64688432 | solution.py:66
  180.2 7.2 collective-permute-start.7
  252.9 7.2 collective-permute-start.7
  323.1 10.1 collective-permute-done.12
  335.6 145.3 %while.62 = (s32[]{:T(128)}, f32[128,5,128]{2,1,0:T(8,128)S(1)}, f32[128,1,1]{0,2,1:T(1,128)}, f32[2,128,5,128]{3,2,1,0:T(8,128)}, f32[128,1,128]{2,0,1:T(8,128)...) while((s32[]{:T(128)}, f32[128,5,128]{2,1,0:T(8,128)S(1)}, ...), condition=%wide.region_3.3_spmd, body=%wide.region_2.2_spmd.sunk | while | flops 8715235 | bytes 64688432 | solution.py:66
  339.3 7.2 collective-permute-start.7
  412.0 7.2 collective-permute-start.7
  482.2 10.9 collective-permute-done.12
  495.4 145.3 %while.62 = (s32[]{:T(128)}, f32[128,5,128]{2,1,0:T(8,128)S(1)}, f32[128,1,1]{0,2,1:T(1,128)}, f32[2,128,5,128]{3,2,1,0:T(8,128)}, f32[128,1,128]{2,0,1:T(8,128)...) while((s32[]{:T(128)}, f32[128,5,128]{2,1,0:T(8,128)S(1)}, ...), condition=%wide.region_3.3_spmd, body=%wide.region_2.2_spmd.sunk | while | flops 8715235 | bytes 64688432 | solution.py:66
  499.2 7.2 collective-permute-start.7
  571.8 7.2 collective-permute-start.7
  642.0 10.9 collective-permute-done.12
  655.3 145.3 %while.62 = (s32[]{:T(128)}, f32[128,5,128]{2,1,0:T(8,128)S(1)}, f32[128,1,1]{0,2,1:T(1,128)}, f32[2,128,5,128]{3,2,1,0:T(8,128)}, f32[128,1,128]{2,0,1:T(8,128)...) while((s32[]{:T(128)}, f32[128,5,128]{2,1,0:T(8,128)S(1)}, ...), condition=%wide.region_3.3_spmd, body=%wide.region_2.2_spmd.sunk | while | flops 8715235 | bytes 64688432 | solution.py:66
  659.0 7.2 collective-permute-start.7
  731.7 7.2 collective-permute-start.7
  801.9 10.9 collective-permute-done.12
  815.1 145.3 %while.62 = (s32[]{:T(128)}, f32[128,5,128]{2,1,0:T(8,128)S(1)}, f32[128,1,1]{0,2,1:T(1,128)}, f32[2,128,5,128]{3,2,1,0:T(8,128)}, f32[128,1,128]{2,0,1:T(8,128)...) while((s32[]{:T(128)}, f32[128,5,128]{2,1,0:T(8,128)S(1)}, ...), condition=%wide.region_3.3_spmd, body=%wide.region_2.2_spmd.sunk | while | flops 8715235 | bytes 64688432 | solution.py:66
  818.9 7.2 collective-permute-start.7
  891.5 7.2 collective-permute-start.7
  961.7 10.9 collective-permute-done.12
  975.0 145.3 %while.62 = (s32[]{:T(128)}, f32[128,5,128]{2,1,0:T(8,128)S(1)}, f32[128,1,1]{0,2,1:T(1,128)}, f32[2,128,5,128]{3,2,1,0:T(8,128)}, f32[128,1,128]{2,0,1:T(8,128)...) while((s32[]{:T(128)}, f32[128,5,128]{2,1,0:T(8,128)S(1)}, ...), condition=%wide.region_3.3_spmd, body=%wide.region_2.2_spmd.sunk | while | flops 8715235 | bytes 64688432 | solution.py:66
  978.7 7.2 collective-permute-start.7
  1051.4 7.2 collective-permute-start.7
  1121.6 10.9 collective-permute-done.12
  1134.7 155.2 %while.61 = (s32[]{:T(128)}, f32[128,5,128]{2,1,0:T(8,128)S(1)}, f32[2,128,5,128]{3,2,1,0:T(8,128)}, f32[2,128,5,128]{3,2,1,0:T(8,128)}, f32[128,1,128]{2,0,1:T(...) while((s32[]{:T(128)}, f32[128,5,128]{2,1,0:T(8,128)S(1)}, ...), condition=%wide.region_6.7_spmd.clone, body=%wide.region_5.6_spmd.clone.sunk | while | flops 8715491 | bytes 66577184 | solution.py:66
  1139.0 7.2 collective-permute-start.1
  1216.6 7.2 collective-permute-start.1
  (1444 shorter events, 1107.8 us)
Async XLA Ops:
  18.1 14.1 %collective-permute-start.6 = (f32[16,5,128]{2,1,0:T(8,128)S(1)}, f32[16,5,128]{2,1,0:T(8,128)S(1)}, u32[]{:S(2)}, u32[]{:S(2)}) collective-permute-start(f32[16,5,128]{2,1,0:T(8,128)S(1)} %gather_fusion.9), channel_id=1, source_target_pairs={{1,0},{2,1},{3,2},{4,3},{5,4},{6,5},{7,6},{8,7},{9,8},{10,9},{11,1... | collective-permute-start | bytes 122888 | tf_op jit(solution)/shard_map/while/body/eval_jaxpr/while/body/eval_jaxpr/ppermute | solution.py:15
  90.8 14.1 %collective-permute-start.6 = (f32[16,5,128]{2,1,0:T(8,128)S(1)}, f32[16,5,128]{2,1,0:T(8,128)S(1)}, u32[]{:S(2)}, u32[]{:S(2)}) collective-permute-start(f32[16,5,128]{2,1,0:T(8,128)S(1)} %gather_fusion.9), channel_id=1, source_target_pairs={{1,0},{2,1},{3,2},{4,3},{5,4},{6,5},{7,6},{8,7},{9,8},{10,9},{11,1... | collective-permute-start | bytes 122888 | tf_op jit(solution)/shard_map/while/body/eval_jaxpr/while/body/eval_jaxpr/ppermute | solution.py:15
  93.9 10.9 collective-permute-start.7
  162.8 11.3 collective-permute-start.12
  177.0 14.1 %collective-permute-start.6 = (f32[16,5,128]{2,1,0:T(8,128)S(1)}, f32[16,5,128]{2,1,0:T(8,128)S(1)}, u32[]{:S(2)}, u32[]{:S(2)}) collective-permute-start(f32[16,5,128]{2,1,0:T(8,128)S(1)} %gather_fusion.9), channel_id=1, source_target_pairs={{1,0},{2,1},{3,2},{4,3},{5,4},{6,5},{7,6},{8,7},{9,8},{10,9},{11,1... | collective-permute-start | bytes 122888 | tf_op jit(solution)/shard_map/while/body/eval_jaxpr/while/body/eval_jaxpr/ppermute | solution.py:15
  180.2 10.9 collective-permute-start.7
  249.7 14.1 %collective-permute-start.6 = (f32[16,5,128]{2,1,0:T(8,128)S(1)}, f32[16,5,128]{2,1,0:T(8,128)S(1)}, u32[]{:S(2)}, u32[]{:S(2)}) collective-permute-start(f32[16,5,128]{2,1,0:T(8,128)S(1)} %gather_fusion.9), channel_id=1, source_target_pairs={{1,0},{2,1},{3,2},{4,3},{5,4},{6,5},{7,6},{8,7},{9,8},{10,9},{11,1... | collective-permute-start | bytes 122888 | tf_op jit(solution)/shard_map/while/body/eval_jaxpr/while/body/eval_jaxpr/ppermute | solution.py:15
  252.9 10.9 collective-permute-start.7
  321.8 11.4 collective-permute-start.12
  336.2 14.1 %collective-permute-start.6 = (f32[16,5,128]{2,1,0:T(8,128)S(1)}, f32[16,5,128]{2,1,0:T(8,128)S(1)}, u32[]{:S(2)}, u32[]{:S(2)}) collective-permute-start(f32[16,5,128]{2,1,0:T(8,128)S(1)} %gather_fusion.9), channel_id=1, source_target_pairs={{1,0},{2,1},{3,2},{4,3},{5,4},{6,5},{7,6},{8,7},{9,8},{10,9},{11,1... | collective-permute-start | bytes 122888 | tf_op jit(solution)/shard_map/while/body/eval_jaxpr/while/body/eval_jaxpr/ppermute | solution.py:15
  408.8 14.1 %collective-permute-start.6 = (f32[16,5,128]{2,1,0:T(8,128)S(1)}, f32[16,5,128]{2,1,0:T(8,128)S(1)}, u32[]{:S(2)}, u32[]{:S(2)}) collective-permute-start(f32[16,5,128]{2,1,0:T(8,128)S(1)} %gather_fusion.9), channel_id=1, source_target_pairs={{1,0},{2,1},{3,2},{4,3},{5,4},{6,5},{7,6},{8,7},{9,8},{10,9},{11,1... | collective-permute-start | bytes 122888 | tf_op jit(solution)/shard_map/while/body/eval_jaxpr/while/body/eval_jaxpr/ppermute | solution.py:15
  480.9 12.2 collective-permute-start.12
  496.0 14.1 %collective-permute-start.6 = (f32[16,5,128]{2,1,0:T(8,128)S(1)}, f32[16,5,128]{2,1,0:T(8,128)S(1)}, u32[]{:S(2)}, u32[]{:S(2)}) collective-permute-start(f32[16,5,128]{2,1,0:T(8,128)S(1)} %gather_fusion.9), channel_id=1, source_target_pairs={{1,0},{2,1},{3,2},{4,3},{5,4},{6,5},{7,6},{8,7},{9,8},{10,9},{11,1... | collective-permute-start | bytes 122888 | tf_op jit(solution)/shard_map/while/body/eval_jaxpr/while/body/eval_jaxpr/ppermute | solution.py:15
  499.2 10.9 collective-permute-start.7
  568.7 14.1 %collective-permute-start.6 = (f32[16,5,128]{2,1,0:T(8,128)S(1)}, f32[16,5,128]{2,1,0:T(8,128)S(1)}, u32[]{:S(2)}, u32[]{:S(2)}) collective-permute-start(f32[16,5,128]{2,1,0:T(8,128)S(1)} %gather_fusion.9), channel_id=1, source_target_pairs={{1,0},{2,1},{3,2},{4,3},{5,4},{6,5},{7,6},{8,7},{9,8},{10,9},{11,1... | collective-permute-start | bytes 122888 | tf_op jit(solution)/shard_map/while/body/eval_jaxpr/while/body/eval_jaxpr/ppermute | solution.py:15
  571.8 10.9 collective-permute-start.7
  640.7 12.2 collective-permute-start.12
  655.9 14.1 %collective-permute-start.6 = (f32[16,5,128]{2,1,0:T(8,128)S(1)}, f32[16,5,128]{2,1,0:T(8,128)S(1)}, u32[]{:S(2)}, u32[]{:S(2)}) collective-permute-start(f32[16,5,128]{2,1,0:T(8,128)S(1)} %gather_fusion.9), channel_id=1, source_target_pairs={{1,0},{2,1},{3,2},{4,3},{5,4},{6,5},{7,6},{8,7},{9,8},{10,9},{11,1... | collective-permute-start | bytes 122888 | tf_op jit(solution)/shard_map/while/body/eval_jaxpr/while/body/eval_jaxpr/ppermute | solution.py:15
  728.5 14.1 %collective-permute-start.6 = (f32[16,5,128]{2,1,0:T(8,128)S(1)}, f32[16,5,128]{2,1,0:T(8,128)S(1)}, u32[]{:S(2)}, u32[]{:S(2)}) collective-permute-start(f32[16,5,128]{2,1,0:T(8,128)S(1)} %gather_fusion.9), channel_id=1, source_target_pairs={{1,0},{2,1},{3,2},{4,3},{5,4},{6,5},{7,6},{8,7},{9,8},{10,9},{11,1... | collective-permute-start | bytes 122888 | tf_op jit(solution)/shard_map/while/body/eval_jaxpr/while/body/eval_jaxpr/ppermute | solution.py:15
  800.6 12.2 collective-permute-start.12
  815.7 14.1 %collective-permute-start.6 = (f32[16,5,128]{2,1,0:T(8,128)S(1)}, f32[16,5,128]{2,1,0:T(8,128)S(1)}, u32[]{:S(2)}, u32[]{:S(2)}) collective-permute-start(f32[16,5,128]{2,1,0:T(8,128)S(1)} %gather_fusion.9), channel_id=1, source_target_pairs={{1,0},{2,1},{3,2},{4,3},{5,4},{6,5},{7,6},{8,7},{9,8},{10,9},{11,1... | collective-permute-start | bytes 122888 | tf_op jit(solution)/shard_map/while/body/eval_jaxpr/while/body/eval_jaxpr/ppermute | solution.py:15
  888.4 14.1 %collective-permute-start.6 = (f32[16,5,128]{2,1,0:T(8,128)S(1)}, f32[16,5,128]{2,1,0:T(8,128)S(1)}, u32[]{:S(2)}, u32[]{:S(2)}) collective-permute-start(f32[16,5,128]{2,1,0:T(8,128)S(1)} %gather_fusion.9), channel_id=1, source_target_pairs={{1,0},{2,1},{3,2},{4,3},{5,4},{6,5},{7,6},{8,7},{9,8},{10,9},{11,1... | collective-permute-start | bytes 122888 | tf_op jit(solution)/shard_map/while/body/eval_jaxpr/while/body/eval_jaxpr/ppermute | solution.py:15
  960.4 12.2 collective-permute-start.12
  975.6 14.1 %collective-permute-start.6 = (f32[16,5,128]{2,1,0:T(8,128)S(1)}, f32[16,5,128]{2,1,0:T(8,128)S(1)}, u32[]{:S(2)}, u32[]{:S(2)}) collective-permute-start(f32[16,5,128]{2,1,0:T(8,128)S(1)} %gather_fusion.9), channel_id=1, source_target_pairs={{1,0},{2,1},{3,2},{4,3},{5,4},{6,5},{7,6},{8,7},{9,8},{10,9},{11,1... | collective-permute-start | bytes 122888 | tf_op jit(solution)/shard_map/while/body/eval_jaxpr/while/body/eval_jaxpr/ppermute | solution.py:15
  978.7 10.9 collective-permute-start.7
  1048.2 14.1 %collective-permute-start.6 = (f32[16,5,128]{2,1,0:T(8,128)S(1)}, f32[16,5,128]{2,1,0:T(8,128)S(1)}, u32[]{:S(2)}, u32[]{:S(2)}) collective-permute-start(f32[16,5,128]{2,1,0:T(8,128)S(1)} %gather_fusion.9), channel_id=1, source_target_pairs={{1,0},{2,1},{3,2},{4,3},{5,4},{6,5},{7,6},{8,7},{9,8},{10,9},{11,1... | collective-permute-start | bytes 122888 | tf_op jit(solution)/shard_map/while/body/eval_jaxpr/while/body/eval_jaxpr/ppermute | solution.py:15
  1120.3 12.2 collective-permute-start.12
  1135.9 14.7 %collective-permute-start = (f32[16,5,128]{2,1,0:T(8,128)}, f32[16,5,128]{2,1,0:T(8,128)S(1)}, u32[]{:S(2)}, u32[]{:S(2)}) collective-permute-start(f32[16,5,128]{2,1,0:T(8,128)} %gather_fusion), channel_id=1, source_target_pairs={{1,0},{2,1},{3,2},{4,3},{5,4},{6,5},{7,6},{8,7},{9,8},{10,9},{11,1... | collective-permute-start | bytes 122888 | tf_op jit(solution)/shard_map/while/body/eval_jaxpr/ppermute | solution.py:15
  1139.0 11.6 collective-permute-start.1
  1213.4 14.7 %collective-permute-start = (f32[16,5,128]{2,1,0:T(8,128)}, f32[16,5,128]{2,1,0:T(8,128)S(1)}, u32[]{:S(2)}, u32[]{:S(2)}) collective-permute-start(f32[16,5,128]{2,1,0:T(8,128)} %gather_fusion), channel_id=1, source_target_pairs={{1,0},{2,1},{3,2},{4,3},{5,4},{6,5},{7,6},{8,7},{9,8},{10,9},{11,1... | collective-permute-start | bytes 122888 | tf_op jit(solution)/shard_map/while/body/eval_jaxpr/ppermute | solution.py:15
  1216.6 11.6 collective-permute-start.1
  1293.5 11.4 all-to-all-start
  (444 other events, 2517.1 us)
where the time goes:
time: 1320 us; the launch traced here: 1310 us
  local copies, waits for them, and re-layouts  369 us (28%)
  starting transfers between devices  358 us (27%)
  other arithmetic  336 us (25%)
  waiting for transfers between devices  234 us (18%)
    ppermute x103, starting transfers between devices, from_behind(): lax.ppermute(value, axis, [(source, source + steps) for source in range(f...  352 us
    ppermute x103, waiting for transfers between devices, from_behind(): lax.ppermute(value, axis, [(source, source + steps) for source in range(f...  231 us
    gather x48, local copies, waits for them, and re-layouts, operate(): gathered = extended[neighbours]  174 us
    dot_general x48, other arithmetic, operate(): jnp.einsum('bnc,bnkc->bkc', face_coef, gathered, precision=highest)  133 us
    dot_general x48, other arithmetic, operate(): own = jnp.einsum('bijc,bic->bjc', jac, field, precision=highest)  96.4 us
    gather x48, local copies, waits for them, and re-layouts, operate(): from_lower = from_behind(field[to_higher], 'space', 1)  75.9 us
    gather x48, local copies, waits for them, and re-layouts, operate(): from_higher = from_behind(field[to_lower], 'space', -1)  61.4 us
    mul x48, other arithmetic, level_step(): field = live * (field + precond * (rhs - operate(field, jac)))  49.9 us
  transfers between devices with their start and end apart: 104, of which 40 were waited for; matrix products, arithmetic and copies ran while one was open for 12% of the time, Pallas kernels for 0%

commit v1 on v0

v1 whole, which is shorter than its diff:
```python
import jax
import jax.numpy as jnp
from jax import lax
from jax.experimental import pallas as pl
from jax.experimental.pallas import tpu as pltpu
from jax.sharding import PartitionSpec as P

NB = 128
COMP = 5
NEI = 6
HALO = 16
LANES = 128
STEP = 8
ZERO = 2 * NB + 2 * HALO
ROWS = ZERO + 8
inverse_step = 6.0

FACE, PRE, SRC_LATE, SRC_EARLY, MASS, TILES = 5, 6, 7, 8, 9, 10

VMEM = pl.BlockSpec(memory_space=pltpu.VMEM)
SMEM = pl.BlockSpec(memory_space=pltpu.SMEM)
PARAMS = pltpu.CompilerParams(vmem_limit_bytes=40 << 20)
F32 = jnp.float32


def shape(*dims):
    return jax.ShapeDtypeStruct(dims, F32)


def prep_kernel(live_ref, jac, source, face, cell, volume, out):
    count = live_ref[0]
    lane = lax.broadcasted_iota(jnp.int32, (1, LANES), 1)
    row = lax.broadcasted_iota(jnp.int32, (COMP, LANES), 0)
    blank = jnp.zeros((8, LANES), F32)

    def block(b, carry):
        mass = inverse_step * volume[pl.ds(b, 1), :]
        along = cell[pl.ds(b, 1), :]
        faces = face[b]
        total = jnp.sum(faces, axis=0, keepdims=True)
        diagonal = jnp.zeros((COMP, LANES), F32)
        for i in range(COMP):
            diagonal = jnp.where(row == i, jac[b, i], diagonal)
        live = jnp.where(b < count, 1.0, 0.0).astype(F32)
        pre = live * (1.0 / (mass + diagonal + total + 2.0 * along))
        for i in range(TILES):
            out[b, i] = blank
        for i in range(COMP):
            keep = live - pre * (mass + jac[b, i])
            out[b, i, 0:COMP] = jnp.where(row == i, keep, -pre * jac[b, i])
        out[b, FACE, 0:NEI] = faces
        out[b, FACE, NEI : NEI + 1] = jnp.where(lane == 0, 0.0, along)
        out[b, FACE, NEI + 1 : NEI + 2] = jnp.where(lane == LANES - 1, 0.0, along)
        out[b, PRE, 0:COMP] = pre
        out[b, SRC_LATE, 0:COMP] = pre * source[1, b]
        out[b, SRC_EARLY, 0:COMP] = pre * source[0, b]
        out[b, MASS, 0:COMP] = pre * mass
        return carry

    lax.fori_loop(0, NB, block, 0)


def weighted(coef, c, picked):
    total = coef[c, FACE, 0:1] * picked[0]
    for k in range(1, NEI):
        total = total + coef[c, FACE, k : k + 1] * picked[k]
    return total


def advance(ext, b, coef, c, picked, fixed):
    x = ext[b]
    faces = weighted(coef, c, picked)
    faces = faces + coef[c, FACE, NEI : NEI + 1] * pltpu.roll(x, 1, 1)
    faces = faces + coef[c, FACE, NEI + 1 : NEI + 2] * pltpu.roll(x, LANES - 1, 1)
    value = fixed + coef[c, PRE] * faces
    for i in range(COMP):
        value = value + coef[c, i] * ext[b, i : i + 1]
    return value


def iterate(ext, table, coefs, fixed_of, put):
    for half in range(2):
        coef = coefs[half]

        def turn(g, carry, half=half, coef=coef):
            for s in range(STEP):
                c = g * STEP + s
                b = half * NB + c
                picked = [ext[table[b * NEI + k]] for k in range(NEI)]
                put(b, g, s, half, advance(ext, b, coef, c, picked, fixed_of(b, c, coef)))
            return carry

        lax.fori_loop(0, NB // STEP, turn, 0)


def send(ext, table, lists, coefs, fixed_of, outs):
    for half in range(2):
        coef = coefs[half]
        for i in range(HALO):
            c = lists[half * HALO + i]
            b = half * NB + c
            picked = []
            for k in range(NEI):
                slot = table[b * NEI + k]
                picked.append(ext[jnp.where(slot >= 2 * NB, ZERO, slot)])
            ahead = advance(ext, b, coef, c, picked, fixed_of(b, c, coef))
            outs[half][COMP * i : COMP * (i + 1)] = ext[b][0:COMP]
            j = HALO + i
            outs[half][COMP * j : COMP * (j + 1)] = ahead[0:COMP]


def first_kernel(table, lists, mine, other, coef0, coef1, x_out, msg0, msg1, ext):
    blank = jnp.zeros((8, LANES), F32)
    coefs = (coef0, coef1)
    ext[ZERO] = blank
    for half, source in enumerate((mine, other)):

        def turn(g, carry, half=half, source=source):
            for s in range(STEP):
                b = half * NB + g * STEP + s
                ext[b] = blank
                ext[b, 0:COMP] = source[g, COMP * s : COMP * (s + 1)]
                x_out[b] = ext[b]
            return carry

        lax.fori_loop(0, NB // STEP, turn, 0)
    send(ext, table, lists, coefs, lambda b, c, coef: coef[c, SRC_LATE] + coef[c, MASS] * ext[b], (msg0, msg1))


def make_step(stage):
    def kernel(table, lists, fixes, x_in, *refs):
        refs = list(refs)
        r_in = refs.pop(0) if stage else None
        got0, got1, rim, coef0, coef1 = refs[:5]
        del refs[:5]
        if stage < 2:
            x_out, r_out, msg0, msg1 = refs[:4]
            del refs[:4]
        lam = refs.pop(0) if stage else None
        ext, after = refs
        coefs = (coef0, coef1)
        blank = jnp.zeros((8, LANES), F32)
        ext[ZERO] = blank
        after[ZERO] = blank

        def copy(g, carry):
            for s in range(STEP):
                ext[g * STEP + s] = x_in[g * STEP + s]
            return carry

        lax.fori_loop(0, 2 * NB // STEP, copy, 0)
        for half, got in enumerate((got0, got1)):
            for i in range(HALO):
                h = half * HALO + i
                ext[2 * NB + h] = blank
                ext[2 * NB + h, 0:COMP] = got[COMP * i : COMP * (i + 1)]
                after[2 * NB + h] = blank
                j = HALO + i
                after[2 * NB + h, 0:COMP] = got[COMP * j : COMP * (j + 1)]
        for h in range(2 * HALO):
            total = rim[h, 0, 0:1] * ext[fixes[h * NEI]]
            for k in range(1, NEI):
                total = total + rim[h, 0, k : k + 1] * ext[fixes[h * NEI + k]]
            after[2 * NB + h] = after[2 * NB + h] + rim[h, 1] * total

        def store_lam(g, s, value):
            lam[g, COMP * s : COMP * (s + 1)] = value[0:COMP]

        if stage == 0:

            def fixed_a(b, c, coef):
                value = coef[c, SRC_LATE] + coef[c, MASS] * ext[b]
                r_out[b] = value
                return value

            def fixed_b(b, c, coef):
                return r_out[b]

        else:

            def fixed_a(b, c, coef):
                return r_in[b]

            if stage == 1:

                def fixed_b(b, c, coef):
                    value = coef[c, SRC_EARLY] + coef[c, MASS] * after[b]
                    r_out[b] = value
                    return value

            else:
                fixed_b = fixed_a

        def put_a(b, g, s, half, value):
            after[b] = value
            if stage == 1 and half == 0:
                store_lam(g, s, value)

        def put_b(b, g, s, half, value):
            if stage < 2:
                ext[b] = value
                x_out[b] = value
            elif half == 0:
                store_lam(g, s, value)

        iterate(ext, table, coefs, fixed_a, put_a)
        if stage < 2:
            iterate(after, table, coefs, fixed_b, put_b)
            send(ext, table, lists, coefs, lambda b, c, coef: r_out[b], (msg0, msg1))
        else:
            iterate(after, table, coefs, fixed_b, put_b)

    ext = pltpu.VMEM((ROWS, 8, LANES), F32)
    outs = []
    if stage < 2:
        outs += [shape(2 * NB, 8, LANES), shape(2 * NB, 8, LANES)]
        outs += [shape(2 * HALO * COMP, LANES), shape(2 * HALO * COMP, LANES)]
    if stage:
        outs += [shape(NB // STEP, STEP * COMP, LANES)]
    return pl.pallas_call(
        kernel,
        out_shape=outs,
        in_specs=[SMEM] * 3 + [VMEM] * (6 + (stage > 0)),
        out_specs=[VMEM] * len(outs),
        scratch_shapes=[ext, ext],
        compiler_params=PARAMS,
        name=f"step{stage}",
    )


def pick(small, index):
    hit = index[..., None] == lax.iota(jnp.int32, HALO)
    return jnp.sum(jnp.where(hit, small, 0), axis=-1)


def per_device(
    source,
    terminal,
    jacobian,
    face_coef,
    cell_coef,
    neighbours,
    send_blocks,
    live_count,
    volume,
    shape_field,
    weights,
):
    count = lax.axis_size("space")
    rounds = lax.axis_size("tm")
    core = lax.axis_index("space") % 2

    swap = [(d, d ^ 1) for d in range(count)]
    near, far = [], []
    for d in range(count):
        out = 2 * (d % 2) - 1
        if 0 <= d + out < count:
            near.append((d, d + out))
        if 0 <= d - 3 * out < count:
            far.append((d, d - 3 * out))

    def exchange(first, second):
        return lax.ppermute(first, "space", near), lax.ppermute(second, "space", far)

    mine = pl.pallas_call(
        prep_kernel,
        out_shape=shape(NB, TILES, 8, LANES),
        in_specs=[SMEM] + [VMEM] * 5,
        out_specs=VMEM,
        compiler_params=PARAMS,
        name="prep",
    )(live_count, jacobian[0], source, face_coef, cell_coef, volume)
    other = lax.ppermute(mine, "space", swap)

    lists_own = jnp.pad(send_blocks[0].reshape(2 * HALO, 1), ((0, NB - 2 * HALO), (0, 0)))
    ints = jnp.concatenate([neighbours, lists_own], axis=1)
    ints_other = lax.ppermute(ints, "space", swap)
    near_own = neighbours
    near_other = ints_other[:, :NEI]
    sends_other = ints_other[: 2 * HALO, NEI].reshape(2, HALO)
    low_own, high_own = send_blocks[0, 0], send_blocks[0, 1]
    low_other, high_other = sends_other[0], sends_other[1]
    is_low = core == 0
    out_own = jnp.where(is_low, low_own, high_own)
    in_own = jnp.where(is_low, high_own, low_own)
    out_other = jnp.where(is_low, high_other, low_other)
    in_other = jnp.where(is_low, low_other, high_other)

    def place(slots, base, outward, rim_base, partner_base, partner_list):
        side = (slots - NB) // HALO
        order = (slots - NB) % HALO
        across = partner_base + pick(partner_list, order)
        value = jnp.where(side == outward, rim_base + order, across)
        value = jnp.where(slots < NB, base + slots, value)
        return jnp.where(slots >= NB + 2 * HALO, ZERO, value)

    table = jnp.concatenate(
        [
            place(near_own, 0, core, 2 * NB, NB, in_other),
            place(near_other, NB, 1 - core, 2 * NB + HALO, 0, in_own),
        ]
    ).reshape(-1)
    lists = jnp.concatenate([out_own, out_other])

    def rim_message(coef, slots, chosen):
        tiles = coef[chosen, FACE : PRE + 1]
        picked = slots[chosen].astype(F32)
        return jnp.concatenate(
            [tiles, jnp.pad(picked, ((0, 0), (0, LANES - NEI)))[:, None, None, :].repeat(8, axis=2)], axis=1
        )

    rim0, rim1 = exchange(
        rim_message(mine, near_own, out_own), rim_message(other, near_other, out_other)
    )
    rim = jnp.concatenate([rim0[:, :2], rim1[:, :2]])

    def fix(message, outward, base, sent):
        slots = message[:, 2, 0, :NEI].astype(jnp.int32)
        side = (slots - NB) // HALO
        order = (slots - NB) % HALO
        valid = (slots >= NB) & (slots < NB + 2 * HALO) & (side == outward)
        return jnp.where(valid, base + pick(sent, order), ZERO)

    fixes = jnp.concatenate(
        [fix(rim0, 1 - core, 0, out_own), fix(rim1, core, NB, out_other)]
    ).reshape(-1)

    first_call = pl.pallas_call(
        first_kernel,
        out_shape=[
            shape(2 * NB, 8, LANES),
            shape(2 * HALO * COMP, LANES),
            shape(2 * HALO * COMP, LANES),
        ],
        in_specs=[SMEM] * 2 + [VMEM] * 4,
        out_specs=[VMEM] * 3,
        scratch_shapes=[pltpu.VMEM((ROWS, 8, LANES), F32)],
        compiler_params=PARAMS,
        name="first",
    )
    steps = [make_step(stage) for stage in range(3)]

    def slab(incoming):
        partner = lax.ppermute(incoming, "space", swap)
        x, *sent = first_call(table, lists, incoming, partner, mine, other)
        got = exchange(*sent)
        x, fixed, *sent = steps[0](table, lists, fixes, x, *got, rim, mine, other)
        got = exchange(*sent)
        x, fixed, *sent, late = steps[1](table, lists, fixes, x, fixed, *got, rim, mine, other)
        got = exchange(*sent)
        (early,) = steps[2](table, lists, fixes, x, fixed, *got, rim, mine, other)
        return early, late

    is_last = lax.axis_index("tm") == rounds - 1
    live = (lax.iota(jnp.int32, NB) < live_count[0]).astype(F32)[:, None, None]
    start = (live * terminal).reshape(NB // STEP, STEP * COMP, LANES)
    back = [(t, t - 1) for t in range(1, rounds)]

    def turn(step_index, incoming):
        early, late = slab(incoming)
        moved = lax.ppermute(early, "tm", back)
        return jnp.where(is_last, start, moved)

    incoming = lax.fori_loop(0, rounds - 1, turn, start)
    early, late = slab(incoming)
    fields = jnp.stack([early, late]).reshape(2, NB, COMP, LANES)
    part = jnp.sum(weights[:, None] * jnp.sum(fields * shape_field[None], axis=(2, 3)), axis=0)
    copies = jnp.broadcast_to(part, (rounds, *part.shape))
    sensitivity = lax.all_to_all(copies, "tm", split_axis=0, concat_axis=0, tiled=True).sum(axis=0)
    return fields, sensitivity


def solution(mesh):
    return jax.shard_map(
        per_device,
        mesh=mesh,
        in_specs=(
            P("tm", "space", None, None),
            P("space", None, None),
            P("tm", "space", None, None, None),
            P("space", None, None),
            P("space", None),
            P("space", None),
            P("space", None, None),
            P("space"),
            P("space", None),
            P("space", None, None),
            P("tm"),
        ),
        out_specs=(P("tm", "space", None, None), P("space")),
        check_vma=False,
    )
```

time: 1320 us -> 761 us (0.58)
  local copies, waits for them, and re-layouts: 369 us -> 26.8 us
  other arithmetic: 336 us -> 4.75 us
  Pallas kernels: 0 us -> 301 us
  starting transfers between devices: 358 us -> 178 us
    gather x144 -> x4, local copies, waits for them, and re-layouts: 312 us -> 7.25 us  [the longest x2 6.13 us: rim_message(): tiles = coef[chosen, FACE:PRE + 1]]
    pallas_call x0 -> x33, Pallas kernels: none -> 301 us  [the longest x8 94.5 us: slab(): steps[1](table, lists, fixes, x, fixed, *got, rim, mine, other)]
    dot_general x96 -> x0, other arithmetic: 230 us -> none  [the longest x48 133 us: operate(): jnp.einsum('bnc,bnkc->bkc', face_coef, gathered, precision=highest)]
    ppermute x103 -> x67, starting transfers between devices: 352 us -> 171 us  [the longest x25 109 us: exchange(): lax.ppermute(first, 'space', near)]
    mul x50 -> x1, other arithmetic: 50.2 us -> 0.09 us  [per_device(): start = (live * terminal).reshape(NB // STEP, STEP * COMP, LANES)]
    while x748 -> x0, local copies, waits for them, and re-layouts: 38.7 us -> none
    concatenate x48 -> x9, other arithmetic: 31.5 us -> 0.49 us  [the longest x2 0.27 us: rim_message(): tiles = coef[chosen, FACE:PRE + 1]]
    ppermute x103 -> x67, waiting for transfers between devices: 231 us -> 241 us  [the longest x25 78 us: exchange(): lax.ppermute(first, 'space', near)]
  transfers between devices with their start and end apart: 104 -> 68, of which waited for: 40 -> 66; matrix products, arithmetic and copies ran while one was open for 12% -> 2% of each run, Pallas kernels for 0% -> 0%
where the time goes in v1:
time: 761 us; the launch traced here: 757 us
  Pallas kernels  301 us (40%)
  waiting for transfers between devices  245 us (32%)
  starting transfers between devices  178 us (23%)
  local copies, waits for them, and re-layouts  26.8 us (4%)
    ppermute x25, starting transfers between devices, exchange(): lax.ppermute(first, 'space', near)  109 us
    pallas_call x8, Pallas kernels, slab(): steps[1](table, lists, fixes, x, fixed, *got, rim, mine, other)  94.5 us
    pallas_call x8, Pallas kernels, slab(): x, fixed, *sent = steps[0](table, lists, fixes, x, *got, rim, mine, other)  89.4 us
    ppermute x25, waiting for transfers between devices, exchange(): lax.ppermute(first, 'space', near)  78 us
    ppermute x7, waiting for transfers between devices, turn(): moved = lax.ppermute(early, 'tm', back)  76.8 us
    ppermute x25, waiting for transfers between devices, exchange(): lax.ppermute(second, 'space', far)  75.9 us
    pallas_call x8, Pallas kernels, slab(): early, = steps[2](table, lists, fixes, x, fixed, *got, rim, mine, other)  72.6 us
    ppermute x25, starting transfers between devices, exchange(): lax.ppermute(second, 'space', far)  48.2 us
  transfers between devices with their start and end apart: 68, of which 66 were waited for; matrix products, arithmetic and copies ran while one was open for 2% of the time, Pallas kernels for 0%

profile of v1, /device:TPU:113, one launch (start us, length us, event | category | flops | bytes accessed | tf_op | source)
XLA Modules:
  0.0 757.2 jit_solution(11523228202016732493)
XLA Ops:
  53.4 614.5 %while.10 = (s32[]{:T(128)}, f32[16,40,128]{2,1,0:T(8,128)S(1)}, pred[]{:T(512)}, s32[1536]{0:T(1024)S(1)}, s32[32]{0:T(128)S(1)}, /*index=5*/f32[128,10,8,128]{...) while((s32[]{:T(128)}, f32[16,40,128]{2,1,0:T(8,128)S(1)}, ...), condition=%wide.region_5.6_spmd, body=%wide.region_4.5_spmd.sunk | while | flops 81922 | bytes 5570990 | solution.py:364
  72.2 11.2 %step0.3 = (f32[256,8,128]{2,1,0:T(8,128)S(1)}, f32[256,8,128]{2,1,0:T(8,128)S(1)}, f32[160,128]{1,0:T(8,128)S(1)}, f32[160,128]{1,0:T(8,128)S(1)}) custom-call(s32[1536]{0:T(1024)S(1)} %get-tuple-element.245.table, s32[32]{0:T(128)S(1)} %get-tuple-element.246.lists, s32[192]{0:T(256)S(1)} %get-tuple-element.249.fixes, ...), custom_call_target="tpu_custom_call" | custom-call | tf_op jit(solution)/shard_map/while/body/eval_jaxpr/step0/pallas_call | solution.py:347
  95.8 11.9 %step1.3 = (f32[256,8,128]{2,1,0:T(8,128)S(1)}, f32[256,8,128]{2,1,0:T(8,128)S(1)}, f32[160,128]{1,0:T(8,128)S(1)}, f32[160,128]{1,0:T(8,128)S(1)}, f32[16,40,128]{2,1,0:T(8,128)}) custom-call(s32[1536]{0:T(1024)S(1)} %get-tuple-element.245.table, s32[32]{0:T(128)S(1)} %get-tuple-element.246.lists, s32[192]{0:T(256)S(1)} %get-tuple-element.249.fixes, ...), custom_call_target="tpu_custom_call" | custom-call | tf_op jit(solution)/shard_map/while/body/eval_jaxpr/step1/pallas_call | solution.py:349
  119.6 9.1 %step2.3 = f32[16,40,128]{2,1,0:T(8,128)S(1)} custom-call(s32[1536]{0:T(1024)S(1)} %get-tuple-element.245.table, s32[32]{0:T(128)S(1)} %get-tuple-element.246.lists, s32[192]{0:T(256)S(1)} %get-tuple-element.249.fixes, f32[256,8,128]{2,1,0:T(8,128)S(1)} %get-tuple-element.216.x_in, f32[256,8,128]{2,1,0:T(8,128)S(1)} %get-tuple-element.217.refs_0_, ...), custom_call_target="tpu_custom_call" | custom-call | tf_op jit(solution)/shard_map/while/body/eval_jaxpr/step2/pallas_call | solution.py:351
  129.9 10.0 %collective-permute-done.7 = f32[16,40,128]{2,1,0:T(8,128)S(1)} collective-permute-done((f32[16,40,128]{2,1,0:T(8,128)S(1)}, f32[16,40,128]{2,1,0:T(8,128)S(1)}, u32[]{:S(2)}, u32[]{:S(2)}) %collective-permute-start.7) | collective-permute-done | bytes 327712 | tf_op jit(solution)/shard_map/while/body/eval_jaxpr/ppermute | solution.py:361
  159.1 11.2 %step0.3 = (f32[256,8,128]{2,1,0:T(8,128)S(1)}, f32[256,8,128]{2,1,0:T(8,128)S(1)}, f32[160,128]{1,0:T(8,128)S(1)}, f32[160,128]{1,0:T(8,128)S(1)}) custom-call(s32[1536]{0:T(1024)S(1)} %get-tuple-element.245.table, s32[32]{0:T(128)S(1)} %get-tuple-element.246.lists, s32[192]{0:T(256)S(1)} %get-tuple-element.249.fixes, ...), custom_call_target="tpu_custom_call" | custom-call | tf_op jit(solution)/shard_map/while/body/eval_jaxpr/step0/pallas_call | solution.py:347
  183.3 11.9 %step1.3 = (f32[256,8,128]{2,1,0:T(8,128)S(1)}, f32[256,8,128]{2,1,0:T(8,128)S(1)}, f32[160,128]{1,0:T(8,128)S(1)}, f32[160,128]{1,0:T(8,128)S(1)}, f32[16,40,128]{2,1,0:T(8,128)}) custom-call(s32[1536]{0:T(1024)S(1)} %get-tuple-element.245.table, s32[32]{0:T(128)S(1)} %get-tuple-element.246.lists, s32[192]{0:T(256)S(1)} %get-tuple-element.249.fixes, ...), custom_call_target="tpu_custom_call" | custom-call | tf_op jit(solution)/shard_map/while/body/eval_jaxpr/step1/pallas_call | solution.py:349
  206.7 9.1 %step2.3 = f32[16,40,128]{2,1,0:T(8,128)S(1)} custom-call(s32[1536]{0:T(1024)S(1)} %get-tuple-element.245.table, s32[32]{0:T(128)S(1)} %get-tuple-element.246.lists, s32[192]{0:T(256)S(1)} %get-tuple-element.249.fixes, f32[256,8,128]{2,1,0:T(8,128)S(1)} %get-tuple-element.216.x_in, f32[256,8,128]{2,1,0:T(8,128)S(1)} %get-tuple-element.217.refs_0_, ...), custom_call_target="tpu_custom_call" | custom-call | tf_op jit(solution)/shard_map/while/body/eval_jaxpr/step2/pallas_call | solution.py:351
  217.1 11.0 %collective-permute-done.7 = f32[16,40,128]{2,1,0:T(8,128)S(1)} collective-permute-done((f32[16,40,128]{2,1,0:T(8,128)S(1)}, f32[16,40,128]{2,1,0:T(8,128)S(1)}, u32[]{:S(2)}, u32[]{:S(2)}) %collective-permute-start.7) | collective-permute-done | bytes 327712 | tf_op jit(solution)/shard_map/while/body/eval_jaxpr/ppermute | solution.py:361
  246.8 11.2 %step0.3 = (f32[256,8,128]{2,1,0:T(8,128)S(1)}, f32[256,8,128]{2,1,0:T(8,128)S(1)}, f32[160,128]{1,0:T(8,128)S(1)}, f32[160,128]{1,0:T(8,128)S(1)}) custom-call(s32[1536]{0:T(1024)S(1)} %get-tuple-element.245.table, s32[32]{0:T(128)S(1)} %get-tuple-element.246.lists, s32[192]{0:T(256)S(1)} %get-tuple-element.249.fixes, ...), custom_call_target="tpu_custom_call" | custom-call | tf_op jit(solution)/shard_map/while/body/eval_jaxpr/step0/pallas_call | solution.py:347
  271.3 11.9 %step1.3 = (f32[256,8,128]{2,1,0:T(8,128)S(1)}, f32[256,8,128]{2,1,0:T(8,128)S(1)}, f32[160,128]{1,0:T(8,128)S(1)}, f32[160,128]{1,0:T(8,128)S(1)}, f32[16,40,128]{2,1,0:T(8,128)}) custom-call(s32[1536]{0:T(1024)S(1)} %get-tuple-element.245.table, s32[32]{0:T(128)S(1)} %get-tuple-element.246.lists, s32[192]{0:T(256)S(1)} %get-tuple-element.249.fixes, ...), custom_call_target="tpu_custom_call" | custom-call | tf_op jit(solution)/shard_map/while/body/eval_jaxpr/step1/pallas_call | solution.py:349
  294.6 9.1 %step2.3 = f32[16,40,128]{2,1,0:T(8,128)S(1)} custom-call(s32[1536]{0:T(1024)S(1)} %get-tuple-element.245.table, s32[32]{0:T(128)S(1)} %get-tuple-element.246.lists, s32[192]{0:T(256)S(1)} %get-tuple-element.249.fixes, f32[256,8,128]{2,1,0:T(8,128)S(1)} %get-tuple-element.216.x_in, f32[256,8,128]{2,1,0:T(8,128)S(1)} %get-tuple-element.217.refs_0_, ...), custom_call_target="tpu_custom_call" | custom-call | tf_op jit(solution)/shard_map/while/body/eval_jaxpr/step2/pallas_call | solution.py:351
  305.0 10.9 %collective-permute-done.7 = f32[16,40,128]{2,1,0:T(8,128)S(1)} collective-permute-done((f32[16,40,128]{2,1,0:T(8,128)S(1)}, f32[16,40,128]{2,1,0:T(8,128)S(1)}, u32[]{:S(2)}, u32[]{:S(2)}) %collective-permute-start.7) | collective-permute-done | bytes 327712 | tf_op jit(solution)/shard_map/while/body/eval_jaxpr/ppermute | solution.py:361
  334.7 11.2 %step0.3 = (f32[256,8,128]{2,1,0:T(8,128)S(1)}, f32[256,8,128]{2,1,0:T(8,128)S(1)}, f32[160,128]{1,0:T(8,128)S(1)}, f32[160,128]{1,0:T(8,128)S(1)}) custom-call(s32[1536]{0:T(1024)S(1)} %get-tuple-element.245.table, s32[32]{0:T(128)S(1)} %get-tuple-element.246.lists, s32[192]{0:T(256)S(1)} %get-tuple-element.249.fixes, ...), custom_call_target="tpu_custom_call" | custom-call | tf_op jit(solution)/shard_map/while/body/eval_jaxpr/step0/pallas_call | solution.py:347
  358.6 11.9 %step1.3 = (f32[256,8,128]{2,1,0:T(8,128)S(1)}, f32[256,8,128]{2,1,0:T(8,128)S(1)}, f32[160,128]{1,0:T(8,128)S(1)}, f32[160,128]{1,0:T(8,128)S(1)}, f32[16,40,128]{2,1,0:T(8,128)}) custom-call(s32[1536]{0:T(1024)S(1)} %get-tuple-element.245.table, s32[32]{0:T(128)S(1)} %get-tuple-element.246.lists, s32[192]{0:T(256)S(1)} %get-tuple-element.249.fixes, ...), custom_call_target="tpu_custom_call" | custom-call | tf_op jit(solution)/shard_map/while/body/eval_jaxpr/step1/pallas_call | solution.py:349
  382.4 9.1 %step2.3 = f32[16,40,128]{2,1,0:T(8,128)S(1)} custom-call(s32[1536]{0:T(1024)S(1)} %get-tuple-element.245.table, s32[32]{0:T(128)S(1)} %get-tuple-element.246.lists, s32[192]{0:T(256)S(1)} %get-tuple-element.249.fixes, f32[256,8,128]{2,1,0:T(8,128)S(1)} %get-tuple-element.216.x_in, f32[256,8,128]{2,1,0:T(8,128)S(1)} %get-tuple-element.217.refs_0_, ...), custom_call_target="tpu_custom_call" | custom-call | tf_op jit(solution)/shard_map/while/body/eval_jaxpr/step2/pallas_call | solution.py:351
  392.7 11.3 %collective-permute-done.7 = f32[16,40,128]{2,1,0:T(8,128)S(1)} collective-permute-done((f32[16,40,128]{2,1,0:T(8,128)S(1)}, f32[16,40,128]{2,1,0:T(8,128)S(1)}, u32[]{:S(2)}, u32[]{:S(2)}) %collective-permute-start.7) | collective-permute-done | bytes 327712 | tf_op jit(solution)/shard_map/while/body/eval_jaxpr/ppermute | solution.py:361
  422.6 11.2 %step0.3 = (f32[256,8,128]{2,1,0:T(8,128)S(1)}, f32[256,8,128]{2,1,0:T(8,128)S(1)}, f32[160,128]{1,0:T(8,128)S(1)}, f32[160,128]{1,0:T(8,128)S(1)}) custom-call(s32[1536]{0:T(1024)S(1)} %get-tuple-element.245.table, s32[32]{0:T(128)S(1)} %get-tuple-element.246.lists, s32[192]{0:T(256)S(1)} %get-tuple-element.249.fixes, ...), custom_call_target="tpu_custom_call" | custom-call | tf_op jit(solution)/shard_map/while/body/eval_jaxpr/step0/pallas_call | solution.py:347
  447.1 11.9 %step1.3 = (f32[256,8,128]{2,1,0:T(8,128)S(1)}, f32[256,8,128]{2,1,0:T(8,128)S(1)}, f32[160,128]{1,0:T(8,128)S(1)}, f32[160,128]{1,0:T(8,128)S(1)}, f32[16,40,128]{2,1,0:T(8,128)}) custom-call(s32[1536]{0:T(1024)S(1)} %get-tuple-element.245.table, s32[32]{0:T(128)S(1)} %get-tuple-element.246.lists, s32[192]{0:T(256)S(1)} %get-tuple-element.249.fixes, ...), custom_call_target="tpu_custom_call" | custom-call | tf_op jit(solution)/shard_map/while/body/eval_jaxpr/step1/pallas_call | solution.py:349
  470.3 9.1 %step2.3 = f32[16,40,128]{2,1,0:T(8,128)S(1)} custom-call(s32[1536]{0:T(1024)S(1)} %get-tuple-element.245.table, s32[32]{0:T(128)S(1)} %get-tuple-element.246.lists, s32[192]{0:T(256)S(1)} %get-tuple-element.249.fixes, f32[256,8,128]{2,1,0:T(8,128)S(1)} %get-tuple-element.216.x_in, f32[256,8,128]{2,1,0:T(8,128)S(1)} %get-tuple-element.217.refs_0_, ...), custom_call_target="tpu_custom_call" | custom-call | tf_op jit(solution)/shard_map/while/body/eval_jaxpr/step2/pallas_call | solution.py:351
  480.7 11.4 %collective-permute-done.7 = f32[16,40,128]{2,1,0:T(8,128)S(1)} collective-permute-done((f32[16,40,128]{2,1,0:T(8,128)S(1)}, f32[16,40,128]{2,1,0:T(8,128)S(1)}, u32[]{:S(2)}, u32[]{:S(2)}) %collective-permute-start.7) | collective-permute-done | bytes 327712 | tf_op jit(solution)/shard_map/while/body/eval_jaxpr/ppermute | solution.py:361
  510.7 11.2 %step0.3 = (f32[256,8,128]{2,1,0:T(8,128)S(1)}, f32[256,8,128]{2,1,0:T(8,128)S(1)}, f32[160,128]{1,0:T(8,128)S(1)}, f32[160,128]{1,0:T(8,128)S(1)}) custom-call(s32[1536]{0:T(1024)S(1)} %get-tuple-element.245.table, s32[32]{0:T(128)S(1)} %get-tuple-element.246.lists, s32[192]{0:T(256)S(1)} %get-tuple-element.249.fixes, ...), custom_call_target="tpu_custom_call" | custom-call | tf_op jit(solution)/shard_map/while/body/eval_jaxpr/step0/pallas_call | solution.py:347
  535.2 11.9 %step1.3 = (f32[256,8,128]{2,1,0:T(8,128)S(1)}, f32[256,8,128]{2,1,0:T(8,128)S(1)}, f32[160,128]{1,0:T(8,128)S(1)}, f32[160,128]{1,0:T(8,128)S(1)}, f32[16,40,128]{2,1,0:T(8,128)}) custom-call(s32[1536]{0:T(1024)S(1)} %get-tuple-element.245.table, s32[32]{0:T(128)S(1)} %get-tuple-element.246.lists, s32[192]{0:T(256)S(1)} %get-tuple-element.249.fixes, ...), custom_call_target="tpu_custom_call" | custom-call | tf_op jit(solution)/shard_map/while/body/eval_jaxpr/step1/pallas_call | solution.py:349
  558.5 9.1 %step2.3 = f32[16,40,128]{2,1,0:T(8,128)S(1)} custom-call(s32[1536]{0:T(1024)S(1)} %get-tuple-element.245.table, s32[32]{0:T(128)S(1)} %get-tuple-element.246.lists, s32[192]{0:T(256)S(1)} %get-tuple-element.249.fixes, f32[256,8,128]{2,1,0:T(8,128)S(1)} %get-tuple-element.216.x_in, f32[256,8,128]{2,1,0:T(8,128)S(1)} %get-tuple-element.217.refs_0_, ...), custom_call_target="tpu_custom_call" | custom-call | tf_op jit(solution)/shard_map/while/body/eval_jaxpr/step2/pallas_call | solution.py:351
  568.9 10.9 %collective-permute-done.7 = f32[16,40,128]{2,1,0:T(8,128)S(1)} collective-permute-done((f32[16,40,128]{2,1,0:T(8,128)S(1)}, f32[16,40,128]{2,1,0:T(8,128)S(1)}, u32[]{:S(2)}, u32[]{:S(2)}) %collective-permute-start.7) | collective-permute-done | bytes 327712 | tf_op jit(solution)/shard_map/while/body/eval_jaxpr/ppermute | solution.py:361
  598.6 11.2 %step0.3 = (f32[256,8,128]{2,1,0:T(8,128)S(1)}, f32[256,8,128]{2,1,0:T(8,128)S(1)}, f32[160,128]{1,0:T(8,128)S(1)}, f32[160,128]{1,0:T(8,128)S(1)}) custom-call(s32[1536]{0:T(1024)S(1)} %get-tuple-element.245.table, s32[32]{0:T(128)S(1)} %get-tuple-element.246.lists, s32[192]{0:T(256)S(1)} %get-tuple-element.249.fixes, ...), custom_call_target="tpu_custom_call" | custom-call | tf_op jit(solution)/shard_map/while/body/eval_jaxpr/step0/pallas_call | solution.py:347
  622.5 11.9 %step1.3 = (f32[256,8,128]{2,1,0:T(8,128)S(1)}, f32[256,8,128]{2,1,0:T(8,128)S(1)}, f32[160,128]{1,0:T(8,128)S(1)}, f32[160,128]{1,0:T(8,128)S(1)}, f32[16,40,128]{2,1,0:T(8,128)}) custom-call(s32[1536]{0:T(1024)S(1)} %get-tuple-element.245.table, s32[32]{0:T(128)S(1)} %get-tuple-element.246.lists, s32[192]{0:T(256)S(1)} %get-tuple-element.249.fixes, ...), custom_call_target="tpu_custom_call" | custom-call | tf_op jit(solution)/shard_map/while/body/eval_jaxpr/step1/pallas_call | solution.py:349
  646.3 9.1 %step2.3 = f32[16,40,128]{2,1,0:T(8,128)S(1)} custom-call(s32[1536]{0:T(1024)S(1)} %get-tuple-element.245.table, s32[32]{0:T(128)S(1)} %get-tuple-element.246.lists, s32[192]{0:T(256)S(1)} %get-tuple-element.249.fixes, f32[256,8,128]{2,1,0:T(8,128)S(1)} %get-tuple-element.216.x_in, f32[256,8,128]{2,1,0:T(8,128)S(1)} %get-tuple-element.217.refs_0_, ...), custom_call_target="tpu_custom_call" | custom-call | tf_op jit(solution)/shard_map/while/body/eval_jaxpr/step2/pallas_call | solution.py:351
  656.6 11.3 %collective-permute-done.7 = f32[16,40,128]{2,1,0:T(8,128)S(1)} collective-permute-done((f32[16,40,128]{2,1,0:T(8,128)S(1)}, f32[16,40,128]{2,1,0:T(8,128)S(1)}, u32[]{:S(2)}, u32[]{:S(2)}) %collective-permute-start.7) | collective-permute-done | bytes 327712 | tf_op jit(solution)/shard_map/while/body/eval_jaxpr/ppermute | solution.py:361
  686.5 11.2 %step0.2 = (f32[256,8,128]{2,1,0:T(8,128)S(1)}, f32[256,8,128]{2,1,0:T(8,128)S(1)}, f32[160,128]{1,0:T(8,128)S(1)}, f32[160,128]{1,0:T(8,128)S(1)}) custom-call(s32[1536]{0:T(1024)S(1)} %get-tuple-element.284, s32[32]{0:T(128)S(1)} %get-tuple-element.287, s32[192]{0:T(256)S(1)} %get-tuple-element.285, f32[256,8,128]{2,1,0:T(8,128)S(1)} %get-tuple-element.78.x_in, ...), custom_call_target="tpu_custom_call" | custom-call | tf_op jit(solution)/shard_map/step0/pallas_call | solution.py:347
  711.0 11.2 %step1.2 = (f32[256,8,128]{2,1,0:T(8,128)S(1)}, f32[256,8,128]{2,1,0:T(8,128)S(1)}, f32[160,128]{1,0:T(8,128)S(1)}, f32[160,128]{1,0:T(8,128)S(1)}, f32[16,40,128]{2,1,0:T(8,128)S(1)}) custom-call(s32[1536]{0:T(1024)S(1)} %get-tuple-element.284, s32[32]{0:T(128)S(1)} %get-tuple-element.287, s32[192]{0:T(256)S(1)} %get-tuple-element.285, ...), custom_call_target="tpu_custom_call" | custom-call | tf_op jit(solution)/shard_map/step1/pallas_call | solution.py:349
  733.5 9.1 %step2.2 = f32[16,40,128]{2,1,0:T(8,128)S(1)} custom-call(s32[1536]{0:T(1024)S(1)} %get-tuple-element.284, s32[32]{0:T(128)S(1)} %get-tuple-element.287, s32[192]{0:T(256)S(1)} %get-tuple-element.285, f32[256,8,128]{2,1,0:T(8,128)S(1)} %get-tuple-element.85.x_in, f32[256,8,128]{2,1,0:T(8,128)S(1)} %get-tuple-element.86.refs_0_, ...), custom_call_target="tpu_custom_call" | custom-call | tf_op jit(solution)/shard_map/step2/pallas_call | solution.py:351
  (239 shorter events, 421.5 us)
Async XLA Ops:
  10.8 23.1 %collective-permute-start.10 = (f32[128,10,8,128]{3,2,1,0:T(8,128)}, f32[128,10,8,128]{3,2,1,0:T(8,128)}, u32[]{:S(2)}, u32[]{:S(2)}) collective-permute-start(f32[128,10,8,128]{3,2,1,0:T(8,128)} %prep.1.coef0.refs_3_.refs_4_), channel_id=1, source_target_pairs={{0,1},{1,0},{2,3},{3,2},{4,5},{5,4},{6,7},{7,6},{8,9},{9,8},{10,11... | collective-permute-start | bytes 15728648 | tf_op jit(solution)/shard_map/ppermute | solution.py:273
  11.6 9.6 %collective-permute-start.8 = (s32[128,7]{1,0:T(8,128)S(1)}, s32[128,7]{1,0:T(8,128)S(1)}, u32[]{:S(2)}, u32[]{:S(2)}) collective-permute-start(s32[128,7]{1,0:T(8,128)S(1)} %copy.158), channel_id=1, source_target_pairs={{0,1},{1,0},{2,3},{3,2},{4,5},{5,4},{6,7},{7,6},{8,9},{9,8},{10,11... | collective-permute-start | bytes 10760 | tf_op jit(solution)/shard_map/ppermute | solution.py:277
  22.7 10.6 %collective-permute-start.9 = (f32[16,3,8,128]{3,2,1,0:T(8,128)S(1)}, f32[16,3,8,128]{3,2,1,0:T(8,128)S(1)}, u32[]{:S(2)}, u32[]{:S(2)}) collective-permute-start(f32[16,3,8,128]{3,2,1,0:T(8,128)S(1)} %pad_maximum_fusion.1), channel_id=1, source_target_pairs={{1,2},{2,1},{3,4},{4,3},{5,6},{6,5},{7,8},{8,7},{9,10},{10,9},{11,... | collective-permute-start | bytes 589832 | tf_op jit(solution)/shard_map/ppermute | solution.py:263
  42.2 10.4 %collective-permute-start.11 = (f32[16,3,8,128]{3,2,1,0:T(8,128)S(1)}, f32[16,3,8,128]{3,2,1,0:T(8,128)S(1)}, u32[]{:S(2)}, u32[]{:S(2)}) collective-permute-start(f32[16,3,8,128]{3,2,1,0:T(8,128)S(1)} %pad_maximum_fusion.2), channel_id=1, source_target_pairs={{0,3},{2,5},{3,0},{4,7},{5,2},{6,9},{7,4},{8,11},{9,6},{10,13},{11... | collective-permute-start | bytes 589832 | tf_op jit(solution)/shard_map/ppermute | solution.py:263
  60.1 9.4 %collective-permute-start.1 = (f32[160,128]{1,0:T(8,128)S(1)}, f32[160,128]{1,0:T(8,128)S(1)}, u32[]{:S(2)}, u32[]{:S(2)}) collective-permute-start(f32[160,128]{1,0:T(8,128)S(1)} %get-tuple-element.210), channel_id=1, source_target_pairs={{1,2},{2,1},{3,4},{4,3},{5,6},{6,5},{7,8},{8,7},{9,10},{10,9},{11,... | collective-permute-start | bytes 245768 | tf_op jit(solution)/shard_map/while/body/eval_jaxpr/ppermute | solution.py:263
  83.4 9.4 %collective-permute-start.3 = (f32[160,128]{1,0:T(8,128)S(1)}, f32[160,128]{1,0:T(8,128)S(1)}, u32[]{:S(2)}, u32[]{:S(2)}) collective-permute-start(f32[160,128]{1,0:T(8,128)S(1)} %get-tuple-element.214), channel_id=1, source_target_pairs={{1,2},{2,1},{3,4},{4,3},{5,6},{6,5},{7,8},{8,7},{9,10},{10,9},{11,... | collective-permute-start | bytes 245768 | tf_op jit(solution)/shard_map/while/body/eval_jaxpr/ppermute | solution.py:263
  107.7 9.4 %collective-permute-start.5 = (f32[160,128]{1,0:T(8,128)S(1)}, f32[160,128]{1,0:T(8,128)S(1)}, u32[]{:S(2)}, u32[]{:S(2)}) collective-permute-start(f32[160,128]{1,0:T(8,128)S(1)} %get-tuple-element.218), channel_id=1, source_target_pairs={{1,2},{2,1},{3,4},{4,3},{5,6},{6,5},{7,8},{8,7},{9,10},{10,9},{11,... | collective-permute-start | bytes 245768 | tf_op jit(solution)/shard_map/while/body/eval_jaxpr/ppermute | solution.py:263
  128.6 11.3 %collective-permute-start.7 = (f32[16,40,128]{2,1,0:T(8,128)S(1)}, f32[16,40,128]{2,1,0:T(8,128)S(1)}, u32[]{:S(2)}, u32[]{:S(2)}) collective-permute-start(f32[16,40,128]{2,1,0:T(8,128)S(1)} %step2.3), channel_id=1, source_target_pairs={{32,0},{64,32},{96,64},{128,96},{160,128},{192,160},{224,192},{33,... | collective-permute-start | bytes 983048 | tf_op jit(solution)/shard_map/while/body/eval_jaxpr/ppermute | solution.py:361
  146.9 9.4 %collective-permute-start.1 = (f32[160,128]{1,0:T(8,128)S(1)}, f32[160,128]{1,0:T(8,128)S(1)}, u32[]{:S(2)}, u32[]{:S(2)}) collective-permute-start(f32[160,128]{1,0:T(8,128)S(1)} %get-tuple-element.210), channel_id=1, source_target_pairs={{1,2},{2,1},{3,4},{4,3},{5,6},{6,5},{7,8},{8,7},{9,10},{10,9},{11,... | collective-permute-start | bytes 245768 | tf_op jit(solution)/shard_map/while/body/eval_jaxpr/ppermute | solution.py:263
  170.3 9.4 %collective-permute-start.3 = (f32[160,128]{1,0:T(8,128)S(1)}, f32[160,128]{1,0:T(8,128)S(1)}, u32[]{:S(2)}, u32[]{:S(2)}) collective-permute-start(f32[160,128]{1,0:T(8,128)S(1)} %get-tuple-element.214), channel_id=1, source_target_pairs={{1,2},{2,1},{3,4},{4,3},{5,6},{6,5},{7,8},{8,7},{9,10},{10,9},{11,... | collective-permute-start | bytes 245768 | tf_op jit(solution)/shard_map/while/body/eval_jaxpr/ppermute | solution.py:263
  215.8 12.3 %collective-permute-start.7 = (f32[16,40,128]{2,1,0:T(8,128)S(1)}, f32[16,40,128]{2,1,0:T(8,128)S(1)}, u32[]{:S(2)}, u32[]{:S(2)}) collective-permute-start(f32[16,40,128]{2,1,0:T(8,128)S(1)} %step2.3), channel_id=1, source_target_pairs={{32,0},{64,32},{96,64},{128,96},{160,128},{192,160},{224,192},{33,... | collective-permute-start | bytes 983048 | tf_op jit(solution)/shard_map/while/body/eval_jaxpr/ppermute | solution.py:361
  234.9 9.4 %collective-permute-start.1 = (f32[160,128]{1,0:T(8,128)S(1)}, f32[160,128]{1,0:T(8,128)S(1)}, u32[]{:S(2)}, u32[]{:S(2)}) collective-permute-start(f32[160,128]{1,0:T(8,128)S(1)} %get-tuple-element.210), channel_id=1, source_target_pairs={{1,2},{2,1},{3,4},{4,3},{5,6},{6,5},{7,8},{8,7},{9,10},{10,9},{11,... | collective-permute-start | bytes 245768 | tf_op jit(solution)/shard_map/while/body/eval_jaxpr/ppermute | solution.py:263
  257.9 9.4 %collective-permute-start.3 = (f32[160,128]{1,0:T(8,128)S(1)}, f32[160,128]{1,0:T(8,128)S(1)}, u32[]{:S(2)}, u32[]{:S(2)}) collective-permute-start(f32[160,128]{1,0:T(8,128)S(1)} %get-tuple-element.214), channel_id=1, source_target_pairs={{1,2},{2,1},{3,4},{4,3},{5,6},{6,5},{7,8},{8,7},{9,10},{10,9},{11,... | collective-permute-start | bytes 245768 | tf_op jit(solution)/shard_map/while/body/eval_jaxpr/ppermute | solution.py:263
  283.2 9.4 %collective-permute-start.5 = (f32[160,128]{1,0:T(8,128)S(1)}, f32[160,128]{1,0:T(8,128)S(1)}, u32[]{:S(2)}, u32[]{:S(2)}) collective-permute-start(f32[160,128]{1,0:T(8,128)S(1)} %get-tuple-element.218), channel_id=1, source_target_pairs={{1,2},{2,1},{3,4},{4,3},{5,6},{6,5},{7,8},{8,7},{9,10},{10,9},{11,... | collective-permute-start | bytes 245768 | tf_op jit(solution)/shard_map/while/body/eval_jaxpr/ppermute | solution.py:263
  303.7 12.2 %collective-permute-start.7 = (f32[16,40,128]{2,1,0:T(8,128)S(1)}, f32[16,40,128]{2,1,0:T(8,128)S(1)}, u32[]{:S(2)}, u32[]{:S(2)}) collective-permute-start(f32[16,40,128]{2,1,0:T(8,128)S(1)} %step2.3), channel_id=1, source_target_pairs={{32,0},{64,32},{96,64},{128,96},{160,128},{192,160},{224,192},{33,... | collective-permute-start | bytes 983048 | tf_op jit(solution)/shard_map/while/body/eval_jaxpr/ppermute | solution.py:361
  322.8 9.4 %collective-permute-start.1 = (f32[160,128]{1,0:T(8,128)S(1)}, f32[160,128]{1,0:T(8,128)S(1)}, u32[]{:S(2)}, u32[]{:S(2)}) collective-permute-start(f32[160,128]{1,0:T(8,128)S(1)} %get-tuple-element.210), channel_id=1, source_target_pairs={{1,2},{2,1},{3,4},{4,3},{5,6},{6,5},{7,8},{8,7},{9,10},{10,9},{11,... | collective-permute-start | bytes 245768 | tf_op jit(solution)/shard_map/while/body/eval_jaxpr/ppermute | solution.py:263
  345.9 9.4 %collective-permute-start.3 = (f32[160,128]{1,0:T(8,128)S(1)}, f32[160,128]{1,0:T(8,128)S(1)}, u32[]{:S(2)}, u32[]{:S(2)}) collective-permute-start(f32[160,128]{1,0:T(8,128)S(1)} %get-tuple-element.214), channel_id=1, source_target_pairs={{1,2},{2,1},{3,4},{4,3},{5,6},{6,5},{7,8},{8,7},{9,10},{10,9},{11,... | collective-permute-start | bytes 245768 | tf_op jit(solution)/shard_map/while/body/eval_jaxpr/ppermute | solution.py:263
  391.4 12.6 %collective-permute-start.7 = (f32[16,40,128]{2,1,0:T(8,128)S(1)}, f32[16,40,128]{2,1,0:T(8,128)S(1)}, u32[]{:S(2)}, u32[]{:S(2)}) collective-permute-start(f32[16,40,128]{2,1,0:T(8,128)S(1)} %step2.3), channel_id=1, source_target_pairs={{32,0},{64,32},{96,64},{128,96},{160,128},{192,160},{224,192},{33,... | collective-permute-start | bytes 983048 | tf_op jit(solution)/shard_map/while/body/eval_jaxpr/ppermute | solution.py:361
  410.8 9.4 %collective-permute-start.1 = (f32[160,128]{1,0:T(8,128)S(1)}, f32[160,128]{1,0:T(8,128)S(1)}, u32[]{:S(2)}, u32[]{:S(2)}) collective-permute-start(f32[160,128]{1,0:T(8,128)S(1)} %get-tuple-element.210), channel_id=1, source_target_pairs={{1,2},{2,1},{3,4},{4,3},{5,6},{6,5},{7,8},{8,7},{9,10},{10,9},{11,... | collective-permute-start | bytes 245768 | tf_op jit(solution)/shard_map/while/body/eval_jaxpr/ppermute | solution.py:263
  433.8 9.4 %collective-permute-start.3 = (f32[160,128]{1,0:T(8,128)S(1)}, f32[160,128]{1,0:T(8,128)S(1)}, u32[]{:S(2)}, u32[]{:S(2)}) collective-permute-start(f32[160,128]{1,0:T(8,128)S(1)} %get-tuple-element.214), channel_id=1, source_target_pairs={{1,2},{2,1},{3,4},{4,3},{5,6},{6,5},{7,8},{8,7},{9,10},{10,9},{11,... | collective-permute-start | bytes 245768 | tf_op jit(solution)/shard_map/while/body/eval_jaxpr/ppermute | solution.py:263
  459.0 9.4 %collective-permute-start.5 = (f32[160,128]{1,0:T(8,128)S(1)}, f32[160,128]{1,0:T(8,128)S(1)}, u32[]{:S(2)}, u32[]{:S(2)}) collective-permute-start(f32[160,128]{1,0:T(8,128)S(1)} %get-tuple-element.218), channel_id=1, source_target_pairs={{1,2},{2,1},{3,4},{4,3},{5,6},{6,5},{7,8},{8,7},{9,10},{10,9},{11,... | collective-permute-start | bytes 245768 | tf_op jit(solution)/shard_map/while/body/eval_jaxpr/ppermute | solution.py:263
  479.4 12.7 %collective-permute-start.7 = (f32[16,40,128]{2,1,0:T(8,128)S(1)}, f32[16,40,128]{2,1,0:T(8,128)S(1)}, u32[]{:S(2)}, u32[]{:S(2)}) collective-permute-start(f32[16,40,128]{2,1,0:T(8,128)S(1)} %step2.3), channel_id=1, source_target_pairs={{32,0},{64,32},{96,64},{128,96},{160,128},{192,160},{224,192},{33,... | collective-permute-start | bytes 983048 | tf_op jit(solution)/shard_map/while/body/eval_jaxpr/ppermute | solution.py:361
  498.8 9.4 %collective-permute-start.1 = (f32[160,128]{1,0:T(8,128)S(1)}, f32[160,128]{1,0:T(8,128)S(1)}, u32[]{:S(2)}, u32[]{:S(2)}) collective-permute-start(f32[160,128]{1,0:T(8,128)S(1)} %get-tuple-element.210), channel_id=1, source_target_pairs={{1,2},{2,1},{3,4},{4,3},{5,6},{6,5},{7,8},{8,7},{9,10},{10,9},{11,... | collective-permute-start | bytes 245768 | tf_op jit(solution)/shard_map/while/body/eval_jaxpr/ppermute | solution.py:263
  521.8 9.4 %collective-permute-start.3 = (f32[160,128]{1,0:T(8,128)S(1)}, f32[160,128]{1,0:T(8,128)S(1)}, u32[]{:S(2)}, u32[]{:S(2)}) collective-permute-start(f32[160,128]{1,0:T(8,128)S(1)} %get-tuple-element.214), channel_id=1, source_target_pairs={{1,2},{2,1},{3,4},{4,3},{5,6},{6,5},{7,8},{8,7},{9,10},{10,9},{11,... | collective-permute-start | bytes 245768 | tf_op jit(solution)/shard_map/while/body/eval_jaxpr/ppermute | solution.py:263
  567.6 12.2 %collective-permute-start.7 = (f32[16,40,128]{2,1,0:T(8,128)S(1)}, f32[16,40,128]{2,1,0:T(8,128)S(1)}, u32[]{:S(2)}, u32[]{:S(2)}) collective-permute-start(f32[16,40,128]{2,1,0:T(8,128)S(1)} %step2.3), channel_id=1, source_target_pairs={{32,0},{64,32},{96,64},{128,96},{160,128},{192,160},{224,192},{33,... | collective-permute-start | bytes 983048 | tf_op jit(solution)/shard_map/while/body/eval_jaxpr/ppermute | solution.py:361
  586.7 9.4 %collective-permute-start.1 = (f32[160,128]{1,0:T(8,128)S(1)}, f32[160,128]{1,0:T(8,128)S(1)}, u32[]{:S(2)}, u32[]{:S(2)}) collective-permute-start(f32[160,128]{1,0:T(8,128)S(1)} %get-tuple-element.210), channel_id=1, source_target_pairs={{1,2},{2,1},{3,4},{4,3},{5,6},{6,5},{7,8},{8,7},{9,10},{10,9},{11,... | collective-permute-start | bytes 245768 | tf_op jit(solution)/shard_map/while/body/eval_jaxpr/ppermute | solution.py:263
  609.8 9.4 %collective-permute-start.3 = (f32[160,128]{1,0:T(8,128)S(1)}, f32[160,128]{1,0:T(8,128)S(1)}, u32[]{:S(2)}, u32[]{:S(2)}) collective-permute-start(f32[160,128]{1,0:T(8,128)S(1)} %get-tuple-element.214), channel_id=1, source_target_pairs={{1,2},{2,1},{3,4},{4,3},{5,6},{6,5},{7,8},{8,7},{9,10},{10,9},{11,... | collective-permute-start | bytes 245768 | tf_op jit(solution)/shard_map/while/body/eval_jaxpr/ppermute | solution.py:263
  655.3 12.6 %collective-permute-start.7 = (f32[16,40,128]{2,1,0:T(8,128)S(1)}, f32[16,40,128]{2,1,0:T(8,128)S(1)}, u32[]{:S(2)}, u32[]{:S(2)}) collective-permute-start(f32[16,40,128]{2,1,0:T(8,128)S(1)} %step2.3), channel_id=1, source_target_pairs={{32,0},{64,32},{96,64},{128,96},{160,128},{192,160},{224,192},{33,... | collective-permute-start | bytes 983048 | tf_op jit(solution)/shard_map/while/body/eval_jaxpr/ppermute | solution.py:361
  674.6 9.4 %collective-permute-start.13 = (f32[160,128]{1,0:T(8,128)S(1)}, f32[160,128]{1,0:T(8,128)S(1)}, u32[]{:S(2)}, u32[]{:S(2)}) collective-permute-start(f32[160,128]{1,0:T(8,128)S(1)} %get-tuple-element.79), channel_id=1, source_target_pairs={{1,2},{2,1},{3,4},{4,3},{5,6},{6,5},{7,8},{8,7},{9,10},{10,9},{11,... | collective-permute-start | bytes 245768 | tf_op jit(solution)/shard_map/ppermute | solution.py:263
  697.7 9.4 %collective-permute-start.15 = (f32[160,128]{1,0:T(8,128)S(1)}, f32[160,128]{1,0:T(8,128)S(1)}, u32[]{:S(2)}, u32[]{:S(2)}) collective-permute-start(f32[160,128]{1,0:T(8,128)S(1)} %get-tuple-element.83), channel_id=1, source_target_pairs={{1,2},{2,1},{3,4},{4,3},{5,6},{6,5},{7,8},{8,7},{9,10},{10,9},{11,... | collective-permute-start | bytes 245768 | tf_op jit(solution)/shard_map/ppermute | solution.py:263
  722.2 9.4 %collective-permute-start.17 = (f32[160,128]{1,0:T(8,128)S(1)}, f32[160,128]{1,0:T(8,128)S(1)}, u32[]{:S(2)}, u32[]{:S(2)}) collective-permute-start(f32[160,128]{1,0:T(8,128)S(1)} %get-tuple-element.87), channel_id=1, source_target_pairs={{1,2},{2,1},{3,4},{4,3},{5,6},{6,5},{7,8},{8,7},{9,10},{10,9},{11,... | collective-permute-start | bytes 245768 | tf_op jit(solution)/shard_map/ppermute | solution.py:263
  745.5 11.2 %all-to-all-start = ((f32[8,1,128]{2,1,0:T(1,128)}), f32[8,1,128]{2,1,0:T(1,128)S(1)}, u32[]{:S(2)}, u32[]{:S(2)}) async-start(f32[8,1,128]{2,1,0:T(1,128)} %broadcast_in_dim.64), calls=%async_computation | async-start | bytes 8192 | tf_op jit(solution)/shard_map/all_to_all | solution.py:369
  (44 other events, 301.9 us)

commit v2 on v1

v2 whole, which is shorter than its diff:
```python
import jax
import jax.numpy as jnp
from jax import lax
from jax.experimental import pallas as pl
from jax.experimental.pallas import tpu as pltpu
from jax.sharding import PartitionSpec as P

NB = 128
COMP = 5
NEI = 6
HALO = 16
LANES = 128
STEP = 8
CHUNKS = 4
ZERO = 2 * NB + 2 * HALO
ROWS = ZERO + 8
inverse_step = 6.0

FACE, PRE, SRC_LATE, SRC_EARLY, MASS, TILES = 5, 6, 7, 8, 9, 10

VMEM = pl.BlockSpec(memory_space=pltpu.VMEM)
SMEM = pl.BlockSpec(memory_space=pltpu.SMEM)
ANY = pl.BlockSpec(memory_space=pl.ANY)
PARAMS = pltpu.CompilerParams(vmem_limit_bytes=28 << 20)
F32 = jnp.float32


def shape(*dims):
    return jax.ShapeDtypeStruct(dims, F32)


def prep_kernel(live_ref, jac, source, face, cell, volume, out):
    count = live_ref[0]
    lane = lax.broadcasted_iota(jnp.int32, (1, LANES), 1)
    row = lax.broadcasted_iota(jnp.int32, (COMP, LANES), 0)
    blank = jnp.zeros((8, LANES), F32)

    def block(b, carry):
        mass = inverse_step * volume[pl.ds(b, 1), :]
        along = cell[pl.ds(b, 1), :]
        faces = face[b]
        total = jnp.sum(faces, axis=0, keepdims=True)
        diagonal = jnp.zeros((COMP, LANES), F32)
        for i in range(COMP):
            diagonal = jnp.where(row == i, jac[b, i], diagonal)
        live = jnp.where(b < count, 1.0, 0.0).astype(F32)
        pre = live * (1.0 / (mass + diagonal + total + 2.0 * along))
        for i in range(TILES):
            out[b, i] = blank
        for i in range(COMP):
            keep = live - pre * (mass + jac[b, i])
            out[b, i, 0:COMP] = jnp.where(row == i, keep, -pre * jac[b, i])
        out[b, FACE, 0:NEI] = faces
        out[b, FACE, NEI : NEI + 1] = jnp.where(lane == 0, 0.0, along)
        out[b, FACE, NEI + 1 : NEI + 2] = jnp.where(lane == LANES - 1, 0.0, along)
        out[b, PRE, 0:COMP] = pre
        out[b, SRC_LATE, 0:COMP] = pre * source[1, b]
        out[b, SRC_EARLY, 0:COMP] = pre * source[0, b]
        out[b, MASS, 0:COMP] = pre * mass
        return carry

    lax.fori_loop(0, NB, block, 0)


def faces_of(ext, table, half, coef, c, rows=None):
    b = half * NB + c
    lead = c if rows is None else rows
    total = None
    for k in range(NEI):
        slot = table[b * NEI + k]
        if rows is not None:
            slot = jnp.where(slot >= 2 * NB, ZERO, slot)
        term = coef[lead, FACE, k : k + 1] * ext[slot]
        total = term if total is None else total + term
    return total


def finish(ext, b, coef, c, faces, fixed):
    x = ext[b]
    faces = faces + coef[c, FACE, NEI : NEI + 1] * pltpu.roll(x, 1, 1)
    faces = faces + coef[c, FACE, NEI + 1 : NEI + 2] * pltpu.roll(x, LANES - 1, 1)
    value = fixed + coef[c, PRE] * faces
    for i in range(COMP):
        value = value + coef[c, i] * ext[b, i : i + 1]
    return value


def iterate(ext, table, coefs, fixed_of, put, wait=None):
    turns = NB // STEP
    for half in range(2):
        coef = coefs[half]

        def gather(g, half=half, coef=coef):
            return tuple(faces_of(ext, table, half, coef, g * STEP + s) for s in range(STEP))

        def turn(g, faces, half=half, coef=coef, gather=gather):
            following = gather(jnp.minimum(g + 1, turns - 1))
            done = []
            for s in range(STEP):
                c = g * STEP + s
                b = half * NB + c
                fixed = fixed_of(b, c, coef)
                done.append((b, s, finish(ext, b, coef, c, faces[s], fixed), fixed))
            for b, s, value, fixed in done:
                put(b, g, s, half, value, fixed)
            return following

        if wait is None:
            lax.fori_loop(0, turns, turn, gather(0))
        else:
            wait(half, 0)
            each = turns // CHUNKS

            def part(n, faces, half=half, turn=turn):
                @pl.when(n + 1 < CHUNKS)
                def _():
                    wait(half, n + 1)

                return lax.fori_loop(n * each, (n + 1) * each, turn, faces)

            lax.fori_loop(0, CHUNKS, part, gather(0))


def send(ext, table, lists, coef, fixed_of, outs):
    for half in range(2):
        for i in range(HALO):
            h = half * HALO + i
            c = lists[h]
            b = half * NB + c
            faces = faces_of(ext, table, half, coef, c, rows=h)
            ahead = finish(ext, b, coef, h, faces, fixed_of(b, h))
            outs[half][COMP * i : COMP * (i + 1)] = ext[b][0:COMP]
            j = HALO + i
            outs[half][COMP * j : COMP * (j + 1)] = ahead[0:COMP]


def unpack(ext, halves):
    blank = jnp.zeros((8, LANES), F32)
    ext[ZERO] = blank
    for half, source in enumerate(halves):

        def turn(g, carry, half=half, source=source):
            for s in range(STEP):
                b = half * NB + g * STEP + s
                ext[b] = blank
                ext[b, 0:COMP] = source[g, COMP * s : COMP * (s + 1)]
            return carry

        lax.fori_loop(0, NB // STEP, turn, 0)


def receive(ext, after, got):
    blank = jnp.zeros((8, LANES), F32)
    for half in range(2):
        for i in range(HALO):
            row = 2 * NB + half * HALO + i
            ext[row] = blank
            ext[row, 0:COMP] = got[half][COMP * i : COMP * (i + 1)]
            after[row] = blank
            j = HALO + i
            after[row, 0:COMP] = got[half][COMP * j : COMP * (j + 1)]


def first_kernel(table, lists, mine, other, listed, msg0, msg1, ext):
    unpack(ext, (mine, other))
    send(ext, table, lists, listed, lambda b, h: listed[h, SRC_LATE] + listed[h, MASS] * ext[b], (msg0, msg1))


def pluck_kernel(lists, mine, other, out, sems):
    copies = []
    for half, source in enumerate((mine, other)):
        for i in range(HALO):
            h = half * HALO + i
            copies.append(pltpu.make_async_copy(source.at[lists[h]], out.at[h], sems.at[h]))
    for copy in copies:
        copy.start()
    for copy in copies:
        copy.wait()


def make_step(stage):
    def kernel(table, lists, fixes, *refs):
        refs = list(refs)

        def take(n):
            head = refs[:n]
            del refs[:n]
            return head

        if stage == 0:
            (flag,) = take(1)
            moved, begun = take(4), take(4)
            rim, listed, hbm0, hbm1 = take(4)
            x_out, r_out, msg0, msg1, coef0, coef1 = take(6)
        elif stage == 1:
            x_in, r_in, got0, got1, rim, listed, coef0, coef1 = take(8)
            x_out, r_out, msg0, msg1, lam = take(5)
        else:
            x_in, r_in, got0, got1, rim, listed, coef0, coef1 = take(8)
            msg0, msg1, lam = take(3)
        ext, after = take(2)
        coefs = (coef0, coef1)
        blank = jnp.zeros((8, LANES), F32)
        after[ZERO] = blank
        wait = None
        if stage == 0:
            (sems,) = take(1)

            def part(half, n):
                rows = pl.ds(n * (NB // CHUNKS), NB // CHUNKS)
                source = (hbm0, hbm1)[half]
                return pltpu.make_async_copy(source.at[rows], coefs[half].at[rows], sems.at[half, n])

            for half in range(2):
                for n in range(CHUNKS):
                    part(half, n).start()

            def wait(half, n):
                part(half, n).wait()

            for value, group in ((0, moved), (1, begun)):

                @pl.when(flag[0] == value)
                def _(group=group):
                    unpack(ext, group[:2])
                    receive(ext, after, group[2:])

        else:
            ext[ZERO] = blank

            def copy(g, carry):
                for s in range(STEP):
                    ext[g * STEP + s] = x_in[g * STEP + s]
                return carry

            lax.fori_loop(0, 2 * NB // STEP, copy, 0)
            receive(ext, after, (got0, got1))
        for h in range(2 * HALO):
            total = rim[h, 0, 0:1] * ext[fixes[h * NEI]]
            for k in range(1, NEI):
                total = total + rim[h, 0, k : k + 1] * ext[fixes[h * NEI + k]]
            after[2 * NB + h] = after[2 * NB + h] + rim[h, 1] * total

        def keep_lam(g, s, value):
            lam[g, COMP * s : COMP * (s + 1)] = value[0:COMP]

        def put_a(b, g, s, half, value, fixed):
            after[b] = value
            if stage == 0:
                r_out[b] = fixed
            if stage == 1 and half == 0:
                keep_lam(g, s, value)

        def put_b(b, g, s, half, value, fixed):
            ext[b] = value
            if stage < 2:
                x_out[b] = value
            if stage == 1:
                r_out[b] = fixed
            if stage == 2 and half == 0:
                keep_lam(g, s, value)

        def late(b, c, coef):
            return coef[c, SRC_LATE] + coef[c, MASS] * ext[b]

        def early(b, c, coef):
            return coef[c, SRC_EARLY] + coef[c, MASS] * after[b]

        def held(b, c, coef):
            return r_out[b] if stage == 0 else r_in[b]

        iterate(ext, table, coefs, held if stage else late, put_a, wait)
        iterate(after, table, coefs, early if stage == 1 else held, put_b)
        if stage < 2:
            ahead = lambda b, h: r_out[b]
        else:
            ahead = lambda b, h: listed[h, SRC_LATE] + listed[h, MASS] * ext[b]
        send(ext, table, lists, listed, ahead, (msg0, msg1))

    ext = pltpu.VMEM((ROWS, 8, LANES), F32)
    message = shape(2 * HALO * COMP, LANES)
    full = shape(2 * NB, 8, LANES)
    lam = shape(NB // STEP, STEP * COMP, LANES)
    scratch = [ext, ext]
    if stage == 0:
        coef = shape(NB, TILES, 8, LANES)
        outs = [full, full, message, message, coef, coef]
        ins = [SMEM] + [VMEM] * 10 + [ANY] * 2
        scratch.append(pltpu.SemaphoreType.DMA((2, CHUNKS)))
    else:
        outs = [full, full, message, message, lam] if stage == 1 else [message, message, lam]
        ins = [VMEM] * 8
    return pl.pallas_call(
        kernel,
        out_shape=outs,
        in_specs=[SMEM] * 3 + ins,
        out_specs=[VMEM] * len(outs),
        scratch_shapes=scratch,
        compiler_params=PARAMS,
        name=f"step{stage}",
    )


def pick(small, index):
    hit = index[..., None] == lax.iota(jnp.int32, HALO)
    return jnp.sum(jnp.where(hit, small, 0), axis=-1)


def per_device(
    source,
    terminal,
    jacobian,
    face_coef,
    cell_coef,
    neighbours,
    send_blocks,
    live_count,
    volume,
    shape_field,
    weights,
):
    count = lax.axis_size("space")
    rounds = lax.axis_size("tm")
    core = lax.axis_index("space") % 2

    swap = [(d, d ^ 1) for d in range(count)]
    near, far = [], []
    for d in range(count):
        out = 2 * (d % 2) - 1
        if 0 <= d + out < count:
            near.append((d, d + out))
        if 0 <= d - 3 * out < count:
            far.append((d, d - 3 * out))

    def exchange(first, second):
        return lax.ppermute(first, "space", near), lax.ppermute(second, "space", far)

    mine = pl.pallas_call(
        prep_kernel,
        out_shape=shape(NB, TILES, 8, LANES),
        in_specs=[SMEM] + [VMEM] * 5,
        out_specs=VMEM,
        compiler_params=PARAMS,
        name="prep",
    )(live_count, jacobian[0], source, face_coef, cell_coef, volume)
    other = lax.ppermute(mine, "space", swap)

    lists_own = jnp.pad(send_blocks[0].reshape(2 * HALO, 1), ((0, NB - 2 * HALO), (0, 0)))
    ints = jnp.concatenate([neighbours, lists_own], axis=1)
    ints_other = lax.ppermute(ints, "space", swap)
    near_own = neighbours
    near_other = ints_other[:, :NEI]
    sends_other = ints_other[: 2 * HALO, NEI].reshape(2, HALO)
    low_own, high_own = send_blocks[0, 0], send_blocks[0, 1]
    low_other, high_other = sends_other[0], sends_other[1]
    is_low = core == 0
    out_own = jnp.where(is_low, low_own, high_own)
    in_own = jnp.where(is_low, high_own, low_own)
    out_other = jnp.where(is_low, high_other, low_other)
    in_other = jnp.where(is_low, low_other, high_other)

    def place(slots, base, outward, rim_base, partner_base, partner_list):
        side = (slots - NB) // HALO
        order = (slots - NB) % HALO
        across = partner_base + pick(partner_list, order)
        value = jnp.where(side == outward, rim_base + order, across)
        value = jnp.where(slots < NB, base + slots, value)
        return jnp.where(slots >= NB + 2 * HALO, ZERO, value)

    table = jnp.concatenate(
        [
            place(near_own, 0, core, 2 * NB, NB, in_other),
            place(near_other, NB, 1 - core, 2 * NB + HALO, 0, in_own),
        ]
    ).reshape(-1)
    lists = jnp.concatenate([out_own, out_other])

    listed = pl.pallas_call(
        pluck_kernel,
        out_shape=shape(2 * HALO, TILES, 8, LANES),
        in_specs=[SMEM] + [ANY] * 2,
        out_specs=VMEM,
        scratch_shapes=[pltpu.SemaphoreType.DMA((2 * HALO,))],
        compiler_params=PARAMS,
        name="pluck",
    )(lists, mine, other)
    listed_next = lax.ppermute(listed, "tm", [(t, t + 1) for t in range(rounds - 1)])

    def rim_message(half, slots, chosen):
        tiles = listed[half * HALO : (half + 1) * HALO, FACE : PRE + 1]
        hit = chosen[:, None] == lax.iota(jnp.int32, NB)
        picked = jnp.sum(jnp.where(hit[..., None], slots.astype(F32), 0.0), axis=1)
        wide = jnp.broadcast_to(
            jnp.pad(picked, ((0, 0), (0, LANES - NEI)))[:, None, None, :], (HALO, 1, 8, LANES)
        )
        return jnp.concatenate([tiles, wide], axis=1)

    rim0, rim1 = exchange(rim_message(0, near_own, out_own), rim_message(1, near_other, out_other))
    rim = jnp.concatenate([rim0[:, :2], rim1[:, :2]])

    def fix(message, outward, base, sent):
        slots = message[:, 2, 0, :NEI].astype(jnp.int32)
        side = (slots - NB) // HALO
        order = (slots - NB) % HALO
        valid = (slots >= NB) & (slots < NB + 2 * HALO) & (side == outward)
        return jnp.where(valid, base + pick(sent, order), ZERO)

    fixes = jnp.concatenate(
        [fix(rim0, 1 - core, 0, out_own), fix(rim1, core, NB, out_other)]
    ).reshape(-1)

    message = shape(2 * HALO * COMP, LANES)
    first_call = pl.pallas_call(
        first_kernel,
        out_shape=[message, message],
        in_specs=[SMEM] * 2 + [VMEM] * 3,
        out_specs=[VMEM] * 2,
        scratch_shapes=[pltpu.VMEM((ROWS, 8, LANES), F32)],
        compiler_params=PARAMS,
        name="first",
    )
    steps = [make_step(stage) for stage in range(3)]

    flag = (lax.axis_index("tm") == rounds - 1).astype(jnp.int32).reshape(1)
    live = (lax.iota(jnp.int32, NB) < live_count[0]).astype(F32)[:, None, None]
    start = (live * terminal).reshape(NB // STEP, STEP * COMP, LANES)
    start_other = lax.ppermute(start, "space", swap)
    begun = (start, start_other, *exchange(*first_call(table, lists, start, start_other, listed)))

    def slab(moved):
        x, fixed, msg0, msg1, coef0, coef1 = steps[0](
            table, lists, fixes, flag, *moved, *begun, rim, listed, mine, other
        )
        got = exchange(msg0, msg1)
        x, fixed, msg0, msg1, late = steps[1](
            table, lists, fixes, x, fixed, *got, rim, listed, coef0, coef1
        )
        got = exchange(msg0, msg1)
        *sent, early = steps[2](table, lists, fixes, x, fixed, *got, rim, listed_next, coef0, coef1)
        return early, late, sent

    def earlier(pairs):
        return [(t * count + d, (t - 1) * count + e) for t in range(1, rounds) for d, e in pairs]

    both = ("tm", "space")
    same = [(d, d) for d in range(count)]

    def turn(step_index, moved):
        early, _, (msg0, msg1) = slab(moved)
        half = lax.ppermute(early, both, earlier(same))
        got0 = lax.ppermute(msg0, both, earlier(near))
        got1 = lax.ppermute(msg1, both, earlier(far))
        return (half, lax.ppermute(half, "space", swap), got0, got1)

    moved = lax.fori_loop(0, rounds - 1, turn, begun)
    early, late, _ = slab(moved)
    fields = jnp.stack([early, late]).reshape(2, NB, COMP, LANES)
    part = jnp.sum(weights[:, None] * jnp.sum(fields * shape_field[None], axis=(2, 3)), axis=0)
    copies = jnp.broadcast_to(part, (rounds, *part.shape))
    sensitivity = lax.all_to_all(copies, "tm", split_axis=0, concat_axis=0, tiled=True).sum(axis=0)
    return fields, sensitivity


def solution(mesh):
    return jax.shard_map(
        per_device,
        mesh=mesh,
        in_specs=(
            P("tm", "space", None, None),
            P("space", None, None),
            P("tm", "space", None, None, None),
            P("space", None, None),
            P("space", None),
            P("space", None),
            P("space", None, None),
            P("space"),
            P("space", None),
            P("space", None, None),
            P("tm"),
        ),
        out_specs=(P("tm", "space", None, None), P("space")),
        check_vma=False,
    )
```

time: 761 us -> 676 us (0.89)
  Pallas kernels: 301 us -> 217 us
  local copies, waits for them, and re-layouts: 26.8 us -> 17.1 us
  waiting for transfers between devices: 245 us -> 254 us
    pallas_call x32 -> x26, Pallas kernels: 296 us -> 212 us  [the longest x8 73.2 us: slab(): steps[0]]
    ppermute x15 -> x30, waiting for transfers between devices: 87.2 us -> 137 us  [the longest x7 96.1 us: turn(): half = lax.ppermute(early, both, earlier(same))]
    ppermute x25 -> x18, waiting for transfers between devices: 78 us -> 41.7 us  [exchange(): lax.ppermute(first, 'space', near)]
    ppermute x25 -> x18, starting transfers between devices: 109 us -> 77.2 us  [exchange(): lax.ppermute(first, 'space', near)]
    ppermute x15 -> x30, starting transfers between devices: 13.6 us -> 39 us  [the longest x7 9.04 us: turn(): got1 = lax.ppermute(msg1, both, earlier(far))]
    ppermute x25 -> x18, waiting for transfers between devices: 75.9 us -> 64.9 us  [exchange(): lax.ppermute(second, 'space', far)]
    ppermute x25 -> x18, starting transfers between devices: 48.2 us -> 43.8 us  [exchange(): lax.ppermute(second, 'space', far)]
  transfers between devices with their start and end apart: 68 -> 69, of which waited for: 66 -> 49; matrix products, arithmetic and copies ran while one was open for 2% -> 2% of each run, Pallas kernels for 0% -> 1%
where the time goes in v2:
time: 676 us; the launch traced here: 672 us
  waiting for transfers between devices  254 us (38%)
  Pallas kernels  217 us (32%)
  starting transfers between devices  173 us (26%)
  local copies, waits for them, and re-layouts  17.1 us (3%)
  other arithmetic  8.23 us (1%)
    ppermute x7, waiting for transfers between devices, turn(): half = lax.ppermute(early, both, earlier(same))  96.1 us
    ppermute x18, starting transfers between devices, exchange(): lax.ppermute(first, 'space', near)  77.2 us
    pallas_call x8, Pallas kernels, slab(): steps[0]  73.2 us
    pallas_call x8, Pallas kernels, slab(): steps[1](table, lists, fixes, x, fixed, *got, rim, listed, coef0, coef1)  67.6 us
    pallas_call x8, Pallas kernels, slab(): steps[2]  67.4 us
    ppermute x18, waiting for transfers between devices, exchange(): lax.ppermute(second, 'space', far)  64.9 us
    ppermute x18, starting transfers between devices, exchange(): lax.ppermute(second, 'space', far)  43.8 us
    ppermute x18, waiting for transfers between devices, exchange(): lax.ppermute(first, 'space', near)  41.7 us
  transfers between devices with their start and end apart: 69, of which 49 were waited for; matrix products, arithmetic and copies ran while one was open for 2% of the time, Pallas kernels for 1%

profile of v2, /device:TPU:113, one launch (start us, length us, event | category | flops | bytes accessed | tf_op | source)
XLA Modules:
  0.0 671.7 jit_solution(12263035099550756920)
XLA Ops:
  45.1 22.3 %collective-permute-done.14.refs_8_ = f32[160,128]{1,0:T(8,128)S(1)} collective-permute-done((f32[160,128]{1,0:T(8,128)S(1)}, f32[160,128]{1,0:T(8,128)S(1)}, u32[]{:S(2)}, u32[]{:S(2)}) %collective-permute-start.14) | collective-permute-done | bytes 81952 | tf_op jit(solution)/shard_map/ppermute | solution.py:336
  74.0 520.8 %while.16 = (s32[]{:T(128)}, f32[16,40,128]{2,1,0:T(8,128)S(1)}, f32[16,40,128]{2,1,0:T(8,128)S(1)}, f32[160,128]{1,0:T(8,128)S(1)}, f32[160,128]{1,0:T(8,128)S(...) while((s32[]{:T(128)}, f32[16,40,128]{2,1,0:T(8,128)S(1)}, ...), condition=%wide.region_7.8_spmd, body=%wide.region_6.7_spmd.sunk | while | flops 2 | bytes 4588013 | solution.py:455
  74.0 9.2 %step0.3 = (f32[256,8,128]{2,1,0:T(8,128)S(1)}, f32[256,8,128]{2,1,0:T(8,128)S(1)}, f32[160,128]{1,0:T(8,128)S(1)}, f32[160,128]{1,0:T(8,128)S(1)}, f32[128,10,8...) custom-call(s32[1536]{0:T(1024)S(1)} %get-tuple-element.375.table, s32[32]{0:T(128)S(1)} %get-tuple-element.376.lists, ...), custom_call_target="tpu_custom_call" | custom-call | tf_op jit(solution)/shard_map/while/body/eval_jaxpr/step0/pallas_call | solution.py:431
  96.1 8.4 %step1.3 = (f32[256,8,128]{2,1,0:T(8,128)S(1)}, f32[256,8,128]{2,1,0:T(8,128)S(1)}, f32[160,128]{1,0:T(8,128)S(1)}, f32[160,128]{1,0:T(8,128)S(1)}, f32[16,40,128]{2,1,0:T(8,128)}) custom-call(s32[1536]{0:T(1024)S(1)} %get-tuple-element.375.table, s32[32]{0:T(128)S(1)} %get-tuple-element.376.lists, s32[192]{0:T(256)S(1)} %get-tuple-element.377.fixes, ...), custom_call_target="tpu_custom_call" | custom-call | tf_op jit(solution)/shard_map/while/body/eval_jaxpr/step1/pallas_call | solution.py:435
  116.3 8.3 %step2.3 = (f32[160,128]{1,0:T(8,128)S(1)}, f32[160,128]{1,0:T(8,128)S(1)}, f32[16,40,128]{2,1,0:T(8,128)S(1)}) custom-call(s32[1536]{0:T(1024)S(1)} %get-tuple-element.375.table, s32[32]{0:T(128)S(1)} %get-tuple-element.376.lists, s32[192]{0:T(256)S(1)} %get-tuple-element.377.fixes, f32[256,8,128]{2,1,0:T(8,128)S(1)} %get-tuple-element.325.refs_0_, ...), custom_call_target="tpu_custom_call" | custom-call | tf_op jit(solution)/shard_map/while/body/eval_jaxpr/step2/pallas_call | solution.py:439
  125.9 9.4 %collective-permute-done.4 = f32[16,40,128]{2,1,0:T(8,128)S(1)} collective-permute-done((f32[16,40,128]{2,1,0:T(8,128)S(1)}, f32[16,40,128]{2,1,0:T(8,128)S(1)}, u32[]{:S(2)}, u32[]{:S(2)}) %collective-permute-start.4) | collective-permute-done | bytes 327712 | tf_op jit(solution)/shard_map/while/body/eval_jaxpr/ppermute | solution.py:450
  145.1 9.2 %step0.3 = (f32[256,8,128]{2,1,0:T(8,128)S(1)}, f32[256,8,128]{2,1,0:T(8,128)S(1)}, f32[160,128]{1,0:T(8,128)S(1)}, f32[160,128]{1,0:T(8,128)S(1)}, f32[128,10,8...) custom-call(s32[1536]{0:T(1024)S(1)} %get-tuple-element.375.table, s32[32]{0:T(128)S(1)} %get-tuple-element.376.lists, ...), custom_call_target="tpu_custom_call" | custom-call | tf_op jit(solution)/shard_map/while/body/eval_jaxpr/step0/pallas_call | solution.py:431
  168.6 8.4 %step1.3 = (f32[256,8,128]{2,1,0:T(8,128)S(1)}, f32[256,8,128]{2,1,0:T(8,128)S(1)}, f32[160,128]{1,0:T(8,128)S(1)}, f32[160,128]{1,0:T(8,128)S(1)}, f32[16,40,128]{2,1,0:T(8,128)}) custom-call(s32[1536]{0:T(1024)S(1)} %get-tuple-element.375.table, s32[32]{0:T(128)S(1)} %get-tuple-element.376.lists, s32[192]{0:T(256)S(1)} %get-tuple-element.377.fixes, ...), custom_call_target="tpu_custom_call" | custom-call | tf_op jit(solution)/shard_map/while/body/eval_jaxpr/step1/pallas_call | solution.py:435
  188.2 8.3 %step2.3 = (f32[160,128]{1,0:T(8,128)S(1)}, f32[160,128]{1,0:T(8,128)S(1)}, f32[16,40,128]{2,1,0:T(8,128)S(1)}) custom-call(s32[1536]{0:T(1024)S(1)} %get-tuple-element.375.table, s32[32]{0:T(128)S(1)} %get-tuple-element.376.lists, s32[192]{0:T(256)S(1)} %get-tuple-element.377.fixes, f32[256,8,128]{2,1,0:T(8,128)S(1)} %get-tuple-element.325.refs_0_, ...), custom_call_target="tpu_custom_call" | custom-call | tf_op jit(solution)/shard_map/while/body/eval_jaxpr/step2/pallas_call | solution.py:439
  197.8 12.6 %collective-permute-done.4 = f32[16,40,128]{2,1,0:T(8,128)S(1)} collective-permute-done((f32[16,40,128]{2,1,0:T(8,128)S(1)}, f32[16,40,128]{2,1,0:T(8,128)S(1)}, u32[]{:S(2)}, u32[]{:S(2)}) %collective-permute-start.4) | collective-permute-done | bytes 327712 | tf_op jit(solution)/shard_map/while/body/eval_jaxpr/ppermute | solution.py:450
  219.1 9.2 %step0.3 = (f32[256,8,128]{2,1,0:T(8,128)S(1)}, f32[256,8,128]{2,1,0:T(8,128)S(1)}, f32[160,128]{1,0:T(8,128)S(1)}, f32[160,128]{1,0:T(8,128)S(1)}, f32[128,10,8...) custom-call(s32[1536]{0:T(1024)S(1)} %get-tuple-element.375.table, s32[32]{0:T(128)S(1)} %get-tuple-element.376.lists, ...), custom_call_target="tpu_custom_call" | custom-call | tf_op jit(solution)/shard_map/while/body/eval_jaxpr/step0/pallas_call | solution.py:431
  241.0 8.4 %step1.3 = (f32[256,8,128]{2,1,0:T(8,128)S(1)}, f32[256,8,128]{2,1,0:T(8,128)S(1)}, f32[160,128]{1,0:T(8,128)S(1)}, f32[160,128]{1,0:T(8,128)S(1)}, f32[16,40,128]{2,1,0:T(8,128)}) custom-call(s32[1536]{0:T(1024)S(1)} %get-tuple-element.375.table, s32[32]{0:T(128)S(1)} %get-tuple-element.376.lists, s32[192]{0:T(256)S(1)} %get-tuple-element.377.fixes, ...), custom_call_target="tpu_custom_call" | custom-call | tf_op jit(solution)/shard_map/while/body/eval_jaxpr/step1/pallas_call | solution.py:435
  270.1 15.9 %collective-permute-done.4 = f32[16,40,128]{2,1,0:T(8,128)S(1)} collective-permute-done((f32[16,40,128]{2,1,0:T(8,128)S(1)}, f32[16,40,128]{2,1,0:T(8,128)S(1)}, u32[]{:S(2)}, u32[]{:S(2)}) %collective-permute-start.4) | collective-permute-done | bytes 327712 | tf_op jit(solution)/shard_map/while/body/eval_jaxpr/ppermute | solution.py:450
  294.7 9.2 %step0.3 = (f32[256,8,128]{2,1,0:T(8,128)S(1)}, f32[256,8,128]{2,1,0:T(8,128)S(1)}, f32[160,128]{1,0:T(8,128)S(1)}, f32[160,128]{1,0:T(8,128)S(1)}, f32[128,10,8...) custom-call(s32[1536]{0:T(1024)S(1)} %get-tuple-element.375.table, s32[32]{0:T(128)S(1)} %get-tuple-element.376.lists, ...), custom_call_target="tpu_custom_call" | custom-call | tf_op jit(solution)/shard_map/while/body/eval_jaxpr/step0/pallas_call | solution.py:431
  316.2 8.4 %step1.3 = (f32[256,8,128]{2,1,0:T(8,128)S(1)}, f32[256,8,128]{2,1,0:T(8,128)S(1)}, f32[160,128]{1,0:T(8,128)S(1)}, f32[160,128]{1,0:T(8,128)S(1)}, f32[16,40,128]{2,1,0:T(8,128)}) custom-call(s32[1536]{0:T(1024)S(1)} %get-tuple-element.375.table, s32[32]{0:T(128)S(1)} %get-tuple-element.376.lists, s32[192]{0:T(256)S(1)} %get-tuple-element.377.fixes, ...), custom_call_target="tpu_custom_call" | custom-call | tf_op jit(solution)/shard_map/while/body/eval_jaxpr/step1/pallas_call | solution.py:435
  336.1 8.3 %step2.3 = (f32[160,128]{1,0:T(8,128)S(1)}, f32[160,128]{1,0:T(8,128)S(1)}, f32[16,40,128]{2,1,0:T(8,128)S(1)}) custom-call(s32[1536]{0:T(1024)S(1)} %get-tuple-element.375.table, s32[32]{0:T(128)S(1)} %get-tuple-element.376.lists, s32[192]{0:T(256)S(1)} %get-tuple-element.377.fixes, f32[256,8,128]{2,1,0:T(8,128)S(1)} %get-tuple-element.325.refs_0_, ...), custom_call_target="tpu_custom_call" | custom-call | tf_op jit(solution)/shard_map/while/body/eval_jaxpr/step2/pallas_call | solution.py:439
  345.7 14.6 %collective-permute-done.4 = f32[16,40,128]{2,1,0:T(8,128)S(1)} collective-permute-done((f32[16,40,128]{2,1,0:T(8,128)S(1)}, f32[16,40,128]{2,1,0:T(8,128)S(1)}, u32[]{:S(2)}, u32[]{:S(2)}) %collective-permute-start.4) | collective-permute-done | bytes 327712 | tf_op jit(solution)/shard_map/while/body/eval_jaxpr/ppermute | solution.py:450
  369.8 9.2 %step0.3 = (f32[256,8,128]{2,1,0:T(8,128)S(1)}, f32[256,8,128]{2,1,0:T(8,128)S(1)}, f32[160,128]{1,0:T(8,128)S(1)}, f32[160,128]{1,0:T(8,128)S(1)}, f32[128,10,8...) custom-call(s32[1536]{0:T(1024)S(1)} %get-tuple-element.375.table, s32[32]{0:T(128)S(1)} %get-tuple-element.376.lists, ...), custom_call_target="tpu_custom_call" | custom-call | tf_op jit(solution)/shard_map/while/body/eval_jaxpr/step0/pallas_call | solution.py:431
  391.2 8.4 %step1.3 = (f32[256,8,128]{2,1,0:T(8,128)S(1)}, f32[256,8,128]{2,1,0:T(8,128)S(1)}, f32[160,128]{1,0:T(8,128)S(1)}, f32[160,128]{1,0:T(8,128)S(1)}, f32[16,40,128]{2,1,0:T(8,128)}) custom-call(s32[1536]{0:T(1024)S(1)} %get-tuple-element.375.table, s32[32]{0:T(128)S(1)} %get-tuple-element.376.lists, s32[192]{0:T(256)S(1)} %get-tuple-element.377.fixes, ...), custom_call_target="tpu_custom_call" | custom-call | tf_op jit(solution)/shard_map/while/body/eval_jaxpr/step1/pallas_call | solution.py:435
  411.1 8.3 %step2.3 = (f32[160,128]{1,0:T(8,128)S(1)}, f32[160,128]{1,0:T(8,128)S(1)}, f32[16,40,128]{2,1,0:T(8,128)S(1)}) custom-call(s32[1536]{0:T(1024)S(1)} %get-tuple-element.375.table, s32[32]{0:T(128)S(1)} %get-tuple-element.376.lists, s32[192]{0:T(256)S(1)} %get-tuple-element.377.fixes, f32[256,8,128]{2,1,0:T(8,128)S(1)} %get-tuple-element.325.refs_0_, ...), custom_call_target="tpu_custom_call" | custom-call | tf_op jit(solution)/shard_map/while/body/eval_jaxpr/step2/pallas_call | solution.py:439
  420.8 14.5 %collective-permute-done.4 = f32[16,40,128]{2,1,0:T(8,128)S(1)} collective-permute-done((f32[16,40,128]{2,1,0:T(8,128)S(1)}, f32[16,40,128]{2,1,0:T(8,128)S(1)}, u32[]{:S(2)}, u32[]{:S(2)}) %collective-permute-start.4) | collective-permute-done | bytes 327712 | tf_op jit(solution)/shard_map/while/body/eval_jaxpr/ppermute | solution.py:450
  444.8 9.2 %step0.3 = (f32[256,8,128]{2,1,0:T(8,128)S(1)}, f32[256,8,128]{2,1,0:T(8,128)S(1)}, f32[160,128]{1,0:T(8,128)S(1)}, f32[160,128]{1,0:T(8,128)S(1)}, f32[128,10,8...) custom-call(s32[1536]{0:T(1024)S(1)} %get-tuple-element.375.table, s32[32]{0:T(128)S(1)} %get-tuple-element.376.lists, ...), custom_call_target="tpu_custom_call" | custom-call | tf_op jit(solution)/shard_map/while/body/eval_jaxpr/step0/pallas_call | solution.py:431
  466.2 8.4 %step1.3 = (f32[256,8,128]{2,1,0:T(8,128)S(1)}, f32[256,8,128]{2,1,0:T(8,128)S(1)}, f32[160,128]{1,0:T(8,128)S(1)}, f32[160,128]{1,0:T(8,128)S(1)}, f32[16,40,128]{2,1,0:T(8,128)}) custom-call(s32[1536]{0:T(1024)S(1)} %get-tuple-element.375.table, s32[32]{0:T(128)S(1)} %get-tuple-element.376.lists, s32[192]{0:T(256)S(1)} %get-tuple-element.377.fixes, ...), custom_call_target="tpu_custom_call" | custom-call | tf_op jit(solution)/shard_map/while/body/eval_jaxpr/step1/pallas_call | solution.py:435
  486.1 8.3 %step2.3 = (f32[160,128]{1,0:T(8,128)S(1)}, f32[160,128]{1,0:T(8,128)S(1)}, f32[16,40,128]{2,1,0:T(8,128)S(1)}) custom-call(s32[1536]{0:T(1024)S(1)} %get-tuple-element.375.table, s32[32]{0:T(128)S(1)} %get-tuple-element.376.lists, s32[192]{0:T(256)S(1)} %get-tuple-element.377.fixes, f32[256,8,128]{2,1,0:T(8,128)S(1)} %get-tuple-element.325.refs_0_, ...), custom_call_target="tpu_custom_call" | custom-call | tf_op jit(solution)/shard_map/while/body/eval_jaxpr/step2/pallas_call | solution.py:439
  495.8 14.5 %collective-permute-done.4 = f32[16,40,128]{2,1,0:T(8,128)S(1)} collective-permute-done((f32[16,40,128]{2,1,0:T(8,128)S(1)}, f32[16,40,128]{2,1,0:T(8,128)S(1)}, u32[]{:S(2)}, u32[]{:S(2)}) %collective-permute-start.4) | collective-permute-done | bytes 327712 | tf_op jit(solution)/shard_map/while/body/eval_jaxpr/ppermute | solution.py:450
  519.8 9.2 %step0.3 = (f32[256,8,128]{2,1,0:T(8,128)S(1)}, f32[256,8,128]{2,1,0:T(8,128)S(1)}, f32[160,128]{1,0:T(8,128)S(1)}, f32[160,128]{1,0:T(8,128)S(1)}, f32[128,10,8...) custom-call(s32[1536]{0:T(1024)S(1)} %get-tuple-element.375.table, s32[32]{0:T(128)S(1)} %get-tuple-element.376.lists, ...), custom_call_target="tpu_custom_call" | custom-call | tf_op jit(solution)/shard_map/while/body/eval_jaxpr/step0/pallas_call | solution.py:431
  541.1 8.4 %step1.3 = (f32[256,8,128]{2,1,0:T(8,128)S(1)}, f32[256,8,128]{2,1,0:T(8,128)S(1)}, f32[160,128]{1,0:T(8,128)S(1)}, f32[160,128]{1,0:T(8,128)S(1)}, f32[16,40,128]{2,1,0:T(8,128)}) custom-call(s32[1536]{0:T(1024)S(1)} %get-tuple-element.375.table, s32[32]{0:T(128)S(1)} %get-tuple-element.376.lists, s32[192]{0:T(256)S(1)} %get-tuple-element.377.fixes, ...), custom_call_target="tpu_custom_call" | custom-call | tf_op jit(solution)/shard_map/while/body/eval_jaxpr/step1/pallas_call | solution.py:435
  570.8 14.5 %collective-permute-done.4 = f32[16,40,128]{2,1,0:T(8,128)S(1)} collective-permute-done((f32[16,40,128]{2,1,0:T(8,128)S(1)}, f32[16,40,128]{2,1,0:T(8,128)S(1)}, u32[]{:S(2)}, u32[]{:S(2)}) %collective-permute-start.4) | collective-permute-done | bytes 327712 | tf_op jit(solution)/shard_map/while/body/eval_jaxpr/ppermute | solution.py:450
  594.8 9.2 %step0.2 = (f32[256,8,128]{2,1,0:T(8,128)S(1)}, f32[256,8,128]{2,1,0:T(8,128)S(1)}, f32[160,128]{1,0:T(8,128)S(1)}, f32[160,128]{1,0:T(8,128)S(1)}, f32[128,10,8...) custom-call(s32[1536]{0:T(1024)S(1)} %get-tuple-element.426, s32[32]{0:T(128)S(1)} %get-tuple-element.428, ...), custom_call_target="tpu_custom_call" | custom-call | tf_op jit(solution)/shard_map/step0/pallas_call | solution.py:431
  616.2 8.4 %step1.2 = (f32[256,8,128]{2,1,0:T(8,128)S(1)}, f32[256,8,128]{2,1,0:T(8,128)S(1)}, f32[160,128]{1,0:T(8,128)S(1)}, f32[160,128]{1,0:T(8,128)S(1)}, f32[16,40,128]{2,1,0:T(8,128)S(1)}) custom-call(s32[1536]{0:T(1024)S(1)} %get-tuple-element.426, s32[32]{0:T(128)S(1)} %get-tuple-element.428, s32[192]{0:T(256)S(1)} %get-tuple-element.427, ...), custom_call_target="tpu_custom_call" | custom-call | tf_op jit(solution)/shard_map/step1/pallas_call | solution.py:435
  641.2 9.0 %step2.2 = (f32[160,128]{1,0:T(8,128)}, f32[160,128]{1,0:T(8,128)}, f32[16,40,128]{2,1,0:T(8,128)S(1)}) custom-call(s32[1536]{0:T(1024)S(1)} %get-tuple-element.426, s32[32]{0:T(128)S(1)} %get-tuple-element.428, s32[192]{0:T(256)S(1)} %get-tuple-element.427, f32[256,8,128]{2,1,0:T(8,128)S(1)} %get-tuple-element.136.refs_0_, ...), custom_call_target="tpu_custom_call" | custom-call | tf_op jit(solution)/shard_map/step2/pallas_call | solution.py:439
  654.1 12.1 %all-to-all-start = ((f32[8,1,128]{2,1,0:T(1,128)}), f32[8,1,128]{2,1,0:T(1,128)S(1)}, u32[]{:S(2)}, u32[]{:S(2)}) async-start(f32[8,1,128]{2,1,0:T(1,128)} %broadcast_in_dim.106), calls=%async_computation | async-start | bytes 8192 | tf_op jit(solution)/shard_map/all_to_all | solution.py:460
  (227 shorter events, 347.3 us)
Async XLA Ops:
  10.8 9.9 %collective-permute-start.9 = (f32[128,10,8,128]{3,2,1,0:T(8,128)}, f32[128,10,8,128]{3,2,1,0:T(8,128)}, u32[]{:S(2)}, u32[]{:S(2)}) collective-permute-start(f32[128,10,8,128]{3,2,1,0:T(8,128)} %prep.1.mine.refs_11_), channel_id=1, source_target_pairs={{0,1},{1,0},{2,3},{3,2},{4,5},{5,4},{6,7},{7,6},{8,9},{9,8},{10,11... | collective-permute-start | bytes 15728648 | tf_op jit(solution)/shard_map/ppermute | solution.py:346
  12.0 15.9 %collective-permute-start.12 = (f32[16,40,128]{2,1,0:T(8,128)S(1)}, f32[16,40,128]{2,1,0:T(8,128)S(1)}, u32[]{:S(2)}, u32[]{:S(2)}) collective-permute-start(f32[16,40,128]{2,1,0:T(8,128)S(1)} %reshape.159.mine.refs_5_), channel_id=1, source_target_pairs={{0,1},{1,0},{2,3},{3,2},{4,5},{5,4},{6,7},{7,6},{8,9},{9,8},{10,11... | collective-permute-start | bytes 983048 | tf_op jit(solution)/shard_map/ppermute | solution.py:427
  22.9 44.6 %collective-permute-start.10 = (f32[16,3,8,128]{3,2,1,0:T(8,128)S(1)}, f32[16,3,8,128]{3,2,1,0:T(8,128)}, u32[]{:S(2)}, u32[]{:S(2)}) collective-permute-start(f32[16,3,8,128]{3,2,1,0:T(8,128)S(1)} %pad_maximum_fusion.1), channel_id=1, source_target_pairs={{1,2},{2,1},{3,4},{4,3},{5,6},{6,5},{7,8},{8,7},{9,10},{10,9},{11,... | collective-permute-start | bytes 589832 | tf_op jit(solution)/shard_map/ppermute | solution.py:336
  28.0 46.0 %collective-permute-start.15 = (f32[32,10,8,128]{3,2,1,0:T(8,128)S(1)}, f32[32,10,8,128]{3,2,1,0:T(8,128)}, u32[]{:S(2)}, u32[]{:S(2)}) collective-permute-start(f32[32,10,8,128]{3,2,1,0:T(8,128)S(1)} %pluck.1.listed.refs_10_.refs_5_), channel_id=1, source_target_pairs={{0,32},{32,64},{64,96},{96,128},{128,160},{160,192},{192,224},{1,3... | collective-permute-start | bytes 3932168 | tf_op jit(solution)/shard_map/ppermute | solution.py:387
  34.2 10.9 %collective-permute-start.13 = (f32[160,128]{1,0:T(8,128)S(1)}, f32[160,128]{1,0:T(8,128)S(1)}, u32[]{:S(2)}, u32[]{:S(2)}) collective-permute-start(f32[160,128]{1,0:T(8,128)S(1)} %get-tuple-element.124), channel_id=1, source_target_pairs={{1,2},{2,1},{3,4},{4,3},{5,6},{6,5},{7,8},{8,7},{9,10},{10,9},{11,... | collective-permute-start | bytes 245768 | tf_op jit(solution)/shard_map/ppermute | solution.py:336
  37.3 30.1 %collective-permute-start.14 = (f32[160,128]{1,0:T(8,128)S(1)}, f32[160,128]{1,0:T(8,128)S(1)}, u32[]{:S(2)}, u32[]{:S(2)}) collective-permute-start(f32[160,128]{1,0:T(8,128)S(1)} %get-tuple-element.125), channel_id=1, source_target_pairs={{0,3},{2,5},{3,0},{4,7},{5,2},{6,9},{7,4},{8,11},{9,6},{10,13},{11... | collective-permute-start | bytes 245768 | tf_op jit(solution)/shard_map/ppermute | solution.py:336
  40.3 29.1 %collective-permute-start.11 = (f32[16,3,8,128]{3,2,1,0:T(8,128)}, f32[16,3,8,128]{3,2,1,0:T(8,128)}, u32[]{:S(2)}, u32[]{:S(2)}) collective-permute-start(f32[16,3,8,128]{3,2,1,0:T(8,128)} %pad_maximum_fusion.2), channel_id=1, source_target_pairs={{0,3},{2,5},{3,0},{4,7},{5,2},{6,9},{7,4},{8,11},{9,6},{10,13},{11... | collective-permute-start | bytes 589832 | tf_op jit(solution)/shard_map/ppermute | solution.py:336
  83.2 9.4 %collective-permute-start = (f32[160,128]{1,0:T(8,128)S(1)}, f32[160,128]{1,0:T(8,128)S(1)}, u32[]{:S(2)}, u32[]{:S(2)}) collective-permute-start(f32[160,128]{1,0:T(8,128)S(1)} %get-tuple-element.321), channel_id=1, source_target_pairs={{1,2},{2,1},{3,4},{4,3},{5,6},{6,5},{7,8},{8,7},{9,10},{10,9},{11,... | collective-permute-start | bytes 245768 | tf_op jit(solution)/shard_map/while/body/eval_jaxpr/ppermute | solution.py:336
  104.5 9.4 %collective-permute-start.2 = (f32[160,128]{1,0:T(8,128)S(1)}, f32[160,128]{1,0:T(8,128)S(1)}, u32[]{:S(2)}, u32[]{:S(2)}) collective-permute-start(f32[160,128]{1,0:T(8,128)S(1)} %get-tuple-element.327), channel_id=1, source_target_pairs={{1,2},{2,1},{3,4},{4,3},{5,6},{6,5},{7,8},{8,7},{9,10},{10,9},{11,... | collective-permute-start | bytes 245768 | tf_op jit(solution)/shard_map/while/body/eval_jaxpr/ppermute | solution.py:336
  124.6 10.7 %collective-permute-start.4 = (f32[16,40,128]{2,1,0:T(8,128)S(1)}, f32[16,40,128]{2,1,0:T(8,128)S(1)}, u32[]{:S(2)}, u32[]{:S(2)}) collective-permute-start(f32[16,40,128]{2,1,0:T(8,128)S(1)} %get-tuple-element.329), channel_id=1, source_target_pairs={{32,0},{33,1},{34,2},{35,3},{36,4},{37,5},{38,6},{39,7},{40,8},{41... | collective-permute-start | bytes 983048 | tf_op jit(solution)/shard_map/while/body/eval_jaxpr/ppermute | solution.py:450
  135.3 9.8 %collective-permute-start.5 = (f32[16,40,128]{2,1,0:T(8,128)S(1)}, f32[16,40,128]{2,1,0:T(8,128)S(1)}, u32[]{:S(2)}, u32[]{:S(2)}) collective-permute-start(f32[16,40,128]{2,1,0:T(8,128)S(1)} %collective-permute-done.4), channel_id=1, source_target_pairs={{0,1},{1,0},{2,3},{3,2},{4,5},{5,4},{6,7},{7,6},{8,9},{9,8},{10,11... | collective-permute-start | bytes 983048 | tf_op jit(solution)/shard_map/while/body/eval_jaxpr/ppermute | solution.py:453
  154.2 9.4 %collective-permute-start = (f32[160,128]{1,0:T(8,128)S(1)}, f32[160,128]{1,0:T(8,128)S(1)}, u32[]{:S(2)}, u32[]{:S(2)}) collective-permute-start(f32[160,128]{1,0:T(8,128)S(1)} %get-tuple-element.321), channel_id=1, source_target_pairs={{1,2},{2,1},{3,4},{4,3},{5,6},{6,5},{7,8},{8,7},{9,10},{10,9},{11,... | collective-permute-start | bytes 245768 | tf_op jit(solution)/shard_map/while/body/eval_jaxpr/ppermute | solution.py:336
  177.1 9.4 %collective-permute-start.2 = (f32[160,128]{1,0:T(8,128)S(1)}, f32[160,128]{1,0:T(8,128)S(1)}, u32[]{:S(2)}, u32[]{:S(2)}) collective-permute-start(f32[160,128]{1,0:T(8,128)S(1)} %get-tuple-element.327), channel_id=1, source_target_pairs={{1,2},{2,1},{3,4},{4,3},{5,6},{6,5},{7,8},{8,7},{9,10},{10,9},{11,... | collective-permute-start | bytes 245768 | tf_op jit(solution)/shard_map/while/body/eval_jaxpr/ppermute | solution.py:336
  196.5 13.9 %collective-permute-start.4 = (f32[16,40,128]{2,1,0:T(8,128)S(1)}, f32[16,40,128]{2,1,0:T(8,128)S(1)}, u32[]{:S(2)}, u32[]{:S(2)}) collective-permute-start(f32[16,40,128]{2,1,0:T(8,128)S(1)} %get-tuple-element.329), channel_id=1, source_target_pairs={{32,0},{33,1},{34,2},{35,3},{36,4},{37,5},{38,6},{39,7},{40,8},{41... | collective-permute-start | bytes 983048 | tf_op jit(solution)/shard_map/while/body/eval_jaxpr/ppermute | solution.py:450
  228.3 9.4 %collective-permute-start = (f32[160,128]{1,0:T(8,128)S(1)}, f32[160,128]{1,0:T(8,128)S(1)}, u32[]{:S(2)}, u32[]{:S(2)}) collective-permute-start(f32[160,128]{1,0:T(8,128)S(1)} %get-tuple-element.321), channel_id=1, source_target_pairs={{1,2},{2,1},{3,4},{4,3},{5,6},{6,5},{7,8},{8,7},{9,10},{10,9},{11,... | collective-permute-start | bytes 245768 | tf_op jit(solution)/shard_map/while/body/eval_jaxpr/ppermute | solution.py:336
  249.4 9.4 %collective-permute-start.2 = (f32[160,128]{1,0:T(8,128)S(1)}, f32[160,128]{1,0:T(8,128)S(1)}, u32[]{:S(2)}, u32[]{:S(2)}) collective-permute-start(f32[160,128]{1,0:T(8,128)S(1)} %get-tuple-element.327), channel_id=1, source_target_pairs={{1,2},{2,1},{3,4},{4,3},{5,6},{6,5},{7,8},{8,7},{9,10},{10,9},{11,... | collective-permute-start | bytes 245768 | tf_op jit(solution)/shard_map/while/body/eval_jaxpr/ppermute | solution.py:336
  268.8 17.2 %collective-permute-start.4 = (f32[16,40,128]{2,1,0:T(8,128)S(1)}, f32[16,40,128]{2,1,0:T(8,128)S(1)}, u32[]{:S(2)}, u32[]{:S(2)}) collective-permute-start(f32[16,40,128]{2,1,0:T(8,128)S(1)} %get-tuple-element.329), channel_id=1, source_target_pairs={{32,0},{33,1},{34,2},{35,3},{36,4},{37,5},{38,6},{39,7},{40,8},{41... | collective-permute-start | bytes 983048 | tf_op jit(solution)/shard_map/while/body/eval_jaxpr/ppermute | solution.py:450
  303.9 9.4 %collective-permute-start = (f32[160,128]{1,0:T(8,128)S(1)}, f32[160,128]{1,0:T(8,128)S(1)}, u32[]{:S(2)}, u32[]{:S(2)}) collective-permute-start(f32[160,128]{1,0:T(8,128)S(1)} %get-tuple-element.321), channel_id=1, source_target_pairs={{1,2},{2,1},{3,4},{4,3},{5,6},{6,5},{7,8},{8,7},{9,10},{10,9},{11,... | collective-permute-start | bytes 245768 | tf_op jit(solution)/shard_map/while/body/eval_jaxpr/ppermute | solution.py:336
  344.4 15.9 %collective-permute-start.4 = (f32[16,40,128]{2,1,0:T(8,128)S(1)}, f32[16,40,128]{2,1,0:T(8,128)S(1)}, u32[]{:S(2)}, u32[]{:S(2)}) collective-permute-start(f32[16,40,128]{2,1,0:T(8,128)S(1)} %get-tuple-element.329), channel_id=1, source_target_pairs={{32,0},{33,1},{34,2},{35,3},{36,4},{37,5},{38,6},{39,7},{40,8},{41... | collective-permute-start | bytes 983048 | tf_op jit(solution)/shard_map/while/body/eval_jaxpr/ppermute | solution.py:450
  360.3 9.5 %collective-permute-start.5 = (f32[16,40,128]{2,1,0:T(8,128)S(1)}, f32[16,40,128]{2,1,0:T(8,128)S(1)}, u32[]{:S(2)}, u32[]{:S(2)}) collective-permute-start(f32[16,40,128]{2,1,0:T(8,128)S(1)} %collective-permute-done.4), channel_id=1, source_target_pairs={{0,1},{1,0},{2,3},{3,2},{4,5},{5,4},{6,7},{7,6},{8,9},{9,8},{10,11... | collective-permute-start | bytes 983048 | tf_op jit(solution)/shard_map/while/body/eval_jaxpr/ppermute | solution.py:453
  379.0 9.4 %collective-permute-start = (f32[160,128]{1,0:T(8,128)S(1)}, f32[160,128]{1,0:T(8,128)S(1)}, u32[]{:S(2)}, u32[]{:S(2)}) collective-permute-start(f32[160,128]{1,0:T(8,128)S(1)} %get-tuple-element.321), channel_id=1, source_target_pairs={{1,2},{2,1},{3,4},{4,3},{5,6},{6,5},{7,8},{8,7},{9,10},{10,9},{11,... | collective-permute-start | bytes 245768 | tf_op jit(solution)/shard_map/while/body/eval_jaxpr/ppermute | solution.py:336
  419.5 15.8 %collective-permute-start.4 = (f32[16,40,128]{2,1,0:T(8,128)S(1)}, f32[16,40,128]{2,1,0:T(8,128)S(1)}, u32[]{:S(2)}, u32[]{:S(2)}) collective-permute-start(f32[16,40,128]{2,1,0:T(8,128)S(1)} %get-tuple-element.329), channel_id=1, source_target_pairs={{32,0},{33,1},{34,2},{35,3},{36,4},{37,5},{38,6},{39,7},{40,8},{41... | collective-permute-start | bytes 983048 | tf_op jit(solution)/shard_map/while/body/eval_jaxpr/ppermute | solution.py:450
  435.3 9.5 %collective-permute-start.5 = (f32[16,40,128]{2,1,0:T(8,128)S(1)}, f32[16,40,128]{2,1,0:T(8,128)S(1)}, u32[]{:S(2)}, u32[]{:S(2)}) collective-permute-start(f32[16,40,128]{2,1,0:T(8,128)S(1)} %collective-permute-done.4), channel_id=1, source_target_pairs={{0,1},{1,0},{2,3},{3,2},{4,5},{5,4},{6,7},{7,6},{8,9},{9,8},{10,11... | collective-permute-start | bytes 983048 | tf_op jit(solution)/shard_map/while/body/eval_jaxpr/ppermute | solution.py:453
  454.0 9.4 %collective-permute-start = (f32[160,128]{1,0:T(8,128)S(1)}, f32[160,128]{1,0:T(8,128)S(1)}, u32[]{:S(2)}, u32[]{:S(2)}) collective-permute-start(f32[160,128]{1,0:T(8,128)S(1)} %get-tuple-element.321), channel_id=1, source_target_pairs={{1,2},{2,1},{3,4},{4,3},{5,6},{6,5},{7,8},{8,7},{9,10},{10,9},{11,... | collective-permute-start | bytes 245768 | tf_op jit(solution)/shard_map/while/body/eval_jaxpr/ppermute | solution.py:336
  494.5 15.8 %collective-permute-start.4 = (f32[16,40,128]{2,1,0:T(8,128)S(1)}, f32[16,40,128]{2,1,0:T(8,128)S(1)}, u32[]{:S(2)}, u32[]{:S(2)}) collective-permute-start(f32[16,40,128]{2,1,0:T(8,128)S(1)} %get-tuple-element.329), channel_id=1, source_target_pairs={{32,0},{33,1},{34,2},{35,3},{36,4},{37,5},{38,6},{39,7},{40,8},{41... | collective-permute-start | bytes 983048 | tf_op jit(solution)/shard_map/while/body/eval_jaxpr/ppermute | solution.py:450
  510.3 9.5 %collective-permute-start.5 = (f32[16,40,128]{2,1,0:T(8,128)S(1)}, f32[16,40,128]{2,1,0:T(8,128)S(1)}, u32[]{:S(2)}, u32[]{:S(2)}) collective-permute-start(f32[16,40,128]{2,1,0:T(8,128)S(1)} %collective-permute-done.4), channel_id=1, source_target_pairs={{0,1},{1,0},{2,3},{3,2},{4,5},{5,4},{6,7},{7,6},{8,9},{9,8},{10,11... | collective-permute-start | bytes 983048 | tf_op jit(solution)/shard_map/while/body/eval_jaxpr/ppermute | solution.py:453
  529.0 9.4 %collective-permute-start = (f32[160,128]{1,0:T(8,128)S(1)}, f32[160,128]{1,0:T(8,128)S(1)}, u32[]{:S(2)}, u32[]{:S(2)}) collective-permute-start(f32[160,128]{1,0:T(8,128)S(1)} %get-tuple-element.321), channel_id=1, source_target_pairs={{1,2},{2,1},{3,4},{4,3},{5,6},{6,5},{7,8},{8,7},{9,10},{10,9},{11,... | collective-permute-start | bytes 245768 | tf_op jit(solution)/shard_map/while/body/eval_jaxpr/ppermute | solution.py:336
  569.5 15.8 %collective-permute-start.4 = (f32[16,40,128]{2,1,0:T(8,128)S(1)}, f32[16,40,128]{2,1,0:T(8,128)S(1)}, u32[]{:S(2)}, u32[]{:S(2)}) collective-permute-start(f32[16,40,128]{2,1,0:T(8,128)S(1)} %get-tuple-element.329), channel_id=1, source_target_pairs={{32,0},{33,1},{34,2},{35,3},{36,4},{37,5},{38,6},{39,7},{40,8},{41... | collective-permute-start | bytes 983048 | tf_op jit(solution)/shard_map/while/body/eval_jaxpr/ppermute | solution.py:450
  585.3 9.5 %collective-permute-start.5 = (f32[16,40,128]{2,1,0:T(8,128)S(1)}, f32[16,40,128]{2,1,0:T(8,128)S(1)}, u32[]{:S(2)}, u32[]{:S(2)}) collective-permute-start(f32[16,40,128]{2,1,0:T(8,128)S(1)} %collective-permute-done.4), channel_id=1, source_target_pairs={{0,1},{1,0},{2,3},{3,2},{4,5},{5,4},{6,7},{7,6},{8,9},{9,8},{10,11... | collective-permute-start | bytes 983048 | tf_op jit(solution)/shard_map/while/body/eval_jaxpr/ppermute | solution.py:453
  604.0 9.4 %collective-permute-start.16 = (f32[160,128]{1,0:T(8,128)S(1)}, f32[160,128]{1,0:T(8,128)S(1)}, u32[]{:S(2)}, u32[]{:S(2)}) collective-permute-start(f32[160,128]{1,0:T(8,128)S(1)} %get-tuple-element.132), channel_id=1, source_target_pairs={{1,2},{2,1},{3,4},{4,3},{5,6},{6,5},{7,8},{8,7},{9,10},{10,9},{11,... | collective-permute-start | bytes 245768 | tf_op jit(solution)/shard_map/ppermute | solution.py:336
  624.7 9.4 %collective-permute-start.18 = (f32[160,128]{1,0:T(8,128)S(1)}, f32[160,128]{1,0:T(8,128)S(1)}, u32[]{:S(2)}, u32[]{:S(2)}) collective-permute-start(f32[160,128]{1,0:T(8,128)S(1)} %get-tuple-element.138), channel_id=1, source_target_pairs={{1,2},{2,1},{3,4},{4,3},{5,6},{6,5},{7,8},{8,7},{9,10},{10,9},{11,... | collective-permute-start | bytes 245768 | tf_op jit(solution)/shard_map/ppermute | solution.py:336
  654.1 17.0 %all-to-all-start = ((f32[8,1,128]{2,1,0:T(1,128)}), f32[8,1,128]{2,1,0:T(1,128)S(1)}, u32[]{:S(2)}, u32[]{:S(2)}) async-start(f32[8,1,128]{2,1,0:T(1,128)} %broadcast_in_dim.106), calls=%async_computation | async-start | bytes 8192 | tf_op jit(solution)/shard_map/all_to_all | solution.py:460
  (50 other events, 411.4 us)

commit v3 on v2

--- a/solution.py
+++ b/solution.py
@@ -4,6 +4,7 @@
 from jax.experimental import pallas as pl
 from jax.experimental.pallas import tpu as pltpu
 from jax.sharding import PartitionSpec as P
+
 
 NB = 128
 COMP = 5
@@ -12,6 +13,9 @@
 LANES = 128
 STEP = 8
 CHUNKS = 4
+WIDE = 8
+MESSAGE = 2 * HALO * COMP
+RIM = COMP + NEI + 1
 ZERO = 2 * NB + 2 * HALO
 ROWS = ZERO + 8
 inverse_step = 6.0
@@ -62,15 +66,14 @@
     lax.fori_loop(0, NB, block, 0)
 
 
-def faces_of(ext, table, half, coef, c, rows=None):
-    b = half * NB + c
-    lead = c if rows is None else rows
+def at_row(ext, row):
+    return ext.reshape(ROWS * 8, LANES)[pl.ds(pl.multiple_of(row, 8), 8)]
+
+
+def total_faces(ext, coef, c, slots):
     total = None
-    for k in range(NEI):
-        slot = table[b * NEI + k]
-        if rows is not None:
-            slot = jnp.where(slot >= 2 * NB, ZERO, slot)
-        term = coef[lead, FACE, k : k + 1] * ext[slot]
+    for k, slot in enumerate(slots):
+        term = coef[c, FACE, k : k + 1] * at_row(ext, slot)
         total = term if total is None else total + term
     return total
 
@@ -91,7 +94,11 @@
         coef = coefs[half]
 
         def gather(g, half=half, coef=coef):
-            return tuple(faces_of(ext, table, half, coef, g * STEP + s) for s in range(STEP))
+            row = half * turns + g
+            return tuple(
+                total_faces(ext, coef, g * STEP + s, [table[row, s * NEI + k] for k in range(NEI)])
+                for s in range(STEP)
+            )
 
         def turn(g, faces, half=half, coef=coef, gather=gather):
             following = gather(jnp.minimum(g + 1, turns - 1))
@@ -121,13 +128,12 @@
             lax.fori_loop(0, CHUNKS, part, gather(0))
 
 
-def send(ext, table, lists, coef, fixed_of, outs):
+def send(ext, lists, coef, fixed_of, outs):
     for half in range(2):
         for i in range(HALO):
             h = half * HALO + i
-            c = lists[h]
-            b = half * NB + c
-            faces = faces_of(ext, table, half, coef, c, rows=h)
+            b = lists[h * WIDE + NEI]
+            faces = total_faces(ext, coef, h, [lists[h * WIDE + k] for k in range(NEI)])
             ahead = finish(ext, b, coef, h, faces, fixed_of(b, h))
             outs[half][COMP * i : COMP * (i + 1)] = ext[b][0:COMP]
             j = HALO + i
@@ -161,21 +167,67 @@
             after[row, 0:COMP] = got[half][COMP * j : COMP * (j + 1)]
 
 
-def first_kernel(table, lists, mine, other, listed, msg0, msg1, ext):
+def first_kernel(lists, mine, other, listed, slots, msg0, msg1, ext):
     unpack(ext, (mine, other))
-    send(ext, table, lists, listed, lambda b, h: listed[h, SRC_LATE] + listed[h, MASS] * ext[b], (msg0, msg1))
-
-
-def pluck_kernel(lists, mine, other, out, sems):
+    msgs = (msg0, msg1)
+    send(ext, lists, listed, lambda b, h: listed[h, SRC_LATE] + listed[h, MASS] * ext[b], msgs)
+    for half in range(2):
+        for i in range(HALO):
+            h = half * HALO + i
+            at = MESSAGE + RIM * i
+            msgs[half][at : at + COMP] = listed[h, PRE, 0:COMP]
+            msgs[half][at + COMP : at + COMP + NEI] = listed[h, FACE, 0:NEI]
+            msgs[half][at + COMP + NEI : at + RIM] = slots[h : h + 1]
+
+
+def rim_kernel(got0, got1, rim, slots):
+    blank = jnp.zeros((8, LANES), F32)
+    for half, got in enumerate((got0, got1)):
+        for i in range(HALO):
+            h = half * HALO + i
+            at = MESSAGE + RIM * i
+            rim[h, 0] = blank
+            rim[h, 1] = blank
+            rim[h, 1, 0:COMP] = got[at : at + COMP]
+            rim[h, 0, 0:NEI] = got[at + COMP : at + COMP + NEI]
+            slots[h : h + 1] = got[at + COMP + NEI : at + RIM]
+
+
+PACKED = (0, 1, 2, 3, 4, PRE, SRC_LATE, MASS)
+
+
+def pluck_kernel(lists, mine, other, out, packed, sems):
     copies = []
     for half, source in enumerate((mine, other)):
         for i in range(HALO):
             h = half * HALO + i
-            copies.append(pltpu.make_async_copy(source.at[lists[h]], out.at[h], sems.at[h]))
+            c = lists[h * WIDE + NEI] - half * NB
+            copies.append(pltpu.make_async_copy(source.at[c], out.at[h], sems.at[h]))
     for copy in copies:
         copy.start()
     for copy in copies:
         copy.wait()
+
+    def block(h, carry):
+        for n, tile in enumerate(PACKED):
+            packed[h, COMP * n : COMP * (n + 1)] = out[h, tile, 0:COMP]
+        return carry
+
+    lax.fori_loop(0, 2 * HALO, block, 0)
+
+
+def spread_kernel(packed, listed, out):
+    blank = jnp.zeros((8, LANES), F32)
+
+    def block(h, carry):
+        for n, tile in enumerate(PACKED):
+            out[h, tile] = blank
+            out[h, tile, 0:COMP] = packed[h, COMP * n : COMP * (n + 1)]
+        out[h, SRC_EARLY] = blank
+        out[h, FACE] = listed[h, FACE]
+        return carry
+
+    lax.fori_loop(0, 2 * HALO, block, 0)
 
 
 def make_step(stage):
@@ -195,9 +247,12 @@
         elif stage == 1:
             x_in, r_in, got0, got1, rim, listed, coef0, coef1 = take(8)
             x_out, r_out, msg0, msg1, lam = take(5)
-        else:
+        elif stage == 2:
             x_in, r_in, got0, got1, rim, listed, coef0, coef1 = take(8)
             msg0, msg1, lam = take(3)
+        else:
+            x_in, r_in, got0, got1, rim, coef0, coef1 = take(7)
+            (lam,) = take(1)
         ext, after = take(2)
         coefs = (coef0, coef1)
         blank = jnp.zeros((8, LANES), F32)
@@ -236,9 +291,9 @@
             lax.fori_loop(0, 2 * NB // STEP, copy, 0)
             receive(ext, after, (got0, got1))
         for h in range(2 * HALO):
-            total = rim[h, 0, 0:1] * ext[fixes[h * NEI]]
+            total = rim[h, 0, 0:1] * at_row(ext, fixes[h * NEI])
             for k in range(1, NEI):
-                total = total + rim[h, 0, k : k + 1] * ext[fixes[h * NEI + k]]
+                total = total + rim[h, 0, k : k + 1] * at_row(ext, fixes[h * NEI + k])
             after[2 * NB + h] = after[2 * NB + h] + rim[h, 1] * total
 
         def keep_lam(g, s, value):
@@ -257,7 +312,7 @@
                 x_out[b] = value
             if stage == 1:
                 r_out[b] = fixed
-            if stage == 2 and half == 0:
+            if stage >= 2 and half == 0:
                 keep_lam(g, s, value)
 
         def late(b, c, coef):
@@ -275,10 +330,11 @@
             ahead = lambda b, h: r_out[b]
         else:
             ahead = lambda b, h: listed[h, SRC_LATE] + listed[h, MASS] * ext[b]
-        send(ext, table, lists, listed, ahead, (msg0, msg1))
+        if stage < 3:
+            send(ext, lists, listed, ahead, (msg0, msg1))
 
     ext = pltpu.VMEM((ROWS, 8, LANES), F32)
-    message = shape(2 * HALO * COMP, LANES)
+    message = shape(MESSAGE, LANES)
     full = shape(2 * NB, 8, LANES)
     lam = shape(NB // STEP, STEP * COMP, LANES)
     scratch = [ext, ext]
@@ -288,8 +344,8 @@
         ins = [SMEM] + [VMEM] * 10 + [ANY] * 2
         scratch.append(pltpu.SemaphoreType.DMA((2, CHUNKS)))
     else:
-        outs = [full, full, message, message, lam] if stage == 1 else [message, message, lam]
-        ins = [VMEM] * 8
+        outs = {1: [full, full, message, message, lam], 2: [message, message, lam], 3: [lam]}[stage]
+        ins = [VMEM] * (8 if stage < 3 else 7)
     return pl.pallas_call(
         kernel,
         out_shape=outs,
@@ -297,7 +353,6 @@
         out_specs=[VMEM] * len(outs),
         scratch_shapes=scratch,
         compiler_params=PARAMS,
-        name=f"step{stage}",
     )
 
 
@@ -372,62 +427,80 @@
             place(near_own, 0, core, 2 * NB, NB, in_other),
             place(near_other, NB, 1 - core, 2 * NB + HALO, 0, in_own),
         ]
-    ).reshape(-1)
-    lists = jnp.concatenate([out_own, out_other])
-
-    listed = pl.pallas_call(
+    )
+    rows = jnp.concatenate([out_own, out_other + NB])
+    hit = rows[:, None] == lax.iota(jnp.int32, 2 * NB)
+    inner = jnp.where(table >= 2 * NB, ZERO, table)
+    slots = jnp.sum(jnp.where(hit[..., None], inner, 0), axis=1)
+    lists = jnp.concatenate([8 * slots, rows[:, None], rows[:, None]], axis=1).reshape(-1)
+    table = jnp.pad(8 * table.reshape(-1, STEP * NEI), ((0, 0), (0, LANES - STEP * NEI)))
+    raw = jnp.concatenate([near_own, near_other]).astype(F32)
+    raw = jnp.sum(jnp.where(hit[..., None], raw, 0.0), axis=1)
+    raw = jnp.pad(raw, ((0, 0), (0, LANES - NEI)))
+
+    listed, packed = pl.pallas_call(
         pluck_kernel,
-        out_shape=shape(2 * HALO, TILES, 8, LANES),
+        out_shape=[shape(2 * HALO, TILES, 8, LANES), shape(2 * HALO, len(PACKED) * COMP, LANES)],
         in_specs=[SMEM] + [ANY] * 2,
-        out_specs=VMEM,
+        out_specs=[VMEM] * 2,
         scratch_shapes=[pltpu.SemaphoreType.DMA((2 * HALO,))],
         compiler_params=PARAMS,
         name="pluck",
     )(lists, mine, other)
-    listed_next = lax.ppermute(listed, "tm", [(t, t + 1) for t in range(rounds - 1)])
-
-    def rim_message(half, slots, chosen):
-        tiles = listed[half * HALO : (half + 1) * HALO, FACE : PRE + 1]
-        hit = chosen[:, None] == lax.iota(jnp.int32, NB)
-        picked = jnp.sum(jnp.where(hit[..., None], slots.astype(F32), 0.0), axis=1)
-        wide = jnp.broadcast_to(
-            jnp.pad(picked, ((0, 0), (0, LANES - NEI)))[:, None, None, :], (HALO, 1, 8, LANES)
-        )
-        return jnp.concatenate([tiles, wide], axis=1)
-
-    rim0, rim1 = exchange(rim_message(0, near_own, out_own), rim_message(1, near_other, out_other))
-    rim = jnp.concatenate([rim0[:, :2], rim1[:, :2]])
+
+    live = (lax.iota(jnp.int32, NB) < live_count[0]).astype(F32)[:, None, None]
+    start = (live * terminal).reshape(NB // STEP, STEP * COMP, LANES)
+    start_other = lax.ppermute(start, "space", swap)
+    message = shape(MESSAGE + HALO * RIM, LANES)
+    sent = pl.pallas_call(
+        first_kernel,
+        out_shape=[message, message],
+        in_specs=[SMEM] + [VMEM] * 4,
+        out_specs=[VMEM] * 2,
+        scratch_shapes=[pltpu.VMEM((ROWS, 8, LANES), F32)],
+        compiler_params=PARAMS,
+        name="first",
+    )(lists, start, start_other, listed, raw)
+    got0, got1 = exchange(*sent)
+    rim, rim_slots = pl.pallas_call(
+        rim_kernel,
+        out_shape=[shape(2 * HALO, 2, 8, LANES), shape(2 * HALO, LANES)],
+        in_specs=[VMEM] * 2,
+        out_specs=[VMEM] * 2,
+        compiler_params=PARAMS,
+        name="rim",
+    )(got0, got1)
+    begun = (start, start_other, got0, got1)
 
     def fix(message, outward, base, sent):
-        slots = message[:, 2, 0, :NEI].astype(jnp.int32)
+        slots = message[:, :NEI].astype(jnp.int32)
         side = (slots - NB) // HALO
         order = (slots - NB) % HALO
         valid = (slots >= NB) & (slots < NB + 2 * HALO) & (side == outward)
         return jnp.where(valid, base + pick(sent, order), ZERO)
 
     fixes = jnp.concatenate(
-        [fix(rim0, 1 - core, 0, out_own), fix(rim1, core, NB, out_other)]
-    ).reshape(-1)
-
-    message = shape(2 * HALO * COMP, LANES)
-    first_call = pl.pallas_call(
-        first_kernel,
-        out_shape=[message, message],
-        in_specs=[SMEM] * 2 + [VMEM] * 3,
-        out_specs=[VMEM] * 2,
-        scratch_shapes=[pltpu.VMEM((ROWS, 8, LANES), F32)],
+        [
+            fix(rim_slots[:HALO], 1 - core, 0, out_own),
+            fix(rim_slots[HALO:], core, NB, out_other),
+        ]
+    ).reshape(-1) * 8
+
+    packed, _ = lax.optimization_barrier((packed, got0))
+    packed_next = lax.ppermute(packed, "tm", [(t, t + 1) for t in range(rounds - 1)])
+    listed_next = pl.pallas_call(
+        spread_kernel,
+        out_shape=shape(2 * HALO, TILES, 8, LANES),
+        in_specs=[VMEM] * 2,
+        out_specs=VMEM,
         compiler_params=PARAMS,
-        name="first",
-    )
-    steps = [make_step(stage) for stage in range(3)]
-
+        name="spread",
+    )(packed_next, listed)
+
+    steps = [make_step(stage) for stage in range(4)]
     flag = (lax.axis_index("tm") == rounds - 1).astype(jnp.int32).reshape(1)
-    live = (lax.iota(jnp.int32, NB) < live_count[0]).astype(F32)[:, None, None]
-    start = (live * terminal).reshape(NB // STEP, STEP * COMP, LANES)
-    start_other = lax.ppermute(start, "space", swap)
-    begun = (start, start_other, *exchange(*first_call(table, lists, start, start_other, listed)))
-
-    def slab(moved):
+
+    def slab(moved, last=False):
         x, fixed, msg0, msg1, coef0, coef1 = steps[0](
             table, lists, fixes, flag, *moved, *begun, rim, listed, mine, other
         )
@@ -436,8 +509,10 @@
             table, lists, fixes, x, fixed, *got, rim, listed, coef0, coef1
         )
         got = exchange(msg0, msg1)
-        *sent, early = steps[2](table, lists, fixes, x, fixed, *got, rim, listed_next, coef0, coef1)
-        return early, late, sent
+        if last:
+            (early,) = steps[3](table, lists, fixes, x, fixed, *got, rim, coef0, coef1)
+            return early, late
+        return steps[2](table, lists, fixes, x, fixed, *got, rim, listed_next, coef0, coef1)
 
     def earlier(pairs):
         return [(t * count + d, (t - 1) * count + e) for t in range(1, rounds) for d, e in pairs]
@@ -446,16 +521,26 @@
     same = [(d, d) for d in range(count)]
 
     def turn(step_index, moved):
-        early, _, (msg0, msg1) = slab(moved)
+        msg0, msg1, early = slab(moved)
         half = lax.ppermute(early, both, earlier(same))
         got0 = lax.ppermute(msg0, both, earlier(near))
         got1 = lax.ppermute(msg1, both, earlier(far))
-        return (half, lax.ppermute(half, "space", swap), got0, got1)
-
-    moved = lax.fori_loop(0, rounds - 1, turn, begun)
-    early, late, _ = slab(moved)
-    fields = jnp.stack([early, late]).reshape(2, NB, COMP, LANES)
-    part = jnp.sum(weights[:, None] * jnp.sum(fields * shape_field[None], axis=(2, 3)), axis=0)
+        shared = lax.ppermute(half, "space", swap)
+        return (half, shared, got0, got1)
+
+    moved = (start, start_other, got0[:MESSAGE], got1[:MESSAGE])
+    moved = turn(0, moved)
+    moved = lax.fori_loop(1, rounds - 1, turn, moved)
+    early, late = slab(moved, last=True)
+
+    def weighed(level, value):
+        value = value.reshape(NB, COMP, LANES)
+        return value, weights[level] * jnp.sum(value * shape_field, axis=(1, 2))
+
+    late, part_late = weighed(1, late)
+    early, part_early = weighed(0, early)
+    fields = jnp.stack([early, late])
+    part = part_late + part_early
     copies = jnp.broadcast_to(part, (rounds, *part.shape))
     sensitivity = lax.all_to_all(copies, "tm", split_axis=0, concat_axis=0, tiled=True).sum(axis=0)
     return fields, sensitivity

time: 676 us -> 647 us (0.957)
  waiting for transfers between devices: 254 us -> 239 us
  starting transfers between devices: 173 us -> 161 us
    ppermute x18 -> x17, waiting for transfers between devices: 64.9 us -> 42.4 us  [exchange(): lax.ppermute(second, 'space', far)]
    pallas_call x8 -> x7, Pallas kernels: 67.4 us -> 54.3 us  [slab(): steps[2]]
    pallas_call x2 -> x5, Pallas kernels: 3.39 us -> 12.5 us  [the longest x1 7.49 us: slab(): early, = steps[3](table, lists, fixes, x, fixed, *got, rim, coef0, coef1)]
    ppermute x18 -> x17, starting transfers between devices: 43.8 us -> 38.1 us  [exchange(): lax.ppermute(second, 'space', far)]
    ppermute x18 -> x17, waiting for transfers between devices: 41.7 us -> 46.3 us  [exchange(): lax.ppermute(first, 'space', near)]
    ppermute x18 -> x17, starting transfers between devices: 77.2 us -> 73 us  [exchange(): lax.ppermute(first, 'space', near)]
  transfers between devices with their start and end apart: 69 -> 67, of which waited for: 49 -> 50; matrix products, arithmetic and copies ran while one was open for 2% -> 1% of each run, Pallas kernels for 1% -> 3%
where the time goes in v3:
time: 647 us; the launch traced here: 643 us
  waiting for transfers between devices  239 us (37%)
  Pallas kernels  218 us (34%)
  starting transfers between devices  161 us (25%)
  local copies, waits for them, and re-layouts  16.4 us (3%)
  other arithmetic  6.5 us (1%)
    ppermute x7, waiting for transfers between devices, turn(): half = lax.ppermute(early, both, earlier(same))  99 us
    pallas_call x8, Pallas kernels, slab(): steps[0]  77.6 us
    ppermute x17, starting transfers between devices, exchange(): lax.ppermute(first, 'space', near)  73 us
    pallas_call x8, Pallas kernels, slab(): steps[1](table, lists, fixes, x, fixed, *got, rim, listed, coef0, coef1)  68.1 us
    pallas_call x7, Pallas kernels, slab(): steps[2]  54.3 us
    ppermute x17, waiting for transfers between devices, exchange(): lax.ppermute(first, 'space', near)  46.3 us
    ppermute x17, waiting for transfers between devices, exchange(): lax.ppermute(second, 'space', far)  42.4 us
    ppermute x7, waiting for transfers between devices, turn(): got0 = lax.ppermute(msg0, both, earlier(near))  41.1 us
  transfers between devices with their start and end apart: 67, of which 50 were waited for; matrix products, arithmetic and copies ran while one was open for 1% of the time, Pallas kernels for 3%

profile of v3, /device:TPU:113, one launch (start us, length us, event | category | flops | bytes accessed | tf_op | source)
XLA Modules:
  0.0 642.8 jit_solution(8538186999359052738)
XLA Ops:
  42.9 9.6 %shard_map.122 = (f32[256,8,128]{2,1,0:T(8,128)S(1)}, f32[256,8,128]{2,1,0:T(8,128)S(1)}, f32[160,128]{1,0:T(8,128)S(1)}, f32[160,128]{1,0:T(8,128)S(1)}, f32[12...) custom-call(s32[32,128]{1,0:T(8,128)} %pad.13.table, s32[256]{0:T(256)S(1)} %reshape.73.lists, ...), custom_call_target="tpu_custom_call" | custom-call | tf_op jit(solution)/shard_map/pallas_call | solution.py:504
  64.4 8.5 %shard_map.123 = (f32[256,8,128]{2,1,0:T(8,128)S(1)}, f32[256,8,128]{2,1,0:T(8,128)S(1)}, f32[160,128]{1,0:T(8,128)S(1)}, f32[160,128]{1,0:T(8,128)S(1)}, f32[16,40,128]{2,1,0:T(8,128)}) custom-call(s32[32,128]{1,0:T(8,128)} %pad.13.table, s32[256]{0:T(256)S(1)} %reshape.73.lists, s32[192]{0:T(256)S(1)} %mul.55.fixes, ...), custom_call_target="tpu_custom_call" | custom-call | tf_op jit(solution)/shard_map/pallas_call | solution.py:508
  85.3 7.8 %shard_map.124 = (f32[160,128]{1,0:T(8,128)S(1)}, f32[160,128]{1,0:T(8,128)S(1)}, f32[16,40,128]{2,1,0:T(8,128)S(1)}) custom-call(s32[32,128]{1,0:T(8,128)} %pad.13.table, s32[256]{0:T(256)S(1)} %reshape.73.lists, s32[192]{0:T(256)S(1)} %mul.55.fixes, f32[256,8,128]{2,1,0:T(8,128)S(1)} %get-tuple-element.152.refs_0_, ...), custom_call_target="tpu_custom_call" | custom-call | tf_op jit(solution)/shard_map/pallas_call | solution.py:515
  94.4 10.2 %collective-permute-done.18 = f32[16,40,128]{2,1,0:T(8,128)} collective-permute-done((f32[16,40,128]{2,1,0:T(8,128)S(1)}, f32[16,40,128]{2,1,0:T(8,128)}, u32[]{:S(2)}, u32[]{:S(2)}) %collective-permute-start.18) | collective-permute-done | bytes 327712 | tf_op jit(solution)/shard_map/ppermute | solution.py:525
  113.8 452.6 %while.16 = (s32[]{:T(128)}, f32[16,40,128]{2,1,0:T(8,128)}, f32[16,40,128]{2,1,0:T(8,128)}, f32[160,128]{1,0:T(8,128)}, f32[160,128]{1,0:T(8,128)}, /*index=5*/...) while((s32[]{:T(128)}, f32[16,40,128]{2,1,0:T(8,128)}, ...), condition=%wide.region_7.8_spmd, body=%wide.region_6.7_spmd.sunk | while | flops 2 | bytes 9830921 | solution.py:533
  113.8 9.6 %eval_jaxpr.3 = (f32[256,8,128]{2,1,0:T(8,128)S(1)}, f32[256,8,128]{2,1,0:T(8,128)S(1)}, f32[160,128]{1,0:T(8,128)S(1)}, f32[160,128]{1,0:T(8,128)S(1)}, f32[128...) custom-call(s32[32,128]{1,0:T(8,128)} %get-tuple-element.417.table, s32[256]{0:T(256)S(1)} %get-tuple-element.418.lists, ...), custom_call_target="tpu_custom_call" | custom-call | tf_op jit(solution)/shard_map/while/body/eval_jaxpr/pallas_call | solution.py:504
  137.4 8.6 %eval_jaxpr.4 = (f32[256,8,128]{2,1,0:T(8,128)S(1)}, f32[256,8,128]{2,1,0:T(8,128)S(1)}, f32[160,128]{1,0:T(8,128)S(1)}, f32[160,128]{1,0:T(8,128)S(1)}, f32[16,40,128]{2,1,0:T(8,128)}) custom-call(s32[32,128]{1,0:T(8,128)} %get-tuple-element.417.table, s32[256]{0:T(256)S(1)} %get-tuple-element.418.lists, s32[192]{0:T(256)S(1)} %get-tuple-element.419.fixes, ...), custom_call_target="tpu_custom_call" | custom-call | tf_op jit(solution)/shard_map/while/body/eval_jaxpr/pallas_call | solution.py:508
  156.6 7.8 %eval_jaxpr.5 = (f32[160,128]{1,0:T(8,128)S(1)}, f32[160,128]{1,0:T(8,128)S(1)}, f32[16,40,128]{2,1,0:T(8,128)S(1)}) custom-call(s32[32,128]{1,0:T(8,128)} %get-tuple-element.417.table, s32[256]{0:T(256)S(1)} %get-tuple-element.418.lists, s32[192]{0:T(256)S(1)} %get-tuple-element.419.fixes, f32[256,8,128]{2,1,0:T(8,128)S(1)} %get-tuple-element.367.refs_0_, ...), custom_call_target="tpu_custom_call" | custom-call | tf_op jit(solution)/shard_map/while/body/eval_jaxpr/pallas_call | solution.py:515
  165.6 15.3 %collective-permute-done.4 = f32[16,40,128]{2,1,0:T(8,128)} collective-permute-done((f32[16,40,128]{2,1,0:T(8,128)S(1)}, f32[16,40,128]{2,1,0:T(8,128)}, u32[]{:S(2)}, u32[]{:S(2)}) %collective-permute-start.4) | collective-permute-done | bytes 327712 | tf_op jit(solution)/shard_map/while/body/eval_jaxpr/ppermute | solution.py:525
  189.8 9.6 %eval_jaxpr.3 = (f32[256,8,128]{2,1,0:T(8,128)S(1)}, f32[256,8,128]{2,1,0:T(8,128)S(1)}, f32[160,128]{1,0:T(8,128)S(1)}, f32[160,128]{1,0:T(8,128)S(1)}, f32[128...) custom-call(s32[32,128]{1,0:T(8,128)} %get-tuple-element.417.table, s32[256]{0:T(256)S(1)} %get-tuple-element.418.lists, ...), custom_call_target="tpu_custom_call" | custom-call | tf_op jit(solution)/shard_map/while/body/eval_jaxpr/pallas_call | solution.py:504
  211.7 8.6 %eval_jaxpr.4 = (f32[256,8,128]{2,1,0:T(8,128)S(1)}, f32[256,8,128]{2,1,0:T(8,128)S(1)}, f32[160,128]{1,0:T(8,128)S(1)}, f32[160,128]{1,0:T(8,128)S(1)}, f32[16,40,128]{2,1,0:T(8,128)}) custom-call(s32[32,128]{1,0:T(8,128)} %get-tuple-element.417.table, s32[256]{0:T(256)S(1)} %get-tuple-element.418.lists, s32[192]{0:T(256)S(1)} %get-tuple-element.419.fixes, ...), custom_call_target="tpu_custom_call" | custom-call | tf_op jit(solution)/shard_map/while/body/eval_jaxpr/pallas_call | solution.py:508
  231.8 7.8 %eval_jaxpr.5 = (f32[160,128]{1,0:T(8,128)S(1)}, f32[160,128]{1,0:T(8,128)S(1)}, f32[16,40,128]{2,1,0:T(8,128)S(1)}) custom-call(s32[32,128]{1,0:T(8,128)} %get-tuple-element.417.table, s32[256]{0:T(256)S(1)} %get-tuple-element.418.lists, s32[192]{0:T(256)S(1)} %get-tuple-element.419.fixes, f32[256,8,128]{2,1,0:T(8,128)S(1)} %get-tuple-element.367.refs_0_, ...), custom_call_target="tpu_custom_call" | custom-call | tf_op jit(solution)/shard_map/while/body/eval_jaxpr/pallas_call | solution.py:515
  240.9 14.8 %collective-permute-done.4 = f32[16,40,128]{2,1,0:T(8,128)} collective-permute-done((f32[16,40,128]{2,1,0:T(8,128)S(1)}, f32[16,40,128]{2,1,0:T(8,128)}, u32[]{:S(2)}, u32[]{:S(2)}) %collective-permute-start.4) | collective-permute-done | bytes 327712 | tf_op jit(solution)/shard_map/while/body/eval_jaxpr/ppermute | solution.py:525
  265.2 9.6 %eval_jaxpr.3 = (f32[256,8,128]{2,1,0:T(8,128)S(1)}, f32[256,8,128]{2,1,0:T(8,128)S(1)}, f32[160,128]{1,0:T(8,128)S(1)}, f32[160,128]{1,0:T(8,128)S(1)}, f32[128...) custom-call(s32[32,128]{1,0:T(8,128)} %get-tuple-element.417.table, s32[256]{0:T(256)S(1)} %get-tuple-element.418.lists, ...), custom_call_target="tpu_custom_call" | custom-call | tf_op jit(solution)/shard_map/while/body/eval_jaxpr/pallas_call | solution.py:504
  287.0 8.6 %eval_jaxpr.4 = (f32[256,8,128]{2,1,0:T(8,128)S(1)}, f32[256,8,128]{2,1,0:T(8,128)S(1)}, f32[160,128]{1,0:T(8,128)S(1)}, f32[160,128]{1,0:T(8,128)S(1)}, f32[16,40,128]{2,1,0:T(8,128)}) custom-call(s32[32,128]{1,0:T(8,128)} %get-tuple-element.417.table, s32[256]{0:T(256)S(1)} %get-tuple-element.418.lists, s32[192]{0:T(256)S(1)} %get-tuple-element.419.fixes, ...), custom_call_target="tpu_custom_call" | custom-call | tf_op jit(solution)/shard_map/while/body/eval_jaxpr/pallas_call | solution.py:508
  307.2 7.8 %eval_jaxpr.5 = (f32[160,128]{1,0:T(8,128)S(1)}, f32[160,128]{1,0:T(8,128)S(1)}, f32[16,40,128]{2,1,0:T(8,128)S(1)}) custom-call(s32[32,128]{1,0:T(8,128)} %get-tuple-element.417.table, s32[256]{0:T(256)S(1)} %get-tuple-element.418.lists, s32[192]{0:T(256)S(1)} %get-tuple-element.419.fixes, f32[256,8,128]{2,1,0:T(8,128)S(1)} %get-tuple-element.367.refs_0_, ...), custom_call_target="tpu_custom_call" | custom-call | tf_op jit(solution)/shard_map/while/body/eval_jaxpr/pallas_call | solution.py:515
  316.3 14.7 %collective-permute-done.4 = f32[16,40,128]{2,1,0:T(8,128)} collective-permute-done((f32[16,40,128]{2,1,0:T(8,128)S(1)}, f32[16,40,128]{2,1,0:T(8,128)}, u32[]{:S(2)}, u32[]{:S(2)}) %collective-permute-start.4) | collective-permute-done | bytes 327712 | tf_op jit(solution)/shard_map/while/body/eval_jaxpr/ppermute | solution.py:525
  340.5 9.6 %eval_jaxpr.3 = (f32[256,8,128]{2,1,0:T(8,128)S(1)}, f32[256,8,128]{2,1,0:T(8,128)S(1)}, f32[160,128]{1,0:T(8,128)S(1)}, f32[160,128]{1,0:T(8,128)S(1)}, f32[128...) custom-call(s32[32,128]{1,0:T(8,128)} %get-tuple-element.417.table, s32[256]{0:T(256)S(1)} %get-tuple-element.418.lists, ...), custom_call_target="tpu_custom_call" | custom-call | tf_op jit(solution)/shard_map/while/body/eval_jaxpr/pallas_call | solution.py:504
  362.4 8.6 %eval_jaxpr.4 = (f32[256,8,128]{2,1,0:T(8,128)S(1)}, f32[256,8,128]{2,1,0:T(8,128)S(1)}, f32[160,128]{1,0:T(8,128)S(1)}, f32[160,128]{1,0:T(8,128)S(1)}, f32[16,40,128]{2,1,0:T(8,128)}) custom-call(s32[32,128]{1,0:T(8,128)} %get-tuple-element.417.table, s32[256]{0:T(256)S(1)} %get-tuple-element.418.lists, s32[192]{0:T(256)S(1)} %get-tuple-element.419.fixes, ...), custom_call_target="tpu_custom_call" | custom-call | tf_op jit(solution)/shard_map/while/body/eval_jaxpr/pallas_call | solution.py:508
  382.5 7.8 %eval_jaxpr.5 = (f32[160,128]{1,0:T(8,128)S(1)}, f32[160,128]{1,0:T(8,128)S(1)}, f32[16,40,128]{2,1,0:T(8,128)S(1)}) custom-call(s32[32,128]{1,0:T(8,128)} %get-tuple-element.417.table, s32[256]{0:T(256)S(1)} %get-tuple-element.418.lists, s32[192]{0:T(256)S(1)} %get-tuple-element.419.fixes, f32[256,8,128]{2,1,0:T(8,128)S(1)} %get-tuple-element.367.refs_0_, ...), custom_call_target="tpu_custom_call" | custom-call | tf_op jit(solution)/shard_map/while/body/eval_jaxpr/pallas_call | solution.py:515
  391.6 14.7 %collective-permute-done.4 = f32[16,40,128]{2,1,0:T(8,128)} collective-permute-done((f32[16,40,128]{2,1,0:T(8,128)S(1)}, f32[16,40,128]{2,1,0:T(8,128)}, u32[]{:S(2)}, u32[]{:S(2)}) %collective-permute-start.4) | collective-permute-done | bytes 327712 | tf_op jit(solution)/shard_map/while/body/eval_jaxpr/ppermute | solution.py:525
  415.8 9.6 %eval_jaxpr.3 = (f32[256,8,128]{2,1,0:T(8,128)S(1)}, f32[256,8,128]{2,1,0:T(8,128)S(1)}, f32[160,128]{1,0:T(8,128)S(1)}, f32[160,128]{1,0:T(8,128)S(1)}, f32[128...) custom-call(s32[32,128]{1,0:T(8,128)} %get-tuple-element.417.table, s32[256]{0:T(256)S(1)} %get-tuple-element.418.lists, ...), custom_call_target="tpu_custom_call" | custom-call | tf_op jit(solution)/shard_map/while/body/eval_jaxpr/pallas_call | solution.py:504
  437.7 8.6 %eval_jaxpr.4 = (f32[256,8,128]{2,1,0:T(8,128)S(1)}, f32[256,8,128]{2,1,0:T(8,128)S(1)}, f32[160,128]{1,0:T(8,128)S(1)}, f32[160,128]{1,0:T(8,128)S(1)}, f32[16,40,128]{2,1,0:T(8,128)}) custom-call(s32[32,128]{1,0:T(8,128)} %get-tuple-element.417.table, s32[256]{0:T(256)S(1)} %get-tuple-element.418.lists, s32[192]{0:T(256)S(1)} %get-tuple-element.419.fixes, ...), custom_call_target="tpu_custom_call" | custom-call | tf_op jit(solution)/shard_map/while/body/eval_jaxpr/pallas_call | solution.py:508
  457.8 7.8 %eval_jaxpr.5 = (f32[160,128]{1,0:T(8,128)S(1)}, f32[160,128]{1,0:T(8,128)S(1)}, f32[16,40,128]{2,1,0:T(8,128)S(1)}) custom-call(s32[32,128]{1,0:T(8,128)} %get-tuple-element.417.table, s32[256]{0:T(256)S(1)} %get-tuple-element.418.lists, s32[192]{0:T(256)S(1)} %get-tuple-element.419.fixes, f32[256,8,128]{2,1,0:T(8,128)S(1)} %get-tuple-element.367.refs_0_, ...), custom_call_target="tpu_custom_call" | custom-call | tf_op jit(solution)/shard_map/while/body/eval_jaxpr/pallas_call | solution.py:515
  466.9 14.7 %collective-permute-done.4 = f32[16,40,128]{2,1,0:T(8,128)} collective-permute-done((f32[16,40,128]{2,1,0:T(8,128)S(1)}, f32[16,40,128]{2,1,0:T(8,128)}, u32[]{:S(2)}, u32[]{:S(2)}) %collective-permute-start.4) | collective-permute-done | bytes 327712 | tf_op jit(solution)/shard_map/while/body/eval_jaxpr/ppermute | solution.py:525
  491.1 9.6 %eval_jaxpr.3 = (f32[256,8,128]{2,1,0:T(8,128)S(1)}, f32[256,8,128]{2,1,0:T(8,128)S(1)}, f32[160,128]{1,0:T(8,128)S(1)}, f32[160,128]{1,0:T(8,128)S(1)}, f32[128...) custom-call(s32[32,128]{1,0:T(8,128)} %get-tuple-element.417.table, s32[256]{0:T(256)S(1)} %get-tuple-element.418.lists, ...), custom_call_target="tpu_custom_call" | custom-call | tf_op jit(solution)/shard_map/while/body/eval_jaxpr/pallas_call | solution.py:504
  513.0 8.6 %eval_jaxpr.4 = (f32[256,8,128]{2,1,0:T(8,128)S(1)}, f32[256,8,128]{2,1,0:T(8,128)S(1)}, f32[160,128]{1,0:T(8,128)S(1)}, f32[160,128]{1,0:T(8,128)S(1)}, f32[16,40,128]{2,1,0:T(8,128)}) custom-call(s32[32,128]{1,0:T(8,128)} %get-tuple-element.417.table, s32[256]{0:T(256)S(1)} %get-tuple-element.418.lists, s32[192]{0:T(256)S(1)} %get-tuple-element.419.fixes, ...), custom_call_target="tpu_custom_call" | custom-call | tf_op jit(solution)/shard_map/while/body/eval_jaxpr/pallas_call | solution.py:508
  533.1 7.8 %eval_jaxpr.5 = (f32[160,128]{1,0:T(8,128)S(1)}, f32[160,128]{1,0:T(8,128)S(1)}, f32[16,40,128]{2,1,0:T(8,128)S(1)}) custom-call(s32[32,128]{1,0:T(8,128)} %get-tuple-element.417.table, s32[256]{0:T(256)S(1)} %get-tuple-element.418.lists, s32[192]{0:T(256)S(1)} %get-tuple-element.419.fixes, f32[256,8,128]{2,1,0:T(8,128)S(1)} %get-tuple-element.367.refs_0_, ...), custom_call_target="tpu_custom_call" | custom-call | tf_op jit(solution)/shard_map/while/body/eval_jaxpr/pallas_call | solution.py:515
  542.2 14.7 %collective-permute-done.4 = f32[16,40,128]{2,1,0:T(8,128)} collective-permute-done((f32[16,40,128]{2,1,0:T(8,128)S(1)}, f32[16,40,128]{2,1,0:T(8,128)}, u32[]{:S(2)}, u32[]{:S(2)}) %collective-permute-start.4) | collective-permute-done | bytes 327712 | tf_op jit(solution)/shard_map/while/body/eval_jaxpr/ppermute | solution.py:525
  567.5 10.2 %shard_map.125 = (f32[256,8,128]{2,1,0:T(8,128)S(1)}, f32[256,8,128]{2,1,0:T(8,128)S(1)}, f32[160,128]{1,0:T(8,128)S(1)}, f32[160,128]{1,0:T(8,128)S(1)}, f32[12...) custom-call(s32[32,128]{1,0:T(8,128)} %pad.13.table, s32[256]{0:T(256)S(1)} %get-tuple-element.471, ...), custom_call_target="tpu_custom_call" | custom-call | tf_op jit(solution)/shard_map/pallas_call | solution.py:504
  589.9 7.9 %shard_map.126 = (f32[256,8,128]{2,1,0:T(8,128)S(1)}, f32[256,8,128]{2,1,0:T(8,128)S(1)}, f32[160,128]{1,0:T(8,128)S(1)}, f32[160,128]{1,0:T(8,128)S(1)}, f32[16,40,128]{2,1,0:T(8,128)S(1)}) custom-call(s32[32,128]{1,0:T(8,128)} %pad.13.table, s32[256]{0:T(256)S(1)} %get-tuple-element.471, s32[192]{0:T(256)S(1)} %get-tuple-element.472, ...), custom_call_target="tpu_custom_call" | custom-call | tf_op jit(solution)/shard_map/pallas_call | solution.py:508
  625.8 11.5 %all-to-all-start = ((f32[8,1,128]{2,1,0:T(1,128)}), f32[8,1,128]{2,1,0:T(1,128)S(1)}, u32[]{:S(2)}, u32[]{:S(2)}) async-start(f32[8,1,128]{2,1,0:T(1,128)} %broadcast_in_dim.103), calls=%async_computation | async-start | bytes 8192 | tf_op jit(solution)/shard_map/all_to_all | solution.py:545
  (232 shorter events, 329.9 us)
Async XLA Ops:
  10.8 10.5 %collective-permute-start.10 = (f32[128,10,8,128]{3,2,1,0:T(8,128)}, f32[128,10,8,128]{3,2,1,0:T(8,128)}, u32[]{:S(2)}, u32[]{:S(2)}) collective-permute-start(f32[128,10,8,128]{3,2,1,0:T(8,128)} %prep.1.mine.refs_11_), channel_id=1, source_target_pairs={{0,1},{1,0},{2,3},{3,2},{4,5},{5,4},{6,7},{7,6},{8,9},{9,8},{10,11... | collective-permute-start | bytes 15728648 | tf_op jit(solution)/shard_map/ppermute | solution.py:401
  12.0 11.5 %collective-permute-start.9 = (f32[16,40,128]{2,1,0:T(8,128)S(1)}, f32[16,40,128]{2,1,0:T(8,128)}, u32[]{:S(2)}, u32[]{:S(2)}) collective-permute-start(f32[16,40,128]{2,1,0:T(8,128)S(1)} %reshape.74.mine.refs_1_.refs_5_), channel_id=1, source_target_pairs={{0,1},{1,0},{2,3},{3,2},{4,5},{5,4},{6,7},{7,6},{8,9},{9,8},{10,11... | collective-permute-start | bytes 983048 | tf_op jit(solution)/shard_map/ppermute | solution.py:453
  25.1 10.4 %collective-permute-start.11 = (f32[352,128]{1,0:T(8,128)S(1)}, f32[352,128]{1,0:T(8,128)S(1)}, u32[]{:S(2)}, u32[]{:S(2)}) collective-permute-start(f32[352,128]{1,0:T(8,128)S(1)} %get-tuple-element.142), channel_id=1, source_target_pairs={{1,2},{2,1},{3,4},{4,3},{5,6},{6,5},{7,8},{8,7},{9,10},{10,9},{11,... | collective-permute-start | bytes 540680 | tf_op jit(solution)/shard_map/ppermute | solution.py:391
  29.9 9.7 %collective-permute-start.12 = (f32[352,128]{1,0:T(8,128)S(1)}, f32[352,128]{1,0:T(8,128)}, u32[]{:S(2)}, u32[]{:S(2)}) collective-permute-start(f32[352,128]{1,0:T(8,128)S(1)} %get-tuple-element.143), channel_id=1, source_target_pairs={{0,3},{2,5},{3,0},{4,7},{5,2},{6,9},{7,4},{8,11},{9,6},{10,13},{11... | collective-permute-start | bytes 540680 | tf_op jit(solution)/shard_map/ppermute | solution.py:391
  35.5 43.8 %collective-permute-start.17 = (f32[32,40,128]{2,1,0:T(8,128)S(1)}, f32[32,40,128]{2,1,0:T(8,128)S(1)}, u32[]{:S(2)}, u32[]{:S(2)}) collective-permute-start(f32[32,40,128]{2,1,0:T(8,128)S(1)} %get-tuple-element.157), channel_id=1, source_target_pairs={{0,32},{32,64},{64,96},{96,128},{128,160},{160,192},{192,224},{1,3... | collective-permute-start | bytes 1966088 | tf_op jit(solution)/shard_map/ppermute | solution.py:490
  52.5 9.4 %collective-permute-start.13 = (f32[160,128]{1,0:T(8,128)S(1)}, f32[160,128]{1,0:T(8,128)S(1)}, u32[]{:S(2)}, u32[]{:S(2)}) collective-permute-start(f32[160,128]{1,0:T(8,128)S(1)} %get-tuple-element.148), channel_id=1, source_target_pairs={{1,2},{2,1},{3,4},{4,3},{5,6},{6,5},{7,8},{8,7},{9,10},{10,9},{11,... | collective-permute-start | bytes 245768 | tf_op jit(solution)/shard_map/ppermute | solution.py:391
  72.9 9.4 %collective-permute-start.15 = (f32[160,128]{1,0:T(8,128)S(1)}, f32[160,128]{1,0:T(8,128)S(1)}, u32[]{:S(2)}, u32[]{:S(2)}) collective-permute-start(f32[160,128]{1,0:T(8,128)S(1)} %get-tuple-element.154), channel_id=1, source_target_pairs={{1,2},{2,1},{3,4},{4,3},{5,6},{6,5},{7,8},{8,7},{9,10},{10,9},{11,... | collective-permute-start | bytes 245768 | tf_op jit(solution)/shard_map/ppermute | solution.py:391
  93.1 11.5 %collective-permute-start.18 = (f32[16,40,128]{2,1,0:T(8,128)S(1)}, f32[16,40,128]{2,1,0:T(8,128)}, u32[]{:S(2)}, u32[]{:S(2)}) collective-permute-start(f32[16,40,128]{2,1,0:T(8,128)S(1)} %get-tuple-element.158), channel_id=1, source_target_pairs={{32,0},{33,1},{34,2},{35,3},{36,4},{37,5},{38,6},{39,7},{40,8},{41... | collective-permute-start | bytes 983048 | tf_op jit(solution)/shard_map/ppermute | solution.py:525
  123.5 9.4 %collective-permute-start = (f32[160,128]{1,0:T(8,128)S(1)}, f32[160,128]{1,0:T(8,128)S(1)}, u32[]{:S(2)}, u32[]{:S(2)}) collective-permute-start(f32[160,128]{1,0:T(8,128)S(1)} %get-tuple-element.363), channel_id=1, source_target_pairs={{1,2},{2,1},{3,4},{4,3},{5,6},{6,5},{7,8},{8,7},{9,10},{10,9},{11,... | collective-permute-start | bytes 245768 | tf_op jit(solution)/shard_map/while/body/eval_jaxpr/ppermute | solution.py:391
  146.0 9.4 %collective-permute-start.2 = (f32[160,128]{1,0:T(8,128)S(1)}, f32[160,128]{1,0:T(8,128)S(1)}, u32[]{:S(2)}, u32[]{:S(2)}) collective-permute-start(f32[160,128]{1,0:T(8,128)S(1)} %get-tuple-element.369), channel_id=1, source_target_pairs={{1,2},{2,1},{3,4},{4,3},{5,6},{6,5},{7,8},{8,7},{9,10},{10,9},{11,... | collective-permute-start | bytes 245768 | tf_op jit(solution)/shard_map/while/body/eval_jaxpr/ppermute | solution.py:391
  164.3 16.6 %collective-permute-start.4 = (f32[16,40,128]{2,1,0:T(8,128)S(1)}, f32[16,40,128]{2,1,0:T(8,128)}, u32[]{:S(2)}, u32[]{:S(2)}) collective-permute-start(f32[16,40,128]{2,1,0:T(8,128)S(1)} %get-tuple-element.371), channel_id=1, source_target_pairs={{32,0},{33,1},{34,2},{35,3},{36,4},{37,5},{38,6},{39,7},{40,8},{41... | collective-permute-start | bytes 983048 | tf_op jit(solution)/shard_map/while/body/eval_jaxpr/ppermute | solution.py:525
  199.5 9.4 %collective-permute-start = (f32[160,128]{1,0:T(8,128)S(1)}, f32[160,128]{1,0:T(8,128)S(1)}, u32[]{:S(2)}, u32[]{:S(2)}) collective-permute-start(f32[160,128]{1,0:T(8,128)S(1)} %get-tuple-element.363), channel_id=1, source_target_pairs={{1,2},{2,1},{3,4},{4,3},{5,6},{6,5},{7,8},{8,7},{9,10},{10,9},{11,... | collective-permute-start | bytes 245768 | tf_op jit(solution)/shard_map/while/body/eval_jaxpr/ppermute | solution.py:391
  220.4 9.4 %collective-permute-start.2 = (f32[160,128]{1,0:T(8,128)S(1)}, f32[160,128]{1,0:T(8,128)S(1)}, u32[]{:S(2)}, u32[]{:S(2)}) collective-permute-start(f32[160,128]{1,0:T(8,128)S(1)} %get-tuple-element.369), channel_id=1, source_target_pairs={{1,2},{2,1},{3,4},{4,3},{5,6},{6,5},{7,8},{8,7},{9,10},{10,9},{11,... | collective-permute-start | bytes 245768 | tf_op jit(solution)/shard_map/while/body/eval_jaxpr/ppermute | solution.py:391
  239.6 16.1 %collective-permute-start.4 = (f32[16,40,128]{2,1,0:T(8,128)S(1)}, f32[16,40,128]{2,1,0:T(8,128)}, u32[]{:S(2)}, u32[]{:S(2)}) collective-permute-start(f32[16,40,128]{2,1,0:T(8,128)S(1)} %get-tuple-element.371), channel_id=1, source_target_pairs={{32,0},{33,1},{34,2},{35,3},{36,4},{37,5},{38,6},{39,7},{40,8},{41... | collective-permute-start | bytes 983048 | tf_op jit(solution)/shard_map/while/body/eval_jaxpr/ppermute | solution.py:525
  255.6 9.6 %collective-permute-start.5 = (f32[16,40,128]{2,1,0:T(8,128)}, f32[16,40,128]{2,1,0:T(8,128)}, u32[]{:S(2)}, u32[]{:S(2)}) collective-permute-start(f32[16,40,128]{2,1,0:T(8,128)} %collective-permute-done.4), channel_id=1, source_target_pairs={{0,1},{1,0},{2,3},{3,2},{4,5},{5,4},{6,7},{7,6},{8,9},{9,8},{10,11... | collective-permute-start | bytes 983048 | tf_op jit(solution)/shard_map/while/body/eval_jaxpr/ppermute | solution.py:528
  274.9 9.4 %collective-permute-start = (f32[160,128]{1,0:T(8,128)S(1)}, f32[160,128]{1,0:T(8,128)S(1)}, u32[]{:S(2)}, u32[]{:S(2)}) collective-permute-start(f32[160,128]{1,0:T(8,128)S(1)} %get-tuple-element.363), channel_id=1, source_target_pairs={{1,2},{2,1},{3,4},{4,3},{5,6},{6,5},{7,8},{8,7},{9,10},{10,9},{11,... | collective-permute-start | bytes 245768 | tf_op jit(solution)/shard_map/while/body/eval_jaxpr/ppermute | solution.py:391
  295.7 9.4 %collective-permute-start.2 = (f32[160,128]{1,0:T(8,128)S(1)}, f32[160,128]{1,0:T(8,128)S(1)}, u32[]{:S(2)}, u32[]{:S(2)}) collective-permute-start(f32[160,128]{1,0:T(8,128)S(1)} %get-tuple-element.369), channel_id=1, source_target_pairs={{1,2},{2,1},{3,4},{4,3},{5,6},{6,5},{7,8},{8,7},{9,10},{10,9},{11,... | collective-permute-start | bytes 245768 | tf_op jit(solution)/shard_map/while/body/eval_jaxpr/ppermute | solution.py:391
  315.0 16.0 %collective-permute-start.4 = (f32[16,40,128]{2,1,0:T(8,128)S(1)}, f32[16,40,128]{2,1,0:T(8,128)}, u32[]{:S(2)}, u32[]{:S(2)}) collective-permute-start(f32[16,40,128]{2,1,0:T(8,128)S(1)} %get-tuple-element.371), channel_id=1, source_target_pairs={{32,0},{33,1},{34,2},{35,3},{36,4},{37,5},{38,6},{39,7},{40,8},{41... | collective-permute-start | bytes 983048 | tf_op jit(solution)/shard_map/while/body/eval_jaxpr/ppermute | solution.py:525
  330.9 9.6 %collective-permute-start.5 = (f32[16,40,128]{2,1,0:T(8,128)}, f32[16,40,128]{2,1,0:T(8,128)}, u32[]{:S(2)}, u32[]{:S(2)}) collective-permute-start(f32[16,40,128]{2,1,0:T(8,128)} %collective-permute-done.4), channel_id=1, source_target_pairs={{0,1},{1,0},{2,3},{3,2},{4,5},{5,4},{6,7},{7,6},{8,9},{9,8},{10,11... | collective-permute-start | bytes 983048 | tf_op jit(solution)/shard_map/while/body/eval_jaxpr/ppermute | solution.py:528
  350.2 9.4 %collective-permute-start = (f32[160,128]{1,0:T(8,128)S(1)}, f32[160,128]{1,0:T(8,128)S(1)}, u32[]{:S(2)}, u32[]{:S(2)}) collective-permute-start(f32[160,128]{1,0:T(8,128)S(1)} %get-tuple-element.363), channel_id=1, source_target_pairs={{1,2},{2,1},{3,4},{4,3},{5,6},{6,5},{7,8},{8,7},{9,10},{10,9},{11,... | collective-permute-start | bytes 245768 | tf_op jit(solution)/shard_map/while/body/eval_jaxpr/ppermute | solution.py:391
  371.0 9.4 %collective-permute-start.2 = (f32[160,128]{1,0:T(8,128)S(1)}, f32[160,128]{1,0:T(8,128)S(1)}, u32[]{:S(2)}, u32[]{:S(2)}) collective-permute-start(f32[160,128]{1,0:T(8,128)S(1)} %get-tuple-element.369), channel_id=1, source_target_pairs={{1,2},{2,1},{3,4},{4,3},{5,6},{6,5},{7,8},{8,7},{9,10},{10,9},{11,... | collective-permute-start | bytes 245768 | tf_op jit(solution)/shard_map/while/body/eval_jaxpr/ppermute | solution.py:391
  390.3 16.0 %collective-permute-start.4 = (f32[16,40,128]{2,1,0:T(8,128)S(1)}, f32[16,40,128]{2,1,0:T(8,128)}, u32[]{:S(2)}, u32[]{:S(2)}) collective-permute-start(f32[16,40,128]{2,1,0:T(8,128)S(1)} %get-tuple-element.371), channel_id=1, source_target_pairs={{32,0},{33,1},{34,2},{35,3},{36,4},{37,5},{38,6},{39,7},{40,8},{41... | collective-permute-start | bytes 983048 | tf_op jit(solution)/shard_map/while/body/eval_jaxpr/ppermute | solution.py:525
  406.3 9.6 %collective-permute-start.5 = (f32[16,40,128]{2,1,0:T(8,128)}, f32[16,40,128]{2,1,0:T(8,128)}, u32[]{:S(2)}, u32[]{:S(2)}) collective-permute-start(f32[16,40,128]{2,1,0:T(8,128)} %collective-permute-done.4), channel_id=1, source_target_pairs={{0,1},{1,0},{2,3},{3,2},{4,5},{5,4},{6,7},{7,6},{8,9},{9,8},{10,11... | collective-permute-start | bytes 983048 | tf_op jit(solution)/shard_map/while/body/eval_jaxpr/ppermute | solution.py:528
  425.5 9.4 %collective-permute-start = (f32[160,128]{1,0:T(8,128)S(1)}, f32[160,128]{1,0:T(8,128)S(1)}, u32[]{:S(2)}, u32[]{:S(2)}) collective-permute-start(f32[160,128]{1,0:T(8,128)S(1)} %get-tuple-element.363), channel_id=1, source_target_pairs={{1,2},{2,1},{3,4},{4,3},{5,6},{6,5},{7,8},{8,7},{9,10},{10,9},{11,... | collective-permute-start | bytes 245768 | tf_op jit(solution)/shard_map/while/body/eval_jaxpr/ppermute | solution.py:391
  465.6 16.0 %collective-permute-start.4 = (f32[16,40,128]{2,1,0:T(8,128)S(1)}, f32[16,40,128]{2,1,0:T(8,128)}, u32[]{:S(2)}, u32[]{:S(2)}) collective-permute-start(f32[16,40,128]{2,1,0:T(8,128)S(1)} %get-tuple-element.371), channel_id=1, source_target_pairs={{32,0},{33,1},{34,2},{35,3},{36,4},{37,5},{38,6},{39,7},{40,8},{41... | collective-permute-start | bytes 983048 | tf_op jit(solution)/shard_map/while/body/eval_jaxpr/ppermute | solution.py:525
  481.6 9.6 %collective-permute-start.5 = (f32[16,40,128]{2,1,0:T(8,128)}, f32[16,40,128]{2,1,0:T(8,128)}, u32[]{:S(2)}, u32[]{:S(2)}) collective-permute-start(f32[16,40,128]{2,1,0:T(8,128)} %collective-permute-done.4), channel_id=1, source_target_pairs={{0,1},{1,0},{2,3},{3,2},{4,5},{5,4},{6,7},{7,6},{8,9},{9,8},{10,11... | collective-permute-start | bytes 983048 | tf_op jit(solution)/shard_map/while/body/eval_jaxpr/ppermute | solution.py:528
  500.8 9.4 %collective-permute-start = (f32[160,128]{1,0:T(8,128)S(1)}, f32[160,128]{1,0:T(8,128)S(1)}, u32[]{:S(2)}, u32[]{:S(2)}) collective-permute-start(f32[160,128]{1,0:T(8,128)S(1)} %get-tuple-element.363), channel_id=1, source_target_pairs={{1,2},{2,1},{3,4},{4,3},{5,6},{6,5},{7,8},{8,7},{9,10},{10,9},{11,... | collective-permute-start | bytes 245768 | tf_op jit(solution)/shard_map/while/body/eval_jaxpr/ppermute | solution.py:391
  540.9 16.0 %collective-permute-start.4 = (f32[16,40,128]{2,1,0:T(8,128)S(1)}, f32[16,40,128]{2,1,0:T(8,128)}, u32[]{:S(2)}, u32[]{:S(2)}) collective-permute-start(f32[16,40,128]{2,1,0:T(8,128)S(1)} %get-tuple-element.371), channel_id=1, source_target_pairs={{32,0},{33,1},{34,2},{35,3},{36,4},{37,5},{38,6},{39,7},{40,8},{41... | collective-permute-start | bytes 983048 | tf_op jit(solution)/shard_map/while/body/eval_jaxpr/ppermute | solution.py:525
  556.9 9.6 %collective-permute-start.5 = (f32[16,40,128]{2,1,0:T(8,128)}, f32[16,40,128]{2,1,0:T(8,128)}, u32[]{:S(2)}, u32[]{:S(2)}) collective-permute-start(f32[16,40,128]{2,1,0:T(8,128)} %collective-permute-done.4), channel_id=1, source_target_pairs={{0,1},{1,0},{2,3},{3,2},{4,5},{5,4},{6,7},{7,6},{8,9},{9,8},{10,11... | collective-permute-start | bytes 983048 | tf_op jit(solution)/shard_map/while/body/eval_jaxpr/ppermute | solution.py:528
  577.7 9.4 %collective-permute-start.22 = (f32[160,128]{1,0:T(8,128)S(1)}, f32[160,128]{1,0:T(8,128)S(1)}, u32[]{:S(2)}, u32[]{:S(2)}) collective-permute-start(f32[160,128]{1,0:T(8,128)S(1)} %get-tuple-element.167), channel_id=1, source_target_pairs={{1,2},{2,1},{3,4},{4,3},{5,6},{6,5},{7,8},{8,7},{9,10},{10,9},{11,... | collective-permute-start | bytes 245768 | tf_op jit(solution)/shard_map/ppermute | solution.py:391
  597.8 9.4 %collective-permute-start.24 = (f32[160,128]{1,0:T(8,128)S(1)}, f32[160,128]{1,0:T(8,128)S(1)}, u32[]{:S(2)}, u32[]{:S(2)}) collective-permute-start(f32[160,128]{1,0:T(8,128)S(1)} %get-tuple-element.173), channel_id=1, source_target_pairs={{1,2},{2,1},{3,4},{4,3},{5,6},{6,5},{7,8},{8,7},{9,10},{10,9},{11,... | collective-permute-start | bytes 245768 | tf_op jit(solution)/shard_map/ppermute | solution.py:391
  625.8 16.5 %all-to-all-start = ((f32[8,1,128]{2,1,0:T(1,128)}), f32[8,1,128]{2,1,0:T(1,128)S(1)}, u32[]{:S(2)}, u32[]{:S(2)}) async-start(f32[8,1,128]{2,1,0:T(1,128)} %broadcast_in_dim.103), calls=%async_computation | async-start | bytes 8192 | tf_op jit(solution)/shard_map/all_to_all | solution.py:545
  (55 other events, 528.0 us)

commit v4 on v3

--- a/solution.py
+++ b/solution.py
@@ -12,6 +12,7 @@
 HALO = 16
 LANES = 128
 STEP = 8
+UNROLL = 2
 CHUNKS = 4
 WIDE = 8
 MESSAGE = 2 * HALO * COMP
@@ -20,6 +21,8 @@
 ROWS = ZERO + 8
 inverse_step = 6.0
 
+GROUPS = NB // STEP
+G_PRE, G_LATE, G_EARLY, G_MASS, G_LEFT, G_RIGHT, G_FACE, G_LISTED = 25, 30, 35, 40, 45, 46, 47, 55
 FACE, PRE, SRC_LATE, SRC_EARLY, MASS, TILES = 5, 6, 7, 8, 9, 10
 
 VMEM = pl.BlockSpec(memory_space=pltpu.VMEM)
@@ -33,13 +36,15 @@
     return jax.ShapeDtypeStruct(dims, F32)
 
 
-def prep_kernel(live_ref, jac, source, face, cell, volume, out):
+def prep_kernel(live_ref, chosen, jac, source, face, cell, volume, out):
     count = live_ref[0]
     lane = lax.broadcasted_iota(jnp.int32, (1, LANES), 1)
     row = lax.broadcasted_iota(jnp.int32, (COMP, LANES), 0)
     blank = jnp.zeros((8, LANES), F32)
-
-    def block(b, carry):
+    width = G_LISTED + TILES
+    flat = out.reshape(GROUPS * width * 8, LANES)
+
+    def terms(b):
         mass = inverse_step * volume[pl.ds(b, 1), :]
         along = cell[pl.ds(b, 1), :]
         faces = face[b]
@@ -49,21 +54,36 @@
             diagonal = jnp.where(row == i, jac[b, i], diagonal)
         live = jnp.where(b < count, 1.0, 0.0).astype(F32)
         pre = live * (1.0 / (mass + diagonal + total + 2.0 * along))
-        for i in range(TILES):
-            out[b, i] = blank
+        own = []
         for i in range(COMP):
             keep = live - pre * (mass + jac[b, i])
-            out[b, i, 0:COMP] = jnp.where(row == i, keep, -pre * jac[b, i])
-        out[b, FACE, 0:NEI] = faces
-        out[b, FACE, NEI : NEI + 1] = jnp.where(lane == 0, 0.0, along)
-        out[b, FACE, NEI + 1 : NEI + 2] = jnp.where(lane == LANES - 1, 0.0, along)
-        out[b, PRE, 0:COMP] = pre
-        out[b, SRC_LATE, 0:COMP] = pre * source[1, b]
-        out[b, SRC_EARLY, 0:COMP] = pre * source[0, b]
-        out[b, MASS, 0:COMP] = pre * mass
+            own.append(jnp.where(row == i, keep, -pre * jac[b, i]))
+        left = jnp.where(lane == 0, 0.0, along)
+        right = jnp.where(lane == LANES - 1, 0.0, along)
+        return own, faces, left, right, pre, pre * source[1, b], pre * source[0, b], pre * mass
+
+    def group(g, carry):
+        for s in range(STEP):
+            own, faces, left, right, *rest = terms(g * STEP + s)
+            base = g * (width * 8) + s
+            for n, value in enumerate(own + rest):
+                flat[pl.ds(base + n * (COMP * 8), COMP, stride=8)] = value
+            out[g, G_LEFT, s : s + 1] = left
+            out[g, G_RIGHT, s : s + 1] = right
+            out[g, G_FACE + s, 0:NEI] = faces
+        own, faces, left, right, *rest = terms(chosen[g])
+        for n in range(TILES):
+            out[g, G_LISTED + n] = blank
+        for n, value in enumerate(own):
+            out[g, G_LISTED + n, 0:COMP] = value
+        out[g, G_LISTED + FACE, 0:NEI] = faces
+        out[g, G_LISTED + FACE, NEI : NEI + 1] = left
+        out[g, G_LISTED + FACE, NEI + 1 : NEI + 2] = right
+        for n, value in enumerate(rest):
+            out[g, G_LISTED + PRE + n, 0:COMP] = value
         return carry
 
-    lax.fori_loop(0, NB, block, 0)
+    lax.fori_loop(0, GROUPS, group, 0)
 
 
 def at_row(ext, row):
@@ -88,44 +108,66 @@
     return value
 
 
-def iterate(ext, table, coefs, fixed_of, put, wait=None):
-    turns = NB // STEP
+def rows_of(ref, start):
+    return ref.reshape(ref.shape[0] * 8, LANES).at[pl.ds(start, STEP, stride=8)]
+
+
+def iterate(ext, table, coefs, sums, fixed_of, put, wait=None):
     for half in range(2):
         coef = coefs[half]
 
         def gather(g, half=half, coef=coef):
-            row = half * turns + g
-            return tuple(
-                total_faces(ext, coef, g * STEP + s, [table[row, s * NEI + k] for k in range(NEI)])
-                for s in range(STEP)
-            )
-
-        def turn(g, faces, half=half, coef=coef, gather=gather):
-            following = gather(jnp.minimum(g + 1, turns - 1))
+            row = (half * GROUPS + g) * (STEP * NEI)
+            for s in range(STEP):
+                terms = []
+                for k in range(NEI):
+                    picked = at_row(ext, table.at[pl.ds(s * NEI + k, 2 * NB * NEI - STEP * NEI + 1)][row])
+                    terms.append(coef[g, G_FACE + s, k : k + 1] * picked)
+                total = ((terms[0] + terms[1]) + (terms[2] + terms[3])) + (terms[4] + terms[5])
+                sums[(half * GROUPS + g) * STEP + s] = total
+
+        def turn(t, carry, half=half, coef=coef, gather=gather):
             done = []
-            for s in range(STEP):
-                c = g * STEP + s
-                b = half * NB + c
-                fixed = fixed_of(b, c, coef)
-                done.append((b, s, finish(ext, b, coef, c, faces[s], fixed), fixed))
-            for b, s, value, fixed in done:
-                put(b, g, s, half, value, fixed)
-            return following
-
+            for u in range(UNROLL):
+                g = t * UNROLL + u
+                start = (half * GROUPS + g) * (STEP * 8)
+                x = [rows_of(ext, start + j)[...] for j in range(COMP)]
+                left, right = coef[g, G_LEFT], coef[g, G_RIGHT]
+                for j in range(COMP):
+                    faces = rows_of(sums, start + j)[...]
+                    beside = left * pltpu.roll(x[j], 1, 1) + right * pltpu.roll(x[j], LANES - 1, 1)
+                    own = [coef[g, i * COMP + j] * x[i] for i in range(COMP)]
+                    fixed = fixed_of(start + j, g, j, coef, x[j])
+                    value = (fixed + own[0]) + (own[1] + own[2]) + (own[3] + own[4])
+                    value = value + coef[g, G_PRE + j] * (faces + beside)
+                    done.append((start + j, g, j, value, fixed))
+            for u in range(UNROLL):
+                gather(jnp.minimum((t + 1) * UNROLL + u, GROUPS - 1))
+            for start, g, j, value, fixed in done:
+                put(start, g, j, half, value, fixed)
+            return carry
+
+        def prologue(gather=gather):
+            for u in range(UNROLL):
+                gather(u)
+
+        turns = GROUPS // UNROLL
         if wait is None:
-            lax.fori_loop(0, turns, turn, gather(0))
+            prologue()
+            lax.fori_loop(0, turns, turn, 0)
         else:
             wait(half, 0)
+            prologue()
             each = turns // CHUNKS
 
-            def part(n, faces, half=half, turn=turn):
+            def part(n, carry, half=half, turn=turn):
                 @pl.when(n + 1 < CHUNKS)
                 def _():
                     wait(half, n + 1)
 
-                return lax.fori_loop(n * each, (n + 1) * each, turn, faces)
-
-            lax.fori_loop(0, CHUNKS, part, gather(0))
+                return lax.fori_loop(n * each, (n + 1) * each, turn, carry)
+
+            lax.fori_loop(0, CHUNKS, part, 0)
 
 
 def send(ext, lists, coef, fixed_of, outs):
@@ -196,13 +238,11 @@
 PACKED = (0, 1, 2, 3, 4, PRE, SRC_LATE, MASS)
 
 
-def pluck_kernel(lists, mine, other, out, packed, sems):
+def pluck_kernel(mine, other, out, packed, sems):
     copies = []
     for half, source in enumerate((mine, other)):
-        for i in range(HALO):
-            h = half * HALO + i
-            c = lists[h * WIDE + NEI] - half * NB
-            copies.append(pltpu.make_async_copy(source.at[c], out.at[h], sems.at[h]))
+        tiles = source.at[pl.ds(0, HALO), pl.ds(G_LISTED, TILES)]
+        copies.append(pltpu.make_async_copy(tiles, out.at[pl.ds(half * HALO, HALO)], sems.at[half]))
     for copy in copies:
         copy.start()
     for copy in copies:
@@ -253,7 +293,7 @@
         else:
             x_in, r_in, got0, got1, rim, coef0, coef1 = take(7)
             (lam,) = take(1)
-        ext, after = take(2)
+        ext, after, sums = take(3)
         coefs = (coef0, coef1)
         blank = jnp.zeros((8, LANES), F32)
         after[ZERO] = blank
@@ -262,9 +302,9 @@
             (sems,) = take(1)
 
             def part(half, n):
-                rows = pl.ds(n * (NB // CHUNKS), NB // CHUNKS)
-                source = (hbm0, hbm1)[half]
-                return pltpu.make_async_copy(source.at[rows], coefs[half].at[rows], sems.at[half, n])
+                rows = pl.ds(n * (GROUPS // CHUNKS), GROUPS // CHUNKS)
+                source = (hbm0, hbm1)[half].at[rows, pl.ds(0, G_LISTED)]
+                return pltpu.make_async_copy(source, coefs[half].at[rows], sems.at[half, n])
 
             for half in range(2):
                 for n in range(CHUNKS):
@@ -296,36 +336,37 @@
                 total = total + rim[h, 0, k : k + 1] * at_row(ext, fixes[h * NEI + k])
             after[2 * NB + h] = after[2 * NB + h] + rim[h, 1] * total
 
-        def keep_lam(g, s, value):
-            lam[g, COMP * s : COMP * (s + 1)] = value[0:COMP]
-
-        def put_a(b, g, s, half, value, fixed):
-            after[b] = value
+        def keep_lam(g, j, value):
+            lam[g, pl.ds(j, STEP, stride=COMP)] = value
+
+        def put_a(start, g, j, half, value, fixed):
+            rows_of(after, start)[...] = value
             if stage == 0:
-                r_out[b] = fixed
+                rows_of(r_out, start)[...] = fixed
             if stage == 1 and half == 0:
-                keep_lam(g, s, value)
-
-        def put_b(b, g, s, half, value, fixed):
-            ext[b] = value
+                keep_lam(g, j, value)
+
+        def put_b(start, g, j, half, value, fixed):
+            if stage < 3:
+                rows_of(ext, start)[...] = value
             if stage < 2:
-                x_out[b] = value
+                rows_of(x_out, start)[...] = value
             if stage == 1:
-                r_out[b] = fixed
+                rows_of(r_out, start)[...] = fixed
             if stage >= 2 and half == 0:
-                keep_lam(g, s, value)
-
-        def late(b, c, coef):
-            return coef[c, SRC_LATE] + coef[c, MASS] * ext[b]
-
-        def early(b, c, coef):
-            return coef[c, SRC_EARLY] + coef[c, MASS] * after[b]
-
-        def held(b, c, coef):
-            return r_out[b] if stage == 0 else r_in[b]
-
-        iterate(ext, table, coefs, held if stage else late, put_a, wait)
-        iterate(after, table, coefs, early if stage == 1 else held, put_b)
+                keep_lam(g, j, value)
+
+        def late(start, g, j, coef, x):
+            return coef[g, G_LATE + j] + coef[g, G_MASS + j] * x
+
+        def early(start, g, j, coef, x):
+            return coef[g, G_EARLY + j] + coef[g, G_MASS + j] * x
+
+        def held(start, g, j, coef, x):
+            return rows_of(r_out if stage == 0 else r_in, start)[...]
+
+        iterate(ext, table, coefs, sums, held if stage else late, put_a, wait)
+        iterate(after, table, coefs, sums, early if stage == 1 else held, put_b)
         if stage < 2:
             ahead = lambda b, h: r_out[b]
         else:
@@ -337,9 +378,9 @@
     message = shape(MESSAGE, LANES)
     full = shape(2 * NB, 8, LANES)
     lam = shape(NB // STEP, STEP * COMP, LANES)
-    scratch = [ext, ext]
+    scratch = [ext, ext, pltpu.VMEM((2 * NB, 8, LANES), F32)]
     if stage == 0:
-        coef = shape(NB, TILES, 8, LANES)
+        coef = shape(GROUPS, G_LISTED, 8, LANES)
         outs = [full, full, message, message, coef, coef]
         ins = [SMEM] + [VMEM] * 10 + [ANY] * 2
         scratch.append(pltpu.SemaphoreType.DMA((2, CHUNKS)))
@@ -390,14 +431,17 @@
     def exchange(first, second):
         return lax.ppermute(first, "space", near), lax.ppermute(second, "space", far)
 
+    core_low = core == 0
+    out_own = jnp.where(core_low, send_blocks[0, 0], send_blocks[0, 1])
+
     mine = pl.pallas_call(
         prep_kernel,
-        out_shape=shape(NB, TILES, 8, LANES),
-        in_specs=[SMEM] + [VMEM] * 5,
+        out_shape=shape(GROUPS, G_LISTED + TILES, 8, LANES),
+        in_specs=[SMEM] * 2 + [VMEM] * 5,
         out_specs=VMEM,
         compiler_params=PARAMS,
         name="prep",
-    )(live_count, jacobian[0], source, face_coef, cell_coef, volume)
+    )(live_count, out_own, jacobian[0], source, face_coef, cell_coef, volume)
     other = lax.ppermute(mine, "space", swap)
 
     lists_own = jnp.pad(send_blocks[0].reshape(2 * HALO, 1), ((0, NB - 2 * HALO), (0, 0)))
@@ -408,11 +452,9 @@
     sends_other = ints_other[: 2 * HALO, NEI].reshape(2, HALO)
     low_own, high_own = send_blocks[0, 0], send_blocks[0, 1]
     low_other, high_other = sends_other[0], sends_other[1]
-    is_low = core == 0
-    out_own = jnp.where(is_low, low_own, high_own)
-    in_own = jnp.where(is_low, high_own, low_own)
-    out_other = jnp.where(is_low, high_other, low_other)
-    in_other = jnp.where(is_low, low_other, high_other)
+    in_own = jnp.where(core_low, high_own, low_own)
+    out_other = jnp.where(core_low, high_other, low_other)
+    in_other = jnp.where(core_low, low_other, high_other)
 
     def place(slots, base, outward, rim_base, partner_base, partner_list):
         side = (slots - NB) // HALO
@@ -433,7 +475,7 @@
     inner = jnp.where(table >= 2 * NB, ZERO, table)
     slots = jnp.sum(jnp.where(hit[..., None], inner, 0), axis=1)
     lists = jnp.concatenate([8 * slots, rows[:, None], rows[:, None]], axis=1).reshape(-1)
-    table = jnp.pad(8 * table.reshape(-1, STEP * NEI), ((0, 0), (0, LANES - STEP * NEI)))
+    table = 8 * table.reshape(-1)
     raw = jnp.concatenate([near_own, near_other]).astype(F32)
     raw = jnp.sum(jnp.where(hit[..., None], raw, 0.0), axis=1)
     raw = jnp.pad(raw, ((0, 0), (0, LANES - NEI)))
@@ -441,12 +483,12 @@
     listed, packed = pl.pallas_call(
         pluck_kernel,
         out_shape=[shape(2 * HALO, TILES, 8, LANES), shape(2 * HALO, len(PACKED) * COMP, LANES)],
-        in_specs=[SMEM] + [ANY] * 2,
+        in_specs=[ANY] * 2,
         out_specs=[VMEM] * 2,
-        scratch_shapes=[pltpu.SemaphoreType.DMA((2 * HALO,))],
+        scratch_shapes=[pltpu.SemaphoreType.DMA((2,))],
         compiler_params=PARAMS,
         name="pluck",
-    )(lists, mine, other)
+    )(mine, other)
 
     live = (lax.iota(jnp.int32, NB) < live_count[0]).astype(F32)[:, None, None]
     start = (live * terminal).reshape(NB // STEP, STEP * COMP, LANES)

time: 647 us -> 587 us (0.907)
  Pallas kernels: 218 us -> 161 us
    pallas_call x8, Pallas kernels: 77.6 us -> 59 us  [slab(): steps[0]]
    pallas_call x8, Pallas kernels: 68.1 us -> 50.5 us  [slab(): steps[1](table, lists, fixes, x, fixed, *got, rim, listed, coef0, coef1)]
    pallas_call x7, Pallas kernels: 54.3 us -> 38.5 us  [slab(): steps[2]]
where the time goes in v4:
time: 587 us; the launch traced here: 582 us
  waiting for transfers between devices  238 us (41%)
  Pallas kernels  161 us (27%)
  starting transfers between devices  160 us (27%)
  local copies, waits for them, and re-layouts  14.5 us (2%)
  other arithmetic  6.58 us (1%)
    ppermute x7, waiting for transfers between devices, turn(): half = lax.ppermute(early, both, earlier(same))  99.4 us
    ppermute x17, starting transfers between devices, exchange(): lax.ppermute(first, 'space', near)  72.7 us
    pallas_call x8, Pallas kernels, slab(): steps[0]  59 us
    pallas_call x8, Pallas kernels, slab(): steps[1](table, lists, fixes, x, fixed, *got, rim, listed, coef0, coef1)  50.5 us
    ppermute x17, waiting for transfers between devices, exchange(): lax.ppermute(first, 'space', near)  46.4 us
    ppermute x17, waiting for transfers between devices, exchange(): lax.ppermute(second, 'space', far)  41.9 us
    ppermute x7, waiting for transfers between devices, turn(): got0 = lax.ppermute(msg0, both, earlier(near))  41.1 us
    pallas_call x7, Pallas kernels, slab(): steps[2]  38.5 us
  transfers between devices with their start and end apart: 67, of which 50 were waited for; matrix products, arithmetic and copies ran while one was open for 1% of the time, Pallas kernels for 3%

profile of v4, /device:TPU:113, one launch (start us, length us, event | category | flops | bytes accessed | tf_op | source)
XLA Modules:
  0.0 582.5 jit_solution(14525190125477960331)
XLA Ops:
  10.6 6.1 %collective-permute-done.8 = s32[128,7]{0,1:T(8,128)S(1)} collective-permute-done((s32[128,7]{0,1:T(8,128)S(1)}, s32[128,7]{0,1:T(8,128)S(1)}, u32[]{:S(2)}, u32[]{:S(2)}) %collective-permute-start.8) | collective-permute-done | bytes 3616 | tf_op jit(solution)/shard_map/ppermute | solution.py:449
  38.7 7.2 %shard_map.122 = (f32[256,8,128]{2,1,0:T(8,128)S(1)}, f32[256,8,128]{2,1,0:T(8,128)S(1)}, f32[160,128]{1,0:T(8,128)S(1)}, f32[160,128]{1,0:T(8,128)S(1)}, f32[16...) custom-call(s32[1536]{0:T(1024)} %mul.48.table, s32[256]{0:T(256)S(1)} %reshape.73.lists, s32[192]{0:T(256)S(1)} %mul.54.fixes, ...), custom_call_target="tpu_custom_call" | custom-call | tf_op jit(solution)/shard_map/pallas_call | solution.py:546
  57.7 6.3 %shard_map.123 = (f32[256,8,128]{2,1,0:T(8,128)S(1)}, f32[256,8,128]{2,1,0:T(8,128)S(1)}, f32[160,128]{1,0:T(8,128)S(1)}, f32[160,128]{1,0:T(8,128)S(1)}, f32[16,40,128]{2,1,0:T(8,128)}) custom-call(s32[1536]{0:T(1024)} %mul.48.table, s32[256]{0:T(256)S(1)} %reshape.73.lists, s32[192]{0:T(256)S(1)} %mul.54.fixes, ...), custom_call_target="tpu_custom_call" | custom-call | tf_op jit(solution)/shard_map/pallas_call | solution.py:550
  83.4 10.2 %collective-permute-done.18 = f32[16,40,128]{2,1,0:T(8,128)} collective-permute-done((f32[16,40,128]{2,1,0:T(8,128)S(1)}, f32[16,40,128]{2,1,0:T(8,128)}, u32[]{:S(2)}, u32[]{:S(2)}) %collective-permute-start.18) | collective-permute-done | bytes 327712 | tf_op jit(solution)/shard_map/ppermute | solution.py:567
  102.8 411.8 %while.16 = (s32[]{:T(128)}, f32[16,40,128]{2,1,0:T(8,128)}, f32[16,40,128]{2,1,0:T(8,128)}, f32[160,128]{1,0:T(8,128)}, f32[160,128]{1,0:T(8,128)}, /*index=5*/...) while((s32[]{:T(128)}, f32[16,40,128]{2,1,0:T(8,128)}, ...), condition=%wide.region_7.8_spmd, body=%wide.region_6.7_spmd.sunk | while | flops 2 | bytes 9830921 | solution.py:575
  102.8 7.3 %eval_jaxpr.3 = (f32[256,8,128]{2,1,0:T(8,128)S(1)}, f32[256,8,128]{2,1,0:T(8,128)S(1)}, f32[160,128]{1,0:T(8,128)S(1)}, f32[160,128]{1,0:T(8,128)S(1)}, f32[16,...) custom-call(s32[1536]{0:T(1024)} %get-tuple-element.417.table, s32[256]{0:T(256)S(1)} %get-tuple-element.418.lists, ...), custom_call_target="tpu_custom_call" | custom-call | tf_op jit(solution)/shard_map/while/body/eval_jaxpr/pallas_call | solution.py:546
  110.1 6.5 %collective-permute-start = (f32[160,128]{1,0:T(8,128)S(1)}, f32[160,128]{1,0:T(8,128)S(1)}, u32[]{:S(2)}, u32[]{:S(2)}) collective-permute-start(f32[160,128]{1,0:T(8,128)S(1)} %get-tuple-element.363), channel_id=1, source_target_pairs={{1,2},{2,1},{3,4},{4,3},{5,6},{6,5},{7,8},{8,7},{9,10},{10,9},{11,... | collective-permute-start | bytes 245768 | tf_op jit(solution)/shard_map/while/body/eval_jaxpr/ppermute | solution.py:432
  123.9 6.4 %eval_jaxpr.4 = (f32[256,8,128]{2,1,0:T(8,128)S(1)}, f32[256,8,128]{2,1,0:T(8,128)S(1)}, f32[160,128]{1,0:T(8,128)S(1)}, f32[160,128]{1,0:T(8,128)S(1)}, f32[16,40,128]{2,1,0:T(8,128)}) custom-call(s32[1536]{0:T(1024)} %get-tuple-element.417.table, s32[256]{0:T(256)S(1)} %get-tuple-element.418.lists, s32[192]{0:T(256)S(1)} %get-tuple-element.419.fixes, ...), custom_call_target="tpu_custom_call" | custom-call | tf_op jit(solution)/shard_map/while/body/eval_jaxpr/pallas_call | solution.py:550
  147.4 15.7 %collective-permute-done.4 = f32[16,40,128]{2,1,0:T(8,128)} collective-permute-done((f32[16,40,128]{2,1,0:T(8,128)S(1)}, f32[16,40,128]{2,1,0:T(8,128)}, u32[]{:S(2)}, u32[]{:S(2)}) %collective-permute-start.4) | collective-permute-done | bytes 327712 | tf_op jit(solution)/shard_map/while/body/eval_jaxpr/ppermute | solution.py:567
  166.1 5.8 %collective-permute-done.6 = f32[160,128]{1,0:T(8,128)} collective-permute-done((f32[160,128]{1,0:T(8,128)S(1)}, f32[160,128]{1,0:T(8,128)}, u32[]{:S(2)}, u32[]{:S(2)}) %collective-permute-start.6) | collective-permute-done | bytes 81952 | tf_op jit(solution)/shard_map/while/body/eval_jaxpr/ppermute | solution.py:568
  171.9 7.3 %eval_jaxpr.3 = (f32[256,8,128]{2,1,0:T(8,128)S(1)}, f32[256,8,128]{2,1,0:T(8,128)S(1)}, f32[160,128]{1,0:T(8,128)S(1)}, f32[160,128]{1,0:T(8,128)S(1)}, f32[16,...) custom-call(s32[1536]{0:T(1024)} %get-tuple-element.417.table, s32[256]{0:T(256)S(1)} %get-tuple-element.418.lists, ...), custom_call_target="tpu_custom_call" | custom-call | tf_op jit(solution)/shard_map/while/body/eval_jaxpr/pallas_call | solution.py:546
  191.5 6.4 %eval_jaxpr.4 = (f32[256,8,128]{2,1,0:T(8,128)S(1)}, f32[256,8,128]{2,1,0:T(8,128)S(1)}, f32[160,128]{1,0:T(8,128)S(1)}, f32[160,128]{1,0:T(8,128)S(1)}, f32[16,40,128]{2,1,0:T(8,128)}) custom-call(s32[1536]{0:T(1024)} %get-tuple-element.417.table, s32[256]{0:T(256)S(1)} %get-tuple-element.418.lists, s32[192]{0:T(256)S(1)} %get-tuple-element.419.fixes, ...), custom_call_target="tpu_custom_call" | custom-call | tf_op jit(solution)/shard_map/while/body/eval_jaxpr/pallas_call | solution.py:550
  216.2 14.8 %collective-permute-done.4 = f32[16,40,128]{2,1,0:T(8,128)} collective-permute-done((f32[16,40,128]{2,1,0:T(8,128)S(1)}, f32[16,40,128]{2,1,0:T(8,128)}, u32[]{:S(2)}, u32[]{:S(2)}) %collective-permute-start.4) | collective-permute-done | bytes 327712 | tf_op jit(solution)/shard_map/while/body/eval_jaxpr/ppermute | solution.py:567
  234.6 5.9 %collective-permute-done.6 = f32[160,128]{1,0:T(8,128)} collective-permute-done((f32[160,128]{1,0:T(8,128)S(1)}, f32[160,128]{1,0:T(8,128)}, u32[]{:S(2)}, u32[]{:S(2)}) %collective-permute-start.6) | collective-permute-done | bytes 81952 | tf_op jit(solution)/shard_map/while/body/eval_jaxpr/ppermute | solution.py:568
  240.6 7.3 %eval_jaxpr.3 = (f32[256,8,128]{2,1,0:T(8,128)S(1)}, f32[256,8,128]{2,1,0:T(8,128)S(1)}, f32[160,128]{1,0:T(8,128)S(1)}, f32[160,128]{1,0:T(8,128)S(1)}, f32[16,...) custom-call(s32[1536]{0:T(1024)} %get-tuple-element.417.table, s32[256]{0:T(256)S(1)} %get-tuple-element.418.lists, ...), custom_call_target="tpu_custom_call" | custom-call | tf_op jit(solution)/shard_map/while/body/eval_jaxpr/pallas_call | solution.py:546
  260.1 6.4 %eval_jaxpr.4 = (f32[256,8,128]{2,1,0:T(8,128)S(1)}, f32[256,8,128]{2,1,0:T(8,128)S(1)}, f32[160,128]{1,0:T(8,128)S(1)}, f32[160,128]{1,0:T(8,128)S(1)}, f32[16,40,128]{2,1,0:T(8,128)}) custom-call(s32[1536]{0:T(1024)} %get-tuple-element.417.table, s32[256]{0:T(256)S(1)} %get-tuple-element.418.lists, s32[192]{0:T(256)S(1)} %get-tuple-element.419.fixes, ...), custom_call_target="tpu_custom_call" | custom-call | tf_op jit(solution)/shard_map/while/body/eval_jaxpr/pallas_call | solution.py:550
  284.8 14.7 %collective-permute-done.4 = f32[16,40,128]{2,1,0:T(8,128)} collective-permute-done((f32[16,40,128]{2,1,0:T(8,128)S(1)}, f32[16,40,128]{2,1,0:T(8,128)}, u32[]{:S(2)}, u32[]{:S(2)}) %collective-permute-start.4) | collective-permute-done | bytes 327712 | tf_op jit(solution)/shard_map/while/body/eval_jaxpr/ppermute | solution.py:567
  303.1 5.9 %collective-permute-done.6 = f32[160,128]{1,0:T(8,128)} collective-permute-done((f32[160,128]{1,0:T(8,128)S(1)}, f32[160,128]{1,0:T(8,128)}, u32[]{:S(2)}, u32[]{:S(2)}) %collective-permute-start.6) | collective-permute-done | bytes 81952 | tf_op jit(solution)/shard_map/while/body/eval_jaxpr/ppermute | solution.py:568
  309.1 7.3 %eval_jaxpr.3 = (f32[256,8,128]{2,1,0:T(8,128)S(1)}, f32[256,8,128]{2,1,0:T(8,128)S(1)}, f32[160,128]{1,0:T(8,128)S(1)}, f32[160,128]{1,0:T(8,128)S(1)}, f32[16,...) custom-call(s32[1536]{0:T(1024)} %get-tuple-element.417.table, s32[256]{0:T(256)S(1)} %get-tuple-element.418.lists, ...), custom_call_target="tpu_custom_call" | custom-call | tf_op jit(solution)/shard_map/while/body/eval_jaxpr/pallas_call | solution.py:546
  328.6 6.4 %eval_jaxpr.4 = (f32[256,8,128]{2,1,0:T(8,128)S(1)}, f32[256,8,128]{2,1,0:T(8,128)S(1)}, f32[160,128]{1,0:T(8,128)S(1)}, f32[160,128]{1,0:T(8,128)S(1)}, f32[16,40,128]{2,1,0:T(8,128)}) custom-call(s32[1536]{0:T(1024)} %get-tuple-element.417.table, s32[256]{0:T(256)S(1)} %get-tuple-element.418.lists, s32[192]{0:T(256)S(1)} %get-tuple-element.419.fixes, ...), custom_call_target="tpu_custom_call" | custom-call | tf_op jit(solution)/shard_map/while/body/eval_jaxpr/pallas_call | solution.py:550
  353.3 14.7 %collective-permute-done.4 = f32[16,40,128]{2,1,0:T(8,128)} collective-permute-done((f32[16,40,128]{2,1,0:T(8,128)S(1)}, f32[16,40,128]{2,1,0:T(8,128)}, u32[]{:S(2)}, u32[]{:S(2)}) %collective-permute-start.4) | collective-permute-done | bytes 327712 | tf_op jit(solution)/shard_map/while/body/eval_jaxpr/ppermute | solution.py:567
  371.7 5.9 %collective-permute-done.6 = f32[160,128]{1,0:T(8,128)} collective-permute-done((f32[160,128]{1,0:T(8,128)S(1)}, f32[160,128]{1,0:T(8,128)}, u32[]{:S(2)}, u32[]{:S(2)}) %collective-permute-start.6) | collective-permute-done | bytes 81952 | tf_op jit(solution)/shard_map/while/body/eval_jaxpr/ppermute | solution.py:568
  377.6 7.3 %eval_jaxpr.3 = (f32[256,8,128]{2,1,0:T(8,128)S(1)}, f32[256,8,128]{2,1,0:T(8,128)S(1)}, f32[160,128]{1,0:T(8,128)S(1)}, f32[160,128]{1,0:T(8,128)S(1)}, f32[16,...) custom-call(s32[1536]{0:T(1024)} %get-tuple-element.417.table, s32[256]{0:T(256)S(1)} %get-tuple-element.418.lists, ...), custom_call_target="tpu_custom_call" | custom-call | tf_op jit(solution)/shard_map/while/body/eval_jaxpr/pallas_call | solution.py:546
  397.1 6.4 %eval_jaxpr.4 = (f32[256,8,128]{2,1,0:T(8,128)S(1)}, f32[256,8,128]{2,1,0:T(8,128)S(1)}, f32[160,128]{1,0:T(8,128)S(1)}, f32[160,128]{1,0:T(8,128)S(1)}, f32[16,40,128]{2,1,0:T(8,128)}) custom-call(s32[1536]{0:T(1024)} %get-tuple-element.417.table, s32[256]{0:T(256)S(1)} %get-tuple-element.418.lists, s32[192]{0:T(256)S(1)} %get-tuple-element.419.fixes, ...), custom_call_target="tpu_custom_call" | custom-call | tf_op jit(solution)/shard_map/while/body/eval_jaxpr/pallas_call | solution.py:550
  421.9 14.7 %collective-permute-done.4 = f32[16,40,128]{2,1,0:T(8,128)} collective-permute-done((f32[16,40,128]{2,1,0:T(8,128)S(1)}, f32[16,40,128]{2,1,0:T(8,128)}, u32[]{:S(2)}, u32[]{:S(2)}) %collective-permute-start.4) | collective-permute-done | bytes 327712 | tf_op jit(solution)/shard_map/while/body/eval_jaxpr/ppermute | solution.py:567
  440.2 5.9 %collective-permute-done.6 = f32[160,128]{1,0:T(8,128)} collective-permute-done((f32[160,128]{1,0:T(8,128)S(1)}, f32[160,128]{1,0:T(8,128)}, u32[]{:S(2)}, u32[]{:S(2)}) %collective-permute-start.6) | collective-permute-done | bytes 81952 | tf_op jit(solution)/shard_map/while/body/eval_jaxpr/ppermute | solution.py:568
  446.1 7.3 %eval_jaxpr.3 = (f32[256,8,128]{2,1,0:T(8,128)S(1)}, f32[256,8,128]{2,1,0:T(8,128)S(1)}, f32[160,128]{1,0:T(8,128)S(1)}, f32[160,128]{1,0:T(8,128)S(1)}, f32[16,...) custom-call(s32[1536]{0:T(1024)} %get-tuple-element.417.table, s32[256]{0:T(256)S(1)} %get-tuple-element.418.lists, ...), custom_call_target="tpu_custom_call" | custom-call | tf_op jit(solution)/shard_map/while/body/eval_jaxpr/pallas_call | solution.py:546
  465.6 6.4 %eval_jaxpr.4 = (f32[256,8,128]{2,1,0:T(8,128)S(1)}, f32[256,8,128]{2,1,0:T(8,128)S(1)}, f32[160,128]{1,0:T(8,128)S(1)}, f32[160,128]{1,0:T(8,128)S(1)}, f32[16,40,128]{2,1,0:T(8,128)}) custom-call(s32[1536]{0:T(1024)} %get-tuple-element.417.table, s32[256]{0:T(256)S(1)} %get-tuple-element.418.lists, s32[192]{0:T(256)S(1)} %get-tuple-element.419.fixes, ...), custom_call_target="tpu_custom_call" | custom-call | tf_op jit(solution)/shard_map/while/body/eval_jaxpr/pallas_call | solution.py:550
  490.4 14.7 %collective-permute-done.4 = f32[16,40,128]{2,1,0:T(8,128)} collective-permute-done((f32[16,40,128]{2,1,0:T(8,128)S(1)}, f32[16,40,128]{2,1,0:T(8,128)}, u32[]{:S(2)}, u32[]{:S(2)}) %collective-permute-start.4) | collective-permute-done | bytes 327712 | tf_op jit(solution)/shard_map/while/body/eval_jaxpr/ppermute | solution.py:567
  508.7 5.9 %collective-permute-done.6 = f32[160,128]{1,0:T(8,128)} collective-permute-done((f32[160,128]{1,0:T(8,128)S(1)}, f32[160,128]{1,0:T(8,128)}, u32[]{:S(2)}, u32[]{:S(2)}) %collective-permute-start.6) | collective-permute-done | bytes 81952 | tf_op jit(solution)/shard_map/while/body/eval_jaxpr/ppermute | solution.py:568
  515.7 7.8 %shard_map.125 = (f32[256,8,128]{2,1,0:T(8,128)S(1)}, f32[256,8,128]{2,1,0:T(8,128)S(1)}, f32[160,128]{1,0:T(8,128)S(1)}, f32[160,128]{1,0:T(8,128)S(1)}, f32[16...) custom-call(s32[1536]{0:T(1024)} %mul.48.table, s32[256]{0:T(256)S(1)} %get-tuple-element.471, ...), custom_call_target="tpu_custom_call" | custom-call | tf_op jit(solution)/shard_map/pallas_call | solution.py:546
  565.9 11.1 %all-to-all-start = ((f32[8,1,128]{2,1,0:T(1,128)}), f32[8,1,128]{2,1,0:T(1,128)S(1)}, u32[]{:S(2)}, u32[]{:S(2)}) async-start(f32[8,1,128]{2,1,0:T(1,128)} %broadcast_in_dim.103), calls=%async_computation | async-start | bytes 8192 | tf_op jit(solution)/shard_map/all_to_all | solution.py:587
  (233 shorter events, 317.7 us)
Async XLA Ops:
  20.9 10.4 %collective-permute-start.11 = (f32[352,128]{1,0:T(8,128)S(1)}, f32[352,128]{1,0:T(8,128)S(1)}, u32[]{:S(2)}, u32[]{:S(2)}) collective-permute-start(f32[352,128]{1,0:T(8,128)S(1)} %get-tuple-element.142), channel_id=1, source_target_pairs={{1,2},{2,1},{3,4},{4,3},{5,6},{6,5},{7,8},{8,7},{9,10},{10,9},{11,... | collective-permute-start | bytes 540680 | tf_op jit(solution)/shard_map/ppermute | solution.py:432
  25.7 9.7 %collective-permute-start.12 = (f32[352,128]{1,0:T(8,128)S(1)}, f32[352,128]{1,0:T(8,128)}, u32[]{:S(2)}, u32[]{:S(2)}) collective-permute-start(f32[352,128]{1,0:T(8,128)S(1)} %get-tuple-element.143), channel_id=1, source_target_pairs={{0,3},{2,5},{3,0},{4,7},{5,2},{6,9},{7,4},{8,11},{9,6},{10,13},{11... | collective-permute-start | bytes 540680 | tf_op jit(solution)/shard_map/ppermute | solution.py:432
  31.3 39.2 %collective-permute-start.17 = (f32[32,40,128]{2,1,0:T(8,128)S(1)}, f32[32,40,128]{2,1,0:T(8,128)S(1)}, u32[]{:S(2)}, u32[]{:S(2)}) collective-permute-start(f32[32,40,128]{2,1,0:T(8,128)S(1)} %get-tuple-element.157), channel_id=1, source_target_pairs={{0,32},{32,64},{64,96},{96,128},{128,160},{160,192},{192,224},{1,3... | collective-permute-start | bytes 1966088 | tf_op jit(solution)/shard_map/ppermute | solution.py:532
  45.8 9.4 %collective-permute-start.13 = (f32[160,128]{1,0:T(8,128)S(1)}, f32[160,128]{1,0:T(8,128)S(1)}, u32[]{:S(2)}, u32[]{:S(2)}) collective-permute-start(f32[160,128]{1,0:T(8,128)S(1)} %get-tuple-element.148), channel_id=1, source_target_pairs={{1,2},{2,1},{3,4},{4,3},{5,6},{6,5},{7,8},{8,7},{9,10},{10,9},{11,... | collective-permute-start | bytes 245768 | tf_op jit(solution)/shard_map/ppermute | solution.py:432
  64.0 9.4 %collective-permute-start.15 = (f32[160,128]{1,0:T(8,128)S(1)}, f32[160,128]{1,0:T(8,128)S(1)}, u32[]{:S(2)}, u32[]{:S(2)}) collective-permute-start(f32[160,128]{1,0:T(8,128)S(1)} %get-tuple-element.154), channel_id=1, source_target_pairs={{1,2},{2,1},{3,4},{4,3},{5,6},{6,5},{7,8},{8,7},{9,10},{10,9},{11,... | collective-permute-start | bytes 245768 | tf_op jit(solution)/shard_map/ppermute | solution.py:432
  82.1 11.5 %collective-permute-start.18 = (f32[16,40,128]{2,1,0:T(8,128)S(1)}, f32[16,40,128]{2,1,0:T(8,128)}, u32[]{:S(2)}, u32[]{:S(2)}) collective-permute-start(f32[16,40,128]{2,1,0:T(8,128)S(1)} %get-tuple-element.158), channel_id=1, source_target_pairs={{32,0},{33,1},{34,2},{35,3},{36,4},{37,5},{38,6},{39,7},{40,8},{41... | collective-permute-start | bytes 983048 | tf_op jit(solution)/shard_map/ppermute | solution.py:567
  110.1 9.4 %collective-permute-start = (f32[160,128]{1,0:T(8,128)S(1)}, f32[160,128]{1,0:T(8,128)S(1)}, u32[]{:S(2)}, u32[]{:S(2)}) collective-permute-start(f32[160,128]{1,0:T(8,128)S(1)} %get-tuple-element.363), channel_id=1, source_target_pairs={{1,2},{2,1},{3,4},{4,3},{5,6},{6,5},{7,8},{8,7},{9,10},{10,9},{11,... | collective-permute-start | bytes 245768 | tf_op jit(solution)/shard_map/while/body/eval_jaxpr/ppermute | solution.py:432
  130.3 9.4 %collective-permute-start.2 = (f32[160,128]{1,0:T(8,128)S(1)}, f32[160,128]{1,0:T(8,128)S(1)}, u32[]{:S(2)}, u32[]{:S(2)}) collective-permute-start(f32[160,128]{1,0:T(8,128)S(1)} %get-tuple-element.369), channel_id=1, source_target_pairs={{1,2},{2,1},{3,4},{4,3},{5,6},{6,5},{7,8},{8,7},{9,10},{10,9},{11,... | collective-permute-start | bytes 245768 | tf_op jit(solution)/shard_map/while/body/eval_jaxpr/ppermute | solution.py:432
  146.1 17.0 %collective-permute-start.4 = (f32[16,40,128]{2,1,0:T(8,128)S(1)}, f32[16,40,128]{2,1,0:T(8,128)}, u32[]{:S(2)}, u32[]{:S(2)}) collective-permute-start(f32[16,40,128]{2,1,0:T(8,128)S(1)} %get-tuple-element.371), channel_id=1, source_target_pairs={{32,0},{33,1},{34,2},{35,3},{36,4},{37,5},{38,6},{39,7},{40,8},{41... | collective-permute-start | bytes 983048 | tf_op jit(solution)/shard_map/while/body/eval_jaxpr/ppermute | solution.py:567
  179.3 9.4 %collective-permute-start = (f32[160,128]{1,0:T(8,128)S(1)}, f32[160,128]{1,0:T(8,128)S(1)}, u32[]{:S(2)}, u32[]{:S(2)}) collective-permute-start(f32[160,128]{1,0:T(8,128)S(1)} %get-tuple-element.363), channel_id=1, source_target_pairs={{1,2},{2,1},{3,4},{4,3},{5,6},{6,5},{7,8},{8,7},{9,10},{10,9},{11,... | collective-permute-start | bytes 245768 | tf_op jit(solution)/shard_map/while/body/eval_jaxpr/ppermute | solution.py:432
  198.0 9.4 %collective-permute-start.2 = (f32[160,128]{1,0:T(8,128)S(1)}, f32[160,128]{1,0:T(8,128)S(1)}, u32[]{:S(2)}, u32[]{:S(2)}) collective-permute-start(f32[160,128]{1,0:T(8,128)S(1)} %get-tuple-element.369), channel_id=1, source_target_pairs={{1,2},{2,1},{3,4},{4,3},{5,6},{6,5},{7,8},{8,7},{9,10},{10,9},{11,... | collective-permute-start | bytes 245768 | tf_op jit(solution)/shard_map/while/body/eval_jaxpr/ppermute | solution.py:432
  214.9 16.1 %collective-permute-start.4 = (f32[16,40,128]{2,1,0:T(8,128)S(1)}, f32[16,40,128]{2,1,0:T(8,128)}, u32[]{:S(2)}, u32[]{:S(2)}) collective-permute-start(f32[16,40,128]{2,1,0:T(8,128)S(1)} %get-tuple-element.371), channel_id=1, source_target_pairs={{32,0},{33,1},{34,2},{35,3},{36,4},{37,5},{38,6},{39,7},{40,8},{41... | collective-permute-start | bytes 983048 | tf_op jit(solution)/shard_map/while/body/eval_jaxpr/ppermute | solution.py:567
  231.0 9.6 %collective-permute-start.5 = (f32[16,40,128]{2,1,0:T(8,128)}, f32[16,40,128]{2,1,0:T(8,128)}, u32[]{:S(2)}, u32[]{:S(2)}) collective-permute-start(f32[16,40,128]{2,1,0:T(8,128)} %collective-permute-done.4), channel_id=1, source_target_pairs={{0,1},{1,0},{2,3},{3,2},{4,5},{5,4},{6,7},{7,6},{8,9},{9,8},{10,11... | collective-permute-start | bytes 983048 | tf_op jit(solution)/shard_map/while/body/eval_jaxpr/ppermute | solution.py:570
  247.9 9.4 %collective-permute-start = (f32[160,128]{1,0:T(8,128)S(1)}, f32[160,128]{1,0:T(8,128)S(1)}, u32[]{:S(2)}, u32[]{:S(2)}) collective-permute-start(f32[160,128]{1,0:T(8,128)S(1)} %get-tuple-element.363), channel_id=1, source_target_pairs={{1,2},{2,1},{3,4},{4,3},{5,6},{6,5},{7,8},{8,7},{9,10},{10,9},{11,... | collective-permute-start | bytes 245768 | tf_op jit(solution)/shard_map/while/body/eval_jaxpr/ppermute | solution.py:432
  266.5 9.4 %collective-permute-start.2 = (f32[160,128]{1,0:T(8,128)S(1)}, f32[160,128]{1,0:T(8,128)S(1)}, u32[]{:S(2)}, u32[]{:S(2)}) collective-permute-start(f32[160,128]{1,0:T(8,128)S(1)} %get-tuple-element.369), channel_id=1, source_target_pairs={{1,2},{2,1},{3,4},{4,3},{5,6},{6,5},{7,8},{8,7},{9,10},{10,9},{11,... | collective-permute-start | bytes 245768 | tf_op jit(solution)/shard_map/while/body/eval_jaxpr/ppermute | solution.py:432
  283.5 16.0 %collective-permute-start.4 = (f32[16,40,128]{2,1,0:T(8,128)S(1)}, f32[16,40,128]{2,1,0:T(8,128)}, u32[]{:S(2)}, u32[]{:S(2)}) collective-permute-start(f32[16,40,128]{2,1,0:T(8,128)S(1)} %get-tuple-element.371), channel_id=1, source_target_pairs={{32,0},{33,1},{34,2},{35,3},{36,4},{37,5},{38,6},{39,7},{40,8},{41... | collective-permute-start | bytes 983048 | tf_op jit(solution)/shard_map/while/body/eval_jaxpr/ppermute | solution.py:567
  299.5 9.6 %collective-permute-start.5 = (f32[16,40,128]{2,1,0:T(8,128)}, f32[16,40,128]{2,1,0:T(8,128)}, u32[]{:S(2)}, u32[]{:S(2)}) collective-permute-start(f32[16,40,128]{2,1,0:T(8,128)} %collective-permute-done.4), channel_id=1, source_target_pairs={{0,1},{1,0},{2,3},{3,2},{4,5},{5,4},{6,7},{7,6},{8,9},{9,8},{10,11... | collective-permute-start | bytes 983048 | tf_op jit(solution)/shard_map/while/body/eval_jaxpr/ppermute | solution.py:570
  316.4 9.4 %collective-permute-start = (f32[160,128]{1,0:T(8,128)S(1)}, f32[160,128]{1,0:T(8,128)S(1)}, u32[]{:S(2)}, u32[]{:S(2)}) collective-permute-start(f32[160,128]{1,0:T(8,128)S(1)} %get-tuple-element.363), channel_id=1, source_target_pairs={{1,2},{2,1},{3,4},{4,3},{5,6},{6,5},{7,8},{8,7},{9,10},{10,9},{11,... | collective-permute-start | bytes 245768 | tf_op jit(solution)/shard_map/while/body/eval_jaxpr/ppermute | solution.py:432
  335.0 9.4 %collective-permute-start.2 = (f32[160,128]{1,0:T(8,128)S(1)}, f32[160,128]{1,0:T(8,128)S(1)}, u32[]{:S(2)}, u32[]{:S(2)}) collective-permute-start(f32[160,128]{1,0:T(8,128)S(1)} %get-tuple-element.369), channel_id=1, source_target_pairs={{1,2},{2,1},{3,4},{4,3},{5,6},{6,5},{7,8},{8,7},{9,10},{10,9},{11,... | collective-permute-start | bytes 245768 | tf_op jit(solution)/shard_map/while/body/eval_jaxpr/ppermute | solution.py:432
  352.0 16.0 %collective-permute-start.4 = (f32[16,40,128]{2,1,0:T(8,128)S(1)}, f32[16,40,128]{2,1,0:T(8,128)}, u32[]{:S(2)}, u32[]{:S(2)}) collective-permute-start(f32[16,40,128]{2,1,0:T(8,128)S(1)} %get-tuple-element.371), channel_id=1, source_target_pairs={{32,0},{33,1},{34,2},{35,3},{36,4},{37,5},{38,6},{39,7},{40,8},{41... | collective-permute-start | bytes 983048 | tf_op jit(solution)/shard_map/while/body/eval_jaxpr/ppermute | solution.py:567
  368.0 9.6 %collective-permute-start.5 = (f32[16,40,128]{2,1,0:T(8,128)}, f32[16,40,128]{2,1,0:T(8,128)}, u32[]{:S(2)}, u32[]{:S(2)}) collective-permute-start(f32[16,40,128]{2,1,0:T(8,128)} %collective-permute-done.4), channel_id=1, source_target_pairs={{0,1},{1,0},{2,3},{3,2},{4,5},{5,4},{6,7},{7,6},{8,9},{9,8},{10,11... | collective-permute-start | bytes 983048 | tf_op jit(solution)/shard_map/while/body/eval_jaxpr/ppermute | solution.py:570
  384.9 9.4 %collective-permute-start = (f32[160,128]{1,0:T(8,128)S(1)}, f32[160,128]{1,0:T(8,128)S(1)}, u32[]{:S(2)}, u32[]{:S(2)}) collective-permute-start(f32[160,128]{1,0:T(8,128)S(1)} %get-tuple-element.363), channel_id=1, source_target_pairs={{1,2},{2,1},{3,4},{4,3},{5,6},{6,5},{7,8},{8,7},{9,10},{10,9},{11,... | collective-permute-start | bytes 245768 | tf_op jit(solution)/shard_map/while/body/eval_jaxpr/ppermute | solution.py:432
  403.5 9.4 %collective-permute-start.2 = (f32[160,128]{1,0:T(8,128)S(1)}, f32[160,128]{1,0:T(8,128)S(1)}, u32[]{:S(2)}, u32[]{:S(2)}) collective-permute-start(f32[160,128]{1,0:T(8,128)S(1)} %get-tuple-element.369), channel_id=1, source_target_pairs={{1,2},{2,1},{3,4},{4,3},{5,6},{6,5},{7,8},{8,7},{9,10},{10,9},{11,... | collective-permute-start | bytes 245768 | tf_op jit(solution)/shard_map/while/body/eval_jaxpr/ppermute | solution.py:432
  420.6 16.0 %collective-permute-start.4 = (f32[16,40,128]{2,1,0:T(8,128)S(1)}, f32[16,40,128]{2,1,0:T(8,128)}, u32[]{:S(2)}, u32[]{:S(2)}) collective-permute-start(f32[16,40,128]{2,1,0:T(8,128)S(1)} %get-tuple-element.371), channel_id=1, source_target_pairs={{32,0},{33,1},{34,2},{35,3},{36,4},{37,5},{38,6},{39,7},{40,8},{41... | collective-permute-start | bytes 983048 | tf_op jit(solution)/shard_map/while/body/eval_jaxpr/ppermute | solution.py:567
  436.5 9.6 %collective-permute-start.5 = (f32[16,40,128]{2,1,0:T(8,128)}, f32[16,40,128]{2,1,0:T(8,128)}, u32[]{:S(2)}, u32[]{:S(2)}) collective-permute-start(f32[16,40,128]{2,1,0:T(8,128)} %collective-permute-done.4), channel_id=1, source_target_pairs={{0,1},{1,0},{2,3},{3,2},{4,5},{5,4},{6,7},{7,6},{8,9},{9,8},{10,11... | collective-permute-start | bytes 983048 | tf_op jit(solution)/shard_map/while/body/eval_jaxpr/ppermute | solution.py:570
  453.5 9.4 %collective-permute-start = (f32[160,128]{1,0:T(8,128)S(1)}, f32[160,128]{1,0:T(8,128)S(1)}, u32[]{:S(2)}, u32[]{:S(2)}) collective-permute-start(f32[160,128]{1,0:T(8,128)S(1)} %get-tuple-element.363), channel_id=1, source_target_pairs={{1,2},{2,1},{3,4},{4,3},{5,6},{6,5},{7,8},{8,7},{9,10},{10,9},{11,... | collective-permute-start | bytes 245768 | tf_op jit(solution)/shard_map/while/body/eval_jaxpr/ppermute | solution.py:432
  472.0 9.4 %collective-permute-start.2 = (f32[160,128]{1,0:T(8,128)S(1)}, f32[160,128]{1,0:T(8,128)S(1)}, u32[]{:S(2)}, u32[]{:S(2)}) collective-permute-start(f32[160,128]{1,0:T(8,128)S(1)} %get-tuple-element.369), channel_id=1, source_target_pairs={{1,2},{2,1},{3,4},{4,3},{5,6},{6,5},{7,8},{8,7},{9,10},{10,9},{11,... | collective-permute-start | bytes 245768 | tf_op jit(solution)/shard_map/while/body/eval_jaxpr/ppermute | solution.py:432
  489.1 16.0 %collective-permute-start.4 = (f32[16,40,128]{2,1,0:T(8,128)S(1)}, f32[16,40,128]{2,1,0:T(8,128)}, u32[]{:S(2)}, u32[]{:S(2)}) collective-permute-start(f32[16,40,128]{2,1,0:T(8,128)S(1)} %get-tuple-element.371), channel_id=1, source_target_pairs={{32,0},{33,1},{34,2},{35,3},{36,4},{37,5},{38,6},{39,7},{40,8},{41... | collective-permute-start | bytes 983048 | tf_op jit(solution)/shard_map/while/body/eval_jaxpr/ppermute | solution.py:567
  505.1 9.6 %collective-permute-start.5 = (f32[16,40,128]{2,1,0:T(8,128)}, f32[16,40,128]{2,1,0:T(8,128)}, u32[]{:S(2)}, u32[]{:S(2)}) collective-permute-start(f32[16,40,128]{2,1,0:T(8,128)} %collective-permute-done.4), channel_id=1, source_target_pairs={{0,1},{1,0},{2,3},{3,2},{4,5},{5,4},{6,7},{7,6},{8,9},{9,8},{10,11... | collective-permute-start | bytes 983048 | tf_op jit(solution)/shard_map/while/body/eval_jaxpr/ppermute | solution.py:570
  523.6 9.4 %collective-permute-start.22 = (f32[160,128]{1,0:T(8,128)S(1)}, f32[160,128]{1,0:T(8,128)S(1)}, u32[]{:S(2)}, u32[]{:S(2)}) collective-permute-start(f32[160,128]{1,0:T(8,128)S(1)} %get-tuple-element.167), channel_id=1, source_target_pairs={{1,2},{2,1},{3,4},{4,3},{5,6},{6,5},{7,8},{8,7},{9,10},{10,9},{11,... | collective-permute-start | bytes 245768 | tf_op jit(solution)/shard_map/ppermute | solution.py:432
  541.5 9.4 %collective-permute-start.24 = (f32[160,128]{1,0:T(8,128)S(1)}, f32[160,128]{1,0:T(8,128)S(1)}, u32[]{:S(2)}, u32[]{:S(2)}) collective-permute-start(f32[160,128]{1,0:T(8,128)S(1)} %get-tuple-element.173), channel_id=1, source_target_pairs={{1,2},{2,1},{3,4},{4,3},{5,6},{6,5},{7,8},{8,7},{9,10},{10,9},{11,... | collective-permute-start | bytes 245768 | tf_op jit(solution)/shard_map/ppermute | solution.py:432
  565.9 16.0 %all-to-all-start = ((f32[8,1,128]{2,1,0:T(1,128)}), f32[8,1,128]{2,1,0:T(1,128)S(1)}, u32[]{:S(2)}, u32[]{:S(2)}) async-start(f32[8,1,128]{2,1,0:T(1,128)} %broadcast_in_dim.103), calls=%async_computation | async-start | bytes 8192 | tf_op jit(solution)/shard_map/all_to_all | solution.py:587
  (56 other events, 496.0 us)

commit v5 on v4

--- a/solution.py
+++ b/solution.py
@@ -14,7 +14,9 @@
 STEP = 8
 UNROLL = 2
 CHUNKS = 4
+TABLE = 2 * NB * NEI
 WIDE = 8
+INTS = TABLE + 2 * HALO * (WIDE + NEI)
 MESSAGE = 2 * HALO * COMP
 RIM = COMP + NEI + 1
 ZERO = 2 * NB + 2 * HALO
@@ -37,53 +39,50 @@
 
 
 def prep_kernel(live_ref, chosen, jac, source, face, cell, volume, out):
-    count = live_ref[0]
-    lane = lax.broadcasted_iota(jnp.int32, (1, LANES), 1)
-    row = lax.broadcasted_iota(jnp.int32, (COMP, LANES), 0)
-    blank = jnp.zeros((8, LANES), F32)
+    lane = lax.broadcasted_iota(jnp.int32, (STEP, LANES), 1)
+    row = lax.broadcasted_iota(jnp.int32, (STEP, LANES), 0)
     width = G_LISTED + TILES
     flat = out.reshape(GROUPS * width * 8, LANES)
 
-    def terms(b):
-        mass = inverse_step * volume[pl.ds(b, 1), :]
-        along = cell[pl.ds(b, 1), :]
-        faces = face[b]
-        total = jnp.sum(faces, axis=0, keepdims=True)
-        diagonal = jnp.zeros((COMP, LANES), F32)
-        for i in range(COMP):
-            diagonal = jnp.where(row == i, jac[b, i], diagonal)
-        live = jnp.where(b < count, 1.0, 0.0).astype(F32)
-        pre = live * (1.0 / (mass + diagonal + total + 2.0 * along))
-        own = []
-        for i in range(COMP):
-            keep = live - pre * (mass + jac[b, i])
-            own.append(jnp.where(row == i, keep, -pre * jac[b, i]))
-        left = jnp.where(lane == 0, 0.0, along)
-        right = jnp.where(lane == LANES - 1, 0.0, along)
-        return own, faces, left, right, pre, pre * source[1, b], pre * source[0, b], pre * mass
-
     def group(g, carry):
-        for s in range(STEP):
-            own, faces, left, right, *rest = terms(g * STEP + s)
-            base = g * (width * 8) + s
-            for n, value in enumerate(own + rest):
-                flat[pl.ds(base + n * (COMP * 8), COMP, stride=8)] = value
-            out[g, G_LEFT, s : s + 1] = left
-            out[g, G_RIGHT, s : s + 1] = right
-            out[g, G_FACE + s, 0:NEI] = faces
-        own, faces, left, right, *rest = terms(chosen[g])
+        rows = pl.ds(g * STEP, STEP)
+        mass = inverse_step * volume[rows]
+        along = cell[rows]
+        total = 2.0 * along
+        for k in range(NEI):
+            total = total + face[k, rows]
+            flat[pl.ds((g * width + G_FACE) * 8 + k, STEP, stride=8)] = face[k, rows]
+        live = jnp.where(row + g * STEP < live_ref[0], 1.0, 0.0).astype(F32)
+        for j in range(COMP):
+            diagonal = mass + jac[j, j, rows]
+            pre = live * (1.0 / (diagonal + total))
+            for i in range(COMP):
+                out[g, i * COMP + j] = live - pre * diagonal if i == j else -pre * jac[i, j, rows]
+            out[g, G_PRE + j] = pre
+            out[g, G_LATE + j] = pre * source[1, j, rows]
+            out[g, G_EARLY + j] = pre * source[0, j, rows]
+            out[g, G_MASS + j] = pre * mass
+        out[g, G_LEFT] = jnp.where(lane == 0, 0.0, along)
+        out[g, G_RIGHT] = jnp.where(lane == LANES - 1, 0.0, along)
+        return carry
+
+    lax.fori_loop(0, GROUPS, group, 0)
+    blank = jnp.zeros((8, LANES), F32)
+
+    def listed(i, carry):
+        g, s = chosen[i] // STEP, chosen[i] % STEP
+        base = g * (width * 8) + s
         for n in range(TILES):
-            out[g, G_LISTED + n] = blank
-        for n, value in enumerate(own):
-            out[g, G_LISTED + n, 0:COMP] = value
-        out[g, G_LISTED + FACE, 0:NEI] = faces
-        out[g, G_LISTED + FACE, NEI : NEI + 1] = left
-        out[g, G_LISTED + FACE, NEI + 1 : NEI + 2] = right
-        for n, value in enumerate(rest):
-            out[g, G_LISTED + PRE + n, 0:COMP] = value
+            out[i, G_LISTED + n] = blank
+        for n in range(COMP + 4):
+            tile = n if n < COMP else n + PRE - COMP
+            out[i, G_LISTED + tile, 0:COMP] = flat[pl.ds(base + n * (COMP * 8), COMP, stride=8)]
+        out[i, G_LISTED + FACE, 0:NEI] = out[g, G_FACE + s, 0:NEI]
+        out[i, G_LISTED + FACE, NEI : NEI + 1] = flat[pl.ds(base + G_LEFT * 8, 1)]
+        out[i, G_LISTED + FACE, NEI + 1 : NEI + 2] = flat[pl.ds(base + G_RIGHT * 8, 1)]
         return carry
 
-    lax.fori_loop(0, GROUPS, group, 0)
+    lax.fori_loop(0, HALO, listed, 0)
 
 
 def at_row(ext, row):
@@ -121,7 +120,7 @@
             for s in range(STEP):
                 terms = []
                 for k in range(NEI):
-                    picked = at_row(ext, table.at[pl.ds(s * NEI + k, 2 * NB * NEI - STEP * NEI + 1)][row])
+                    picked = at_row(ext, table.at[pl.ds(s * NEI + k, TABLE - STEP * NEI + 1)][row])
                     terms.append(coef[g, G_FACE + s, k : k + 1] * picked)
                 total = ((terms[0] + terms[1]) + (terms[2] + terms[3])) + (terms[4] + terms[5])
                 sums[(half * GROUPS + g) * STEP + s] = total
@@ -183,18 +182,15 @@
 
 
 def unpack(ext, halves):
-    blank = jnp.zeros((8, LANES), F32)
-    ext[ZERO] = blank
+    ext[ZERO] = jnp.zeros((8, LANES), F32)
     for half, source in enumerate(halves):
 
         def turn(g, carry, half=half, source=source):
-            for s in range(STEP):
-                b = half * NB + g * STEP + s
-                ext[b] = blank
-                ext[b, 0:COMP] = source[g, COMP * s : COMP * (s + 1)]
+            for j in range(COMP):
+                rows_of(ext, (half * GROUPS + g) * (STEP * 8) + j)[...] = source[j, pl.ds(g * STEP, STEP)]
             return carry
 
-        lax.fori_loop(0, NB // STEP, turn, 0)
+        lax.fori_loop(0, GROUPS, turn, 0)
 
 
 def receive(ext, after, got):
@@ -271,8 +267,12 @@
 
 
 def make_step(stage):
-    def kernel(table, lists, fixes, *refs):
-        refs = list(refs)
+    def kernel(ints, *refs):
+        *refs, table, arrived = refs
+        fetch = pltpu.make_async_copy(ints, table, arrived)
+        fetch.start()
+        lists = table.at[pl.ds(TABLE, 2 * HALO * WIDE)]
+        fixes = table.at[pl.ds(TABLE + 2 * HALO * WIDE, 2 * HALO * NEI)]
 
         def take(n):
             head = refs[:n]
@@ -330,6 +330,7 @@
 
             lax.fori_loop(0, 2 * NB // STEP, copy, 0)
             receive(ext, after, (got0, got1))
+        fetch.wait()
         for h in range(2 * HALO):
             total = rim[h, 0, 0:1] * at_row(ext, fixes[h * NEI])
             for k in range(1, NEI):
@@ -337,7 +338,7 @@
             after[2 * NB + h] = after[2 * NB + h] + rim[h, 1] * total
 
         def keep_lam(g, j, value):
-            lam[g, pl.ds(j, STEP, stride=COMP)] = value
+            lam[j, pl.ds(g * STEP, STEP)] = value
 
         def put_a(start, g, j, half, value, fixed):
             rows_of(after, start)[...] = value
@@ -377,8 +378,9 @@
     ext = pltpu.VMEM((ROWS, 8, LANES), F32)
     message = shape(MESSAGE, LANES)
     full = shape(2 * NB, 8, LANES)
-    lam = shape(NB // STEP, STEP * COMP, LANES)
+    lam = shape(COMP, NB, LANES)
     scratch = [ext, ext, pltpu.VMEM((2 * NB, 8, LANES), F32)]
+    integers = [pltpu.SMEM((INTS,), jnp.int32), pltpu.SemaphoreType.DMA]
     if stage == 0:
         coef = shape(GROUPS, G_LISTED, 8, LANES)
         outs = [full, full, message, message, coef, coef]
@@ -390,9 +392,9 @@
     return pl.pallas_call(
         kernel,
         out_shape=outs,
-        in_specs=[SMEM] * 3 + ins,
+        in_specs=[VMEM] + ins,
         out_specs=[VMEM] * len(outs),
-        scratch_shapes=scratch,
+        scratch_shapes=scratch + integers,
         compiler_params=PARAMS,
     )
 
@@ -441,7 +443,15 @@
         out_specs=VMEM,
         compiler_params=PARAMS,
         name="prep",
-    )(live_count, out_own, jacobian[0], source, face_coef, cell_coef, volume)
+    )(
+        live_count,
+        out_own,
+        jacobian[0].transpose(1, 2, 0, 3),
+        source.transpose(0, 2, 1, 3),
+        face_coef.transpose(1, 0, 2),
+        cell_coef,
+        volume,
+    )
     other = lax.ppermute(mine, "space", swap)
 
     lists_own = jnp.pad(send_blocks[0].reshape(2 * HALO, 1), ((0, NB - 2 * HALO), (0, 0)))
@@ -490,8 +500,8 @@
         name="pluck",
     )(mine, other)
 
-    live = (lax.iota(jnp.int32, NB) < live_count[0]).astype(F32)[:, None, None]
-    start = (live * terminal).reshape(NB // STEP, STEP * COMP, LANES)
+    live = (lax.iota(jnp.int32, NB) < live_count[0]).astype(F32)[None, :, None]
+    start = live * terminal.transpose(1, 0, 2)
     start_other = lax.ppermute(start, "space", swap)
     message = shape(MESSAGE + HALO * RIM, LANES)
     sent = pl.pallas_call(
@@ -528,33 +538,38 @@
         ]
     ).reshape(-1) * 8
 
-    packed, _ = lax.optimization_barrier((packed, got0))
-    packed_next = lax.ppermute(packed, "tm", [(t, t + 1) for t in range(rounds - 1)])
-    listed_next = pl.pallas_call(
-        spread_kernel,
-        out_shape=shape(2 * HALO, TILES, 8, LANES),
-        in_specs=[VMEM] * 2,
-        out_specs=VMEM,
-        compiler_params=PARAMS,
-        name="spread",
-    )(packed_next, listed)
+    ints = jnp.concatenate([table, lists, fixes])
+
+    def following(after):
+        sent, _ = lax.optimization_barrier((packed, after))
+        packed_next = lax.ppermute(sent, "tm", [(t, t + 1) for t in range(rounds - 1)])
+        return pl.pallas_call(
+            spread_kernel,
+            out_shape=shape(2 * HALO, TILES, 8, LANES),
+            in_specs=[VMEM] * 2,
+            out_specs=VMEM,
+            compiler_params=PARAMS,
+            name="spread",
+        )(packed_next, listed)
 
     steps = [make_step(stage) for stage in range(4)]
     flag = (lax.axis_index("tm") == rounds - 1).astype(jnp.int32).reshape(1)
 
-    def slab(moved, last=False):
+    def slab(moved, listed_next=None, last=False):
         x, fixed, msg0, msg1, coef0, coef1 = steps[0](
-            table, lists, fixes, flag, *moved, *begun, rim, listed, mine, other
+            ints, flag, *moved, *begun, rim, listed, mine, other
         )
         got = exchange(msg0, msg1)
+        if listed_next is None and not last:
+            listed_next = following(msg0)
         x, fixed, msg0, msg1, late = steps[1](
-            table, lists, fixes, x, fixed, *got, rim, listed, coef0, coef1
+            ints, x, fixed, *got, rim, listed, coef0, coef1
         )
         got = exchange(msg0, msg1)
         if last:
-            (early,) = steps[3](table, lists, fixes, x, fixed, *got, rim, coef0, coef1)
+            (early,) = steps[3](ints, x, fixed, *got, rim, coef0, coef1)
             return early, late
-        return steps[2](table, lists, fixes, x, fixed, *got, rim, listed_next, coef0, coef1)
+        return *steps[2](ints, x, fixed, *got, rim, listed_next, coef0, coef1), listed_next
 
     def earlier(pairs):
         return [(t * count + d, (t - 1) * count + e) for t in range(1, rounds) for d, e in pairs]
@@ -562,26 +577,23 @@
     both = ("tm", "space")
     same = [(d, d) for d in range(count)]
 
-    def turn(step_index, moved):
-        msg0, msg1, early = slab(moved)
+    def turn(step_index, carry):
+        msg0, msg1, early, listed_next = slab(*carry)
         half = lax.ppermute(early, both, earlier(same))
         got0 = lax.ppermute(msg0, both, earlier(near))
         got1 = lax.ppermute(msg1, both, earlier(far))
         shared = lax.ppermute(half, "space", swap)
-        return (half, shared, got0, got1)
+        return (half, shared, got0, got1), listed_next
 
     moved = (start, start_other, got0[:MESSAGE], got1[:MESSAGE])
-    moved = turn(0, moved)
-    moved = lax.fori_loop(1, rounds - 1, turn, moved)
+    carry = turn(0, (moved, None))
+    moved, _ = lax.fori_loop(1, rounds - 1, turn, carry)
     early, late = slab(moved, last=True)
 
-    def weighed(level, value):
-        value = value.reshape(NB, COMP, LANES)
-        return value, weights[level] * jnp.sum(value * shape_field, axis=(1, 2))
-
-    late, part_late = weighed(1, late)
-    early, part_early = weighed(0, early)
-    fields = jnp.stack([early, late])
+    shapes = shape_field.transpose(1, 0, 2)
+    part_late = weights[1] * jnp.sum(late * shapes, axis=(0, 2))
+    part_early = weights[0] * jnp.sum(early * shapes, axis=(0, 2))
+    fields = jnp.stack([early, late]).transpose(0, 2, 1, 3)
     part = part_late + part_early
     copies = jnp.broadcast_to(part, (rounds, *part.shape))
     sensitivity = lax.all_to_all(copies, "tm", split_axis=0, concat_axis=0, tiled=True).sum(axis=0)

time: 587 us -> 597 us (1.017)
  waiting for transfers between devices: 238 us -> 247 us
    ppermute x17, waiting for transfers between devices: 41.9 us -> 53.3 us  [exchange(): lax.ppermute(second, 'space', far)]
  transfers between devices with their start and end apart: 67 -> 67, of which waited for: 50 -> 49; matrix products, arithmetic and copies ran while one was open for 1% -> 1% of each run, Pallas kernels for 3% -> 1%
where the time goes in v5:
time: 597 us; the launch traced here: 593 us
  waiting for transfers between devices  247 us (41%)
  Pallas kernels  164 us (27%)
  starting transfers between devices  163 us (27%)
  local copies, waits for them, and re-layouts  11.6 us (2%)
    ppermute x7, waiting for transfers between devices, turn(): half = lax.ppermute(early, both, earlier(same))  96.6 us
    ppermute x17, starting transfers between devices, exchange(): lax.ppermute(first, 'space', near)  74.4 us
    pallas_call x8, Pallas kernels, slab(): steps[0](ints, flag, *moved, *begun, rim, listed, mine, other)  58.4 us
    ppermute x17, waiting for transfers between devices, exchange(): lax.ppermute(second, 'space', far)  53.3 us
    pallas_call x8, Pallas kernels, slab(): steps[1](ints, x, fixed, *got, rim, listed, coef0, coef1)  52.6 us
    ppermute x17, waiting for transfers between devices, exchange(): lax.ppermute(first, 'space', near)  45.3 us
    ppermute x7, waiting for transfers between devices, turn(): got0 = lax.ppermute(msg0, both, earlier(near))  41.3 us
    pallas_call x7, Pallas kernels, slab(): steps[2](ints, x, fixed, *got, rim, listed_next, coef0, coef1)  40.9 us
  transfers between devices with their start and end apart: 67, of which 49 were waited for; matrix products, arithmetic and copies ran while one was open for 1% of the time, Pallas kernels for 1%

profile of v5, /device:TPU:113, one launch (start us, length us, event | category | flops | bytes accessed | tf_op | source)
XLA Modules:
  0.0 593.0 jit_solution(13571227236542385065)
XLA Ops:
  12.4 6.3 %collective-permute-done.8 = s32[128,7]{0,1:T(8,128)S(1)} collective-permute-done((s32[128,7]{0,1:T(8,128)S(1)}, s32[128,7]{0,1:T(8,128)S(1)}, u32[]{:S(2)}, u32[]{:S(2)}) %collective-permute-start.8) | collective-permute-done | bytes 3616 | tf_op jit(solution)/shard_map/ppermute | solution.py:459
  40.4 7.1 %shard_map.122 = (f32[256,8,128]{2,1,0:T(8,128)S(1)}, f32[256,8,128]{2,1,0:T(8,128)S(1)}, f32[160,128]{1,0:T(8,128)S(1)}, f32[160,128]{1,0:T(8,128)S(1)}, f32[16...) custom-call(s32[1984]{0:T(1024)} %constant_dynamic-update-slice_fusion.ints, s32[1]{0:T(128)} %bitcast.11.refs_0_, ...), custom_call_target="tpu_custom_call" | custom-call | tf_op jit(solution)/shard_map/pallas_call | solution.py:559
  61.0 7.3 %collective-permute-done.14.refs_3_ = f32[160,128]{1,0:T(8,128)S(1)} collective-permute-done((f32[160,128]{1,0:T(8,128)S(1)}, f32[160,128]{1,0:T(8,128)S(1)}, u32[]{:S(2)}, u32[]{:S(2)}) %collective-permute-start.14) | collective-permute-done | bytes 81952 | tf_op jit(solution)/shard_map/ppermute | solution.py:434
  68.4 6.7 %shard_map.123 = (f32[256,8,128]{2,1,0:T(8,128)S(1)}, f32[256,8,128]{2,1,0:T(8,128)S(1)}, f32[160,128]{1,0:T(8,128)S(1)}, f32[160,128]{1,0:T(8,128)S(1)}, f32[5,128,128]{2,1,0:T(8,128)}) custom-call(s32[1984]{0:T(1024)} %constant_dynamic-update-slice_fusion.ints, f32[256,8,128]{2,1,0:T(8,128)S(1)} %get-tuple-element.136.refs_0_, ...), custom_call_target="tpu_custom_call" | custom-call | tf_op jit(solution)/shard_map/pallas_call | solution.py:565
  75.0 7.2 %collective-permute-start.15 = (f32[160,128]{1,0:T(8,128)S(1)}, f32[160,128]{1,0:T(8,128)S(1)}, u32[]{:S(2)}, u32[]{:S(2)}) collective-permute-start(f32[160,128]{1,0:T(8,128)S(1)} %get-tuple-element.144), channel_id=1, source_target_pairs={{1,2},{2,1},{3,4},{4,3},{5,6},{6,5},{7,8},{8,7},{9,10},{10,9},{11,... | collective-permute-start | bytes 245768 | tf_op jit(solution)/shard_map/ppermute | solution.py:434
  97.0 10.1 %collective-permute-done.18 = f32[5,128,128]{2,1,0:T(8,128)} collective-permute-done((f32[5,128,128]{2,1,0:T(8,128)S(1)}, f32[5,128,128]{2,1,0:T(8,128)}, u32[]{:S(2)}, u32[]{:S(2)}) %collective-permute-start.18) | collective-permute-done | bytes 327712 | tf_op jit(solution)/shard_map/ppermute | solution.py:582
  116.4 414.1 %while.16 = (s32[]{:T(128)}, f32[5,128,128]{2,1,0:T(8,128)}, f32[5,128,128]{2,1,0:T(8,128)}, f32[160,128]{1,0:T(8,128)}, f32[160,128]{1,0:T(8,128)}, /*index=5*/...) while((s32[]{:T(128)}, f32[5,128,128]{2,1,0:T(8,128)}, ...), condition=%wide.region_7.8_spmd, body=%wide.region_6.7_spmd.sunk | while | flops 2 | bytes 4587997 | solution.py:590
  116.4 7.3 %eval_jaxpr.3 = (f32[256,8,128]{2,1,0:T(8,128)S(1)}, f32[256,8,128]{2,1,0:T(8,128)S(1)}, f32[160,128]{1,0:T(8,128)S(1)}, f32[160,128]{1,0:T(8,128)S(1)}, f32[16,...) custom-call(s32[1984]{0:T(1024)} %get-tuple-element.379.ints, s32[1]{0:T(128)} %get-tuple-element.380.refs_0_, ...), custom_call_target="tpu_custom_call" | custom-call | tf_op jit(solution)/shard_map/while/body/eval_jaxpr/pallas_call | solution.py:559
  134.9 6.7 %eval_jaxpr.4 = (f32[256,8,128]{2,1,0:T(8,128)S(1)}, f32[256,8,128]{2,1,0:T(8,128)S(1)}, f32[160,128]{1,0:T(8,128)S(1)}, f32[160,128]{1,0:T(8,128)S(1)}, f32[5,128,128]{2,1,0:T(8,128)}) custom-call(s32[1984]{0:T(1024)} %get-tuple-element.379.ints, f32[256,8,128]{2,1,0:T(8,128)S(1)} %get-tuple-element.327.refs_0_, ...), custom_call_target="tpu_custom_call" | custom-call | tf_op jit(solution)/shard_map/while/body/eval_jaxpr/pallas_call | solution.py:565
  141.5 6.2 %collective-permute-start.2 = (f32[160,128]{1,0:T(8,128)S(1)}, f32[160,128]{1,0:T(8,128)S(1)}, u32[]{:S(2)}, u32[]{:S(2)}) collective-permute-start(f32[160,128]{1,0:T(8,128)S(1)} %get-tuple-element.335), channel_id=1, source_target_pairs={{1,2},{2,1},{3,4},{4,3},{5,6},{6,5},{7,8},{8,7},{9,10},{10,9},{11,... | collective-permute-start | bytes 245768 | tf_op jit(solution)/shard_map/while/body/eval_jaxpr/ppermute | solution.py:434
  163.0 12.9 %collective-permute-done.4 = f32[5,128,128]{2,1,0:T(8,128)} collective-permute-done((f32[5,128,128]{2,1,0:T(8,128)S(1)}, f32[5,128,128]{2,1,0:T(8,128)}, u32[]{:S(2)}, u32[]{:S(2)}) %collective-permute-start.4) | collective-permute-done | bytes 327712 | tf_op jit(solution)/shard_map/while/body/eval_jaxpr/ppermute | solution.py:582
  184.8 7.3 %eval_jaxpr.3 = (f32[256,8,128]{2,1,0:T(8,128)S(1)}, f32[256,8,128]{2,1,0:T(8,128)S(1)}, f32[160,128]{1,0:T(8,128)S(1)}, f32[160,128]{1,0:T(8,128)S(1)}, f32[16,...) custom-call(s32[1984]{0:T(1024)} %get-tuple-element.379.ints, s32[1]{0:T(128)} %get-tuple-element.380.refs_0_, ...), custom_call_target="tpu_custom_call" | custom-call | tf_op jit(solution)/shard_map/while/body/eval_jaxpr/pallas_call | solution.py:559
  204.4 6.7 %eval_jaxpr.4 = (f32[256,8,128]{2,1,0:T(8,128)S(1)}, f32[256,8,128]{2,1,0:T(8,128)S(1)}, f32[160,128]{1,0:T(8,128)S(1)}, f32[160,128]{1,0:T(8,128)S(1)}, f32[5,128,128]{2,1,0:T(8,128)}) custom-call(s32[1984]{0:T(1024)} %get-tuple-element.379.ints, f32[256,8,128]{2,1,0:T(8,128)S(1)} %get-tuple-element.327.refs_0_, ...), custom_call_target="tpu_custom_call" | custom-call | tf_op jit(solution)/shard_map/while/body/eval_jaxpr/pallas_call | solution.py:565
  229.7 14.8 %collective-permute-done.4 = f32[5,128,128]{2,1,0:T(8,128)} collective-permute-done((f32[5,128,128]{2,1,0:T(8,128)S(1)}, f32[5,128,128]{2,1,0:T(8,128)}, u32[]{:S(2)}, u32[]{:S(2)}) %collective-permute-start.4) | collective-permute-done | bytes 327712 | tf_op jit(solution)/shard_map/while/body/eval_jaxpr/ppermute | solution.py:582
  248.1 5.9 %collective-permute-done.6 = f32[160,128]{1,0:T(8,128)} collective-permute-done((f32[160,128]{1,0:T(8,128)S(1)}, f32[160,128]{1,0:T(8,128)}, u32[]{:S(2)}, u32[]{:S(2)}) %collective-permute-start.6) | collective-permute-done | bytes 81952 | tf_op jit(solution)/shard_map/while/body/eval_jaxpr/ppermute | solution.py:583
  254.0 7.3 %eval_jaxpr.3 = (f32[256,8,128]{2,1,0:T(8,128)S(1)}, f32[256,8,128]{2,1,0:T(8,128)S(1)}, f32[160,128]{1,0:T(8,128)S(1)}, f32[160,128]{1,0:T(8,128)S(1)}, f32[16,...) custom-call(s32[1984]{0:T(1024)} %get-tuple-element.379.ints, s32[1]{0:T(128)} %get-tuple-element.380.refs_0_, ...), custom_call_target="tpu_custom_call" | custom-call | tf_op jit(solution)/shard_map/while/body/eval_jaxpr/pallas_call | solution.py:559
  273.5 6.7 %eval_jaxpr.4 = (f32[256,8,128]{2,1,0:T(8,128)S(1)}, f32[256,8,128]{2,1,0:T(8,128)S(1)}, f32[160,128]{1,0:T(8,128)S(1)}, f32[160,128]{1,0:T(8,128)S(1)}, f32[5,128,128]{2,1,0:T(8,128)}) custom-call(s32[1984]{0:T(1024)} %get-tuple-element.379.ints, f32[256,8,128]{2,1,0:T(8,128)S(1)} %get-tuple-element.327.refs_0_, ...), custom_call_target="tpu_custom_call" | custom-call | tf_op jit(solution)/shard_map/while/body/eval_jaxpr/pallas_call | solution.py:565
  298.9 14.7 %collective-permute-done.4 = f32[5,128,128]{2,1,0:T(8,128)} collective-permute-done((f32[5,128,128]{2,1,0:T(8,128)S(1)}, f32[5,128,128]{2,1,0:T(8,128)}, u32[]{:S(2)}, u32[]{:S(2)}) %collective-permute-start.4) | collective-permute-done | bytes 327712 | tf_op jit(solution)/shard_map/while/body/eval_jaxpr/ppermute | solution.py:582
  317.2 5.9 %collective-permute-done.6 = f32[160,128]{1,0:T(8,128)} collective-permute-done((f32[160,128]{1,0:T(8,128)S(1)}, f32[160,128]{1,0:T(8,128)}, u32[]{:S(2)}, u32[]{:S(2)}) %collective-permute-start.6) | collective-permute-done | bytes 81952 | tf_op jit(solution)/shard_map/while/body/eval_jaxpr/ppermute | solution.py:583
  323.1 7.3 %eval_jaxpr.3 = (f32[256,8,128]{2,1,0:T(8,128)S(1)}, f32[256,8,128]{2,1,0:T(8,128)S(1)}, f32[160,128]{1,0:T(8,128)S(1)}, f32[160,128]{1,0:T(8,128)S(1)}, f32[16,...) custom-call(s32[1984]{0:T(1024)} %get-tuple-element.379.ints, s32[1]{0:T(128)} %get-tuple-element.380.refs_0_, ...), custom_call_target="tpu_custom_call" | custom-call | tf_op jit(solution)/shard_map/while/body/eval_jaxpr/pallas_call | solution.py:559
  342.6 6.7 %eval_jaxpr.4 = (f32[256,8,128]{2,1,0:T(8,128)S(1)}, f32[256,8,128]{2,1,0:T(8,128)S(1)}, f32[160,128]{1,0:T(8,128)S(1)}, f32[160,128]{1,0:T(8,128)S(1)}, f32[5,128,128]{2,1,0:T(8,128)}) custom-call(s32[1984]{0:T(1024)} %get-tuple-element.379.ints, f32[256,8,128]{2,1,0:T(8,128)S(1)} %get-tuple-element.327.refs_0_, ...), custom_call_target="tpu_custom_call" | custom-call | tf_op jit(solution)/shard_map/while/body/eval_jaxpr/pallas_call | solution.py:565
  368.0 14.7 %collective-permute-done.4 = f32[5,128,128]{2,1,0:T(8,128)} collective-permute-done((f32[5,128,128]{2,1,0:T(8,128)S(1)}, f32[5,128,128]{2,1,0:T(8,128)}, u32[]{:S(2)}, u32[]{:S(2)}) %collective-permute-start.4) | collective-permute-done | bytes 327712 | tf_op jit(solution)/shard_map/while/body/eval_jaxpr/ppermute | solution.py:582
  386.3 5.9 %collective-permute-done.6 = f32[160,128]{1,0:T(8,128)} collective-permute-done((f32[160,128]{1,0:T(8,128)S(1)}, f32[160,128]{1,0:T(8,128)}, u32[]{:S(2)}, u32[]{:S(2)}) %collective-permute-start.6) | collective-permute-done | bytes 81952 | tf_op jit(solution)/shard_map/while/body/eval_jaxpr/ppermute | solution.py:583
  392.3 7.3 %eval_jaxpr.3 = (f32[256,8,128]{2,1,0:T(8,128)S(1)}, f32[256,8,128]{2,1,0:T(8,128)S(1)}, f32[160,128]{1,0:T(8,128)S(1)}, f32[160,128]{1,0:T(8,128)S(1)}, f32[16,...) custom-call(s32[1984]{0:T(1024)} %get-tuple-element.379.ints, s32[1]{0:T(128)} %get-tuple-element.380.refs_0_, ...), custom_call_target="tpu_custom_call" | custom-call | tf_op jit(solution)/shard_map/while/body/eval_jaxpr/pallas_call | solution.py:559
  411.8 6.7 %eval_jaxpr.4 = (f32[256,8,128]{2,1,0:T(8,128)S(1)}, f32[256,8,128]{2,1,0:T(8,128)S(1)}, f32[160,128]{1,0:T(8,128)S(1)}, f32[160,128]{1,0:T(8,128)S(1)}, f32[5,128,128]{2,1,0:T(8,128)}) custom-call(s32[1984]{0:T(1024)} %get-tuple-element.379.ints, f32[256,8,128]{2,1,0:T(8,128)S(1)} %get-tuple-element.327.refs_0_, ...), custom_call_target="tpu_custom_call" | custom-call | tf_op jit(solution)/shard_map/while/body/eval_jaxpr/pallas_call | solution.py:565
  437.1 14.7 %collective-permute-done.4 = f32[5,128,128]{2,1,0:T(8,128)} collective-permute-done((f32[5,128,128]{2,1,0:T(8,128)S(1)}, f32[5,128,128]{2,1,0:T(8,128)}, u32[]{:S(2)}, u32[]{:S(2)}) %collective-permute-start.4) | collective-permute-done | bytes 327712 | tf_op jit(solution)/shard_map/while/body/eval_jaxpr/ppermute | solution.py:582
  461.4 7.3 %eval_jaxpr.3 = (f32[256,8,128]{2,1,0:T(8,128)S(1)}, f32[256,8,128]{2,1,0:T(8,128)S(1)}, f32[160,128]{1,0:T(8,128)S(1)}, f32[160,128]{1,0:T(8,128)S(1)}, f32[16,...) custom-call(s32[1984]{0:T(1024)} %get-tuple-element.379.ints, s32[1]{0:T(128)} %get-tuple-element.380.refs_0_, ...), custom_call_target="tpu_custom_call" | custom-call | tf_op jit(solution)/shard_map/while/body/eval_jaxpr/pallas_call | solution.py:559
  480.9 6.7 %eval_jaxpr.4 = (f32[256,8,128]{2,1,0:T(8,128)S(1)}, f32[256,8,128]{2,1,0:T(8,128)S(1)}, f32[160,128]{1,0:T(8,128)S(1)}, f32[160,128]{1,0:T(8,128)S(1)}, f32[5,128,128]{2,1,0:T(8,128)}) custom-call(s32[1984]{0:T(1024)} %get-tuple-element.379.ints, f32[256,8,128]{2,1,0:T(8,128)S(1)} %get-tuple-element.327.refs_0_, ...), custom_call_target="tpu_custom_call" | custom-call | tf_op jit(solution)/shard_map/while/body/eval_jaxpr/pallas_call | solution.py:565
  506.3 14.7 %collective-permute-done.4 = f32[5,128,128]{2,1,0:T(8,128)} collective-permute-done((f32[5,128,128]{2,1,0:T(8,128)S(1)}, f32[5,128,128]{2,1,0:T(8,128)}, u32[]{:S(2)}, u32[]{:S(2)}) %collective-permute-start.4) | collective-permute-done | bytes 327712 | tf_op jit(solution)/shard_map/while/body/eval_jaxpr/ppermute | solution.py:582
  530.5 7.3 %shard_map.125 = (f32[256,8,128]{2,1,0:T(8,128)S(1)}, f32[256,8,128]{2,1,0:T(8,128)S(1)}, f32[160,128]{1,0:T(8,128)S(1)}, f32[160,128]{1,0:T(8,128)S(1)}, f32[16...) custom-call(s32[1984]{0:T(1024)} %constant_dynamic-update-slice_fusion.ints, s32[1]{0:T(128)} %bitcast.11.refs_0_, ...), custom_call_target="tpu_custom_call" | custom-call | tf_op jit(solution)/shard_map/pallas_call | solution.py:559
  550.0 6.0 %shard_map.126 = (f32[256,8,128]{2,1,0:T(8,128)S(1)}, f32[256,8,128]{2,1,0:T(8,128)S(1)}, f32[160,128]{1,0:T(8,128)S(1)}, f32[160,128]{1,0:T(8,128)S(1)}, f32[5,128,128]{2,1,0:T(8,128)S(1)}) custom-call(s32[1984]{0:T(1024)} %constant_dynamic-update-slice_fusion.ints, f32[256,8,128]{2,1,0:T(8,128)S(1)} %get-tuple-element.155.refs_0_, ...), custom_call_target="tpu_custom_call" | custom-call | tf_op jit(solution)/shard_map/pallas_call | solution.py:565
  574.8 12.6 %all-to-all-start = ((f32[8,1,128]{2,1,0:T(1,128)}), f32[8,1,128]{2,1,0:T(1,128)S(1)}, u32[]{:S(2)}, u32[]{:S(2)}) async-start(f32[8,1,128]{2,1,0:T(1,128)} %broadcast_in_dim.103), calls=%async_computation | async-start | bytes 8192 | tf_op jit(solution)/shard_map/all_to_all | solution.py:599
  (207 shorter events, 325.7 us)
Async XLA Ops:
  10.9 9.4 %collective-permute-start.10 = (f32[16,65,8,128]{3,2,1,0:T(8,128)}, f32[16,65,8,128]{3,2,1,0:T(8,128)}, u32[]{:S(2)}, u32[]{:S(2)}) collective-permute-start(f32[16,65,8,128]{3,2,1,0:T(8,128)} %prep.1.mine.refs_11_), channel_id=1, source_target_pairs={{0,1},{1,0},{2,3},{3,2},{4,5},{5,4},{6,7},{7,6},{8,9},{9,8},{10,11... | collective-permute-start | bytes 12779528 | tf_op jit(solution)/shard_map/ppermute | solution.py:455
  11.9 9.9 %collective-permute-start.9 = (f32[5,128,128]{2,1,0:T(8,128)S(1)}, f32[5,128,128]{2,1,0:T(8,128)}, u32[]{:S(2)}, u32[]{:S(2)}) collective-permute-start(f32[5,128,128]{2,1,0:T(8,128)S(1)} %multiply_bitcast_fusion.mine.refs_1_.refs_5_), channel_id=1, source_target_pairs={{0,1},{1,0},{2,3},{3,2},{4,5},{5,4},{6,7},{7,6},{8,9},{9,8},{10,11... | collective-permute-start | bytes 983048 | tf_op jit(solution)/shard_map/ppermute | solution.py:505
  23.3 10.4 %collective-permute-start.11 = (f32[352,128]{1,0:T(8,128)S(1)}, f32[352,128]{1,0:T(8,128)S(1)}, u32[]{:S(2)}, u32[]{:S(2)}) collective-permute-start(f32[352,128]{1,0:T(8,128)S(1)} %get-tuple-element.132), channel_id=1, source_target_pairs={{1,2},{2,1},{3,4},{4,3},{5,6},{6,5},{7,8},{8,7},{9,10},{10,9},{11,... | collective-permute-start | bytes 540680 | tf_op jit(solution)/shard_map/ppermute | solution.py:434
  28.1 9.6 %collective-permute-start.12 = (f32[352,128]{1,0:T(8,128)S(1)}, f32[352,128]{1,0:T(8,128)S(1)}, u32[]{:S(2)}, u32[]{:S(2)}) collective-permute-start(f32[352,128]{1,0:T(8,128)S(1)} %get-tuple-element.133), channel_id=1, source_target_pairs={{0,3},{2,5},{3,0},{4,7},{5,2},{6,9},{7,4},{8,11},{9,6},{10,13},{11... | collective-permute-start | bytes 540680 | tf_op jit(solution)/shard_map/ppermute | solution.py:434
  47.6 36.6 %collective-permute-start.17 = (f32[32,40,128]{2,1,0:T(8,128)S(1)}, f32[32,40,128]{2,1,0:T(8,128)S(1)}, u32[]{:S(2)}, u32[]{:S(2)}) collective-permute-start(f32[32,40,128]{2,1,0:T(8,128)S(1)} %get-tuple-element.147), channel_id=1, source_target_pairs={{0,32},{32,64},{64,96},{96,128},{128,160},{160,192},{192,224},{1,3... | collective-permute-start | bytes 1966088 | tf_op jit(solution)/shard_map/ppermute | solution.py:545
  51.0 10.0 %collective-permute-start.13 = (f32[160,128]{1,0:T(8,128)S(1)}, f32[160,128]{1,0:T(8,128)S(1)}, u32[]{:S(2)}, u32[]{:S(2)}) collective-permute-start(f32[160,128]{1,0:T(8,128)S(1)} %get-tuple-element.138), channel_id=1, source_target_pairs={{1,2},{2,1},{3,4},{4,3},{5,6},{6,5},{7,8},{8,7},{9,10},{10,9},{11,... | collective-permute-start | bytes 245768 | tf_op jit(solution)/shard_map/ppermute | solution.py:434
  53.9 14.4 %collective-permute-start.14 = (f32[160,128]{1,0:T(8,128)S(1)}, f32[160,128]{1,0:T(8,128)S(1)}, u32[]{:S(2)}, u32[]{:S(2)}) collective-permute-start(f32[160,128]{1,0:T(8,128)S(1)} %get-tuple-element.139), channel_id=1, source_target_pairs={{0,3},{2,5},{3,0},{4,7},{5,2},{6,9},{7,4},{8,11},{9,6},{10,13},{11... | collective-permute-start | bytes 245768 | tf_op jit(solution)/shard_map/ppermute | solution.py:434
  75.0 9.4 %collective-permute-start.15 = (f32[160,128]{1,0:T(8,128)S(1)}, f32[160,128]{1,0:T(8,128)S(1)}, u32[]{:S(2)}, u32[]{:S(2)}) collective-permute-start(f32[160,128]{1,0:T(8,128)S(1)} %get-tuple-element.144), channel_id=1, source_target_pairs={{1,2},{2,1},{3,4},{4,3},{5,6},{6,5},{7,8},{8,7},{9,10},{10,9},{11,... | collective-permute-start | bytes 245768 | tf_op jit(solution)/shard_map/ppermute | solution.py:434
  95.7 11.4 %collective-permute-start.18 = (f32[5,128,128]{2,1,0:T(8,128)S(1)}, f32[5,128,128]{2,1,0:T(8,128)}, u32[]{:S(2)}, u32[]{:S(2)}) collective-permute-start(f32[5,128,128]{2,1,0:T(8,128)S(1)} %get-tuple-element.148), channel_id=1, source_target_pairs={{32,0},{33,1},{34,2},{35,3},{36,4},{37,5},{38,6},{39,7},{40,8},{41... | collective-permute-start | bytes 983048 | tf_op jit(solution)/shard_map/ppermute | solution.py:582
  123.7 9.4 %collective-permute-start = (f32[160,128]{1,0:T(8,128)S(1)}, f32[160,128]{1,0:T(8,128)S(1)}, u32[]{:S(2)}, u32[]{:S(2)}) collective-permute-start(f32[160,128]{1,0:T(8,128)S(1)} %get-tuple-element.329), channel_id=1, source_target_pairs={{1,2},{2,1},{3,4},{4,3},{5,6},{6,5},{7,8},{8,7},{9,10},{10,9},{11,... | collective-permute-start | bytes 245768 | tf_op jit(solution)/shard_map/while/body/eval_jaxpr/ppermute | solution.py:434
  141.5 9.4 %collective-permute-start.2 = (f32[160,128]{1,0:T(8,128)S(1)}, f32[160,128]{1,0:T(8,128)S(1)}, u32[]{:S(2)}, u32[]{:S(2)}) collective-permute-start(f32[160,128]{1,0:T(8,128)S(1)} %get-tuple-element.335), channel_id=1, source_target_pairs={{1,2},{2,1},{3,4},{4,3},{5,6},{6,5},{7,8},{8,7},{9,10},{10,9},{11,... | collective-permute-start | bytes 245768 | tf_op jit(solution)/shard_map/while/body/eval_jaxpr/ppermute | solution.py:434
  161.7 14.2 %collective-permute-start.4 = (f32[5,128,128]{2,1,0:T(8,128)S(1)}, f32[5,128,128]{2,1,0:T(8,128)}, u32[]{:S(2)}, u32[]{:S(2)}) collective-permute-start(f32[5,128,128]{2,1,0:T(8,128)S(1)} %get-tuple-element.337), channel_id=1, source_target_pairs={{32,0},{33,1},{34,2},{35,3},{36,4},{37,5},{38,6},{39,7},{40,8},{41... | collective-permute-start | bytes 983048 | tf_op jit(solution)/shard_map/while/body/eval_jaxpr/ppermute | solution.py:582
  192.1 9.4 %collective-permute-start = (f32[160,128]{1,0:T(8,128)S(1)}, f32[160,128]{1,0:T(8,128)S(1)}, u32[]{:S(2)}, u32[]{:S(2)}) collective-permute-start(f32[160,128]{1,0:T(8,128)S(1)} %get-tuple-element.329), channel_id=1, source_target_pairs={{1,2},{2,1},{3,4},{4,3},{5,6},{6,5},{7,8},{8,7},{9,10},{10,9},{11,... | collective-permute-start | bytes 245768 | tf_op jit(solution)/shard_map/while/body/eval_jaxpr/ppermute | solution.py:434
  211.0 9.4 %collective-permute-start.2 = (f32[160,128]{1,0:T(8,128)S(1)}, f32[160,128]{1,0:T(8,128)S(1)}, u32[]{:S(2)}, u32[]{:S(2)}) collective-permute-start(f32[160,128]{1,0:T(8,128)S(1)} %get-tuple-element.335), channel_id=1, source_target_pairs={{1,2},{2,1},{3,4},{4,3},{5,6},{6,5},{7,8},{8,7},{9,10},{10,9},{11,... | collective-permute-start | bytes 245768 | tf_op jit(solution)/shard_map/while/body/eval_jaxpr/ppermute | solution.py:434
  228.4 16.1 %collective-permute-start.4 = (f32[5,128,128]{2,1,0:T(8,128)S(1)}, f32[5,128,128]{2,1,0:T(8,128)}, u32[]{:S(2)}, u32[]{:S(2)}) collective-permute-start(f32[5,128,128]{2,1,0:T(8,128)S(1)} %get-tuple-element.337), channel_id=1, source_target_pairs={{32,0},{33,1},{34,2},{35,3},{36,4},{37,5},{38,6},{39,7},{40,8},{41... | collective-permute-start | bytes 983048 | tf_op jit(solution)/shard_map/while/body/eval_jaxpr/ppermute | solution.py:582
  244.4 9.5 %collective-permute-start.5 = (f32[5,128,128]{2,1,0:T(8,128)}, f32[5,128,128]{2,1,0:T(8,128)}, u32[]{:S(2)}, u32[]{:S(2)}) collective-permute-start(f32[5,128,128]{2,1,0:T(8,128)} %collective-permute-done.4), channel_id=1, source_target_pairs={{0,1},{1,0},{2,3},{3,2},{4,5},{5,4},{6,7},{7,6},{8,9},{9,8},{10,11... | collective-permute-start | bytes 983048 | tf_op jit(solution)/shard_map/while/body/eval_jaxpr/ppermute | solution.py:585
  261.3 9.4 %collective-permute-start = (f32[160,128]{1,0:T(8,128)S(1)}, f32[160,128]{1,0:T(8,128)S(1)}, u32[]{:S(2)}, u32[]{:S(2)}) collective-permute-start(f32[160,128]{1,0:T(8,128)S(1)} %get-tuple-element.329), channel_id=1, source_target_pairs={{1,2},{2,1},{3,4},{4,3},{5,6},{6,5},{7,8},{8,7},{9,10},{10,9},{11,... | collective-permute-start | bytes 245768 | tf_op jit(solution)/shard_map/while/body/eval_jaxpr/ppermute | solution.py:434
  280.2 9.4 %collective-permute-start.2 = (f32[160,128]{1,0:T(8,128)S(1)}, f32[160,128]{1,0:T(8,128)S(1)}, u32[]{:S(2)}, u32[]{:S(2)}) collective-permute-start(f32[160,128]{1,0:T(8,128)S(1)} %get-tuple-element.335), channel_id=1, source_target_pairs={{1,2},{2,1},{3,4},{4,3},{5,6},{6,5},{7,8},{8,7},{9,10},{10,9},{11,... | collective-permute-start | bytes 245768 | tf_op jit(solution)/shard_map/while/body/eval_jaxpr/ppermute | solution.py:434
  297.6 16.0 %collective-permute-start.4 = (f32[5,128,128]{2,1,0:T(8,128)S(1)}, f32[5,128,128]{2,1,0:T(8,128)}, u32[]{:S(2)}, u32[]{:S(2)}) collective-permute-start(f32[5,128,128]{2,1,0:T(8,128)S(1)} %get-tuple-element.337), channel_id=1, source_target_pairs={{32,0},{33,1},{34,2},{35,3},{36,4},{37,5},{38,6},{39,7},{40,8},{41... | collective-permute-start | bytes 983048 | tf_op jit(solution)/shard_map/while/body/eval_jaxpr/ppermute | solution.py:582
  313.6 9.5 %collective-permute-start.5 = (f32[5,128,128]{2,1,0:T(8,128)}, f32[5,128,128]{2,1,0:T(8,128)}, u32[]{:S(2)}, u32[]{:S(2)}) collective-permute-start(f32[5,128,128]{2,1,0:T(8,128)} %collective-permute-done.4), channel_id=1, source_target_pairs={{0,1},{1,0},{2,3},{3,2},{4,5},{5,4},{6,7},{7,6},{8,9},{9,8},{10,11... | collective-permute-start | bytes 983048 | tf_op jit(solution)/shard_map/while/body/eval_jaxpr/ppermute | solution.py:585
  330.5 9.4 %collective-permute-start = (f32[160,128]{1,0:T(8,128)S(1)}, f32[160,128]{1,0:T(8,128)S(1)}, u32[]{:S(2)}, u32[]{:S(2)}) collective-permute-start(f32[160,128]{1,0:T(8,128)S(1)} %get-tuple-element.329), channel_id=1, source_target_pairs={{1,2},{2,1},{3,4},{4,3},{5,6},{6,5},{7,8},{8,7},{9,10},{10,9},{11,... | collective-permute-start | bytes 245768 | tf_op jit(solution)/shard_map/while/body/eval_jaxpr/ppermute | solution.py:434
  349.3 9.4 %collective-permute-start.2 = (f32[160,128]{1,0:T(8,128)S(1)}, f32[160,128]{1,0:T(8,128)S(1)}, u32[]{:S(2)}, u32[]{:S(2)}) collective-permute-start(f32[160,128]{1,0:T(8,128)S(1)} %get-tuple-element.335), channel_id=1, source_target_pairs={{1,2},{2,1},{3,4},{4,3},{5,6},{6,5},{7,8},{8,7},{9,10},{10,9},{11,... | collective-permute-start | bytes 245768 | tf_op jit(solution)/shard_map/while/body/eval_jaxpr/ppermute | solution.py:434
  366.7 16.0 %collective-permute-start.4 = (f32[5,128,128]{2,1,0:T(8,128)S(1)}, f32[5,128,128]{2,1,0:T(8,128)}, u32[]{:S(2)}, u32[]{:S(2)}) collective-permute-start(f32[5,128,128]{2,1,0:T(8,128)S(1)} %get-tuple-element.337), channel_id=1, source_target_pairs={{32,0},{33,1},{34,2},{35,3},{36,4},{37,5},{38,6},{39,7},{40,8},{41... | collective-permute-start | bytes 983048 | tf_op jit(solution)/shard_map/while/body/eval_jaxpr/ppermute | solution.py:582
  382.7 9.5 %collective-permute-start.5 = (f32[5,128,128]{2,1,0:T(8,128)}, f32[5,128,128]{2,1,0:T(8,128)}, u32[]{:S(2)}, u32[]{:S(2)}) collective-permute-start(f32[5,128,128]{2,1,0:T(8,128)} %collective-permute-done.4), channel_id=1, source_target_pairs={{0,1},{1,0},{2,3},{3,2},{4,5},{5,4},{6,7},{7,6},{8,9},{9,8},{10,11... | collective-permute-start | bytes 983048 | tf_op jit(solution)/shard_map/while/body/eval_jaxpr/ppermute | solution.py:585
  399.6 9.4 %collective-permute-start = (f32[160,128]{1,0:T(8,128)S(1)}, f32[160,128]{1,0:T(8,128)S(1)}, u32[]{:S(2)}, u32[]{:S(2)}) collective-permute-start(f32[160,128]{1,0:T(8,128)S(1)} %get-tuple-element.329), channel_id=1, source_target_pairs={{1,2},{2,1},{3,4},{4,3},{5,6},{6,5},{7,8},{8,7},{9,10},{10,9},{11,... | collective-permute-start | bytes 245768 | tf_op jit(solution)/shard_map/while/body/eval_jaxpr/ppermute | solution.py:434
  418.4 9.4 %collective-permute-start.2 = (f32[160,128]{1,0:T(8,128)S(1)}, f32[160,128]{1,0:T(8,128)S(1)}, u32[]{:S(2)}, u32[]{:S(2)}) collective-permute-start(f32[160,128]{1,0:T(8,128)S(1)} %get-tuple-element.335), channel_id=1, source_target_pairs={{1,2},{2,1},{3,4},{4,3},{5,6},{6,5},{7,8},{8,7},{9,10},{10,9},{11,... | collective-permute-start | bytes 245768 | tf_op jit(solution)/shard_map/while/body/eval_jaxpr/ppermute | solution.py:434
  435.8 16.0 %collective-permute-start.4 = (f32[5,128,128]{2,1,0:T(8,128)S(1)}, f32[5,128,128]{2,1,0:T(8,128)}, u32[]{:S(2)}, u32[]{:S(2)}) collective-permute-start(f32[5,128,128]{2,1,0:T(8,128)S(1)} %get-tuple-element.337), channel_id=1, source_target_pairs={{32,0},{33,1},{34,2},{35,3},{36,4},{37,5},{38,6},{39,7},{40,8},{41... | collective-permute-start | bytes 983048 | tf_op jit(solution)/shard_map/while/body/eval_jaxpr/ppermute | solution.py:582
  451.8 9.5 %collective-permute-start.5 = (f32[5,128,128]{2,1,0:T(8,128)}, f32[5,128,128]{2,1,0:T(8,128)}, u32[]{:S(2)}, u32[]{:S(2)}) collective-permute-start(f32[5,128,128]{2,1,0:T(8,128)} %collective-permute-done.4), channel_id=1, source_target_pairs={{0,1},{1,0},{2,3},{3,2},{4,5},{5,4},{6,7},{7,6},{8,9},{9,8},{10,11... | collective-permute-start | bytes 983048 | tf_op jit(solution)/shard_map/while/body/eval_jaxpr/ppermute | solution.py:585
  468.7 9.4 %collective-permute-start = (f32[160,128]{1,0:T(8,128)S(1)}, f32[160,128]{1,0:T(8,128)S(1)}, u32[]{:S(2)}, u32[]{:S(2)}) collective-permute-start(f32[160,128]{1,0:T(8,128)S(1)} %get-tuple-element.329), channel_id=1, source_target_pairs={{1,2},{2,1},{3,4},{4,3},{5,6},{6,5},{7,8},{8,7},{9,10},{10,9},{11,... | collective-permute-start | bytes 245768 | tf_op jit(solution)/shard_map/while/body/eval_jaxpr/ppermute | solution.py:434
  505.0 16.0 %collective-permute-start.4 = (f32[5,128,128]{2,1,0:T(8,128)S(1)}, f32[5,128,128]{2,1,0:T(8,128)}, u32[]{:S(2)}, u32[]{:S(2)}) collective-permute-start(f32[5,128,128]{2,1,0:T(8,128)S(1)} %get-tuple-element.337), channel_id=1, source_target_pairs={{32,0},{33,1},{34,2},{35,3},{36,4},{37,5},{38,6},{39,7},{40,8},{41... | collective-permute-start | bytes 983048 | tf_op jit(solution)/shard_map/while/body/eval_jaxpr/ppermute | solution.py:582
  521.0 9.5 %collective-permute-start.5 = (f32[5,128,128]{2,1,0:T(8,128)}, f32[5,128,128]{2,1,0:T(8,128)}, u32[]{:S(2)}, u32[]{:S(2)}) collective-permute-start(f32[5,128,128]{2,1,0:T(8,128)} %collective-permute-done.4), channel_id=1, source_target_pairs={{0,1},{1,0},{2,3},{3,2},{4,5},{5,4},{6,7},{7,6},{8,9},{9,8},{10,11... | collective-permute-start | bytes 983048 | tf_op jit(solution)/shard_map/while/body/eval_jaxpr/ppermute | solution.py:585
  574.8 17.7 %all-to-all-start = ((f32[8,1,128]{2,1,0:T(1,128)}), f32[8,1,128]{2,1,0:T(1,128)S(1)}, u32[]{:S(2)}, u32[]{:S(2)}) async-start(f32[8,1,128]{2,1,0:T(1,128)} %broadcast_in_dim.103), calls=%async_computation | async-start | bytes 8192 | tf_op jit(solution)/shard_map/all_to_all | solution.py:599
  (46 other events, 338.8 us)

commit v6 on v5

--- a/solution.py
+++ b/solution.py
@@ -14,9 +14,7 @@
 STEP = 8
 UNROLL = 2
 CHUNKS = 4
-TABLE = 2 * NB * NEI
 WIDE = 8
-INTS = TABLE + 2 * HALO * (WIDE + NEI)
 MESSAGE = 2 * HALO * COMP
 RIM = COMP + NEI + 1
 ZERO = 2 * NB + 2 * HALO
@@ -120,7 +118,7 @@
             for s in range(STEP):
                 terms = []
                 for k in range(NEI):
-                    picked = at_row(ext, table.at[pl.ds(s * NEI + k, TABLE - STEP * NEI + 1)][row])
+                    picked = at_row(ext, table.at[pl.ds(s * NEI + k, 2 * NB * NEI - STEP * NEI + 1)][row])
                     terms.append(coef[g, G_FACE + s, k : k + 1] * picked)
                 total = ((terms[0] + terms[1]) + (terms[2] + terms[3])) + (terms[4] + terms[5])
                 sums[(half * GROUPS + g) * STEP + s] = total
@@ -267,12 +265,8 @@
 
 
 def make_step(stage):
-    def kernel(ints, *refs):
-        *refs, table, arrived = refs
-        fetch = pltpu.make_async_copy(ints, table, arrived)
-        fetch.start()
-        lists = table.at[pl.ds(TABLE, 2 * HALO * WIDE)]
-        fixes = table.at[pl.ds(TABLE + 2 * HALO * WIDE, 2 * HALO * NEI)]
+    def kernel(table, lists, fixes, *refs):
+        refs = list(refs)
 
         def take(n):
             head = refs[:n]
@@ -330,7 +324,6 @@
 
             lax.fori_loop(0, 2 * NB // STEP, copy, 0)
             receive(ext, after, (got0, got1))
-        fetch.wait()
         for h in range(2 * HALO):
             total = rim[h, 0, 0:1] * at_row(ext, fixes[h * NEI])
             for k in range(1, NEI):
@@ -380,7 +373,6 @@
     full = shape(2 * NB, 8, LANES)
     lam = shape(COMP, NB, LANES)
     scratch = [ext, ext, pltpu.VMEM((2 * NB, 8, LANES), F32)]
-    integers = [pltpu.SMEM((INTS,), jnp.int32), pltpu.SemaphoreType.DMA]
     if stage == 0:
         coef = shape(GROUPS, G_LISTED, 8, LANES)
         outs = [full, full, message, message, coef, coef]
@@ -392,9 +384,9 @@
     return pl.pallas_call(
         kernel,
         out_shape=outs,
-        in_specs=[VMEM] + ins,
+        in_specs=[SMEM] * 3 + ins,
         out_specs=[VMEM] * len(outs),
-        scratch_shapes=scratch + integers,
+        scratch_shapes=scratch,
         compiler_params=PARAMS,
     )
 
@@ -441,7 +433,7 @@
         out_shape=shape(GROUPS, G_LISTED + TILES, 8, LANES),
         in_specs=[SMEM] * 2 + [VMEM] * 5,
         out_specs=VMEM,
-        compiler_params=PARAMS,
+        compiler_params=pltpu.CompilerParams(vmem_limit_bytes=60 << 20),
         name="prep",
     )(
         live_count,
@@ -538,38 +530,33 @@
         ]
     ).reshape(-1) * 8
 
-    ints = jnp.concatenate([table, lists, fixes])
-
-    def following(after):
-        sent, _ = lax.optimization_barrier((packed, after))
-        packed_next = lax.ppermute(sent, "tm", [(t, t + 1) for t in range(rounds - 1)])
-        return pl.pallas_call(
-            spread_kernel,
-            out_shape=shape(2 * HALO, TILES, 8, LANES),
-            in_specs=[VMEM] * 2,
-            out_specs=VMEM,
-            compiler_params=PARAMS,
-            name="spread",
-        )(packed_next, listed)
+    packed, _ = lax.optimization_barrier((packed, got0))
+    packed_next = lax.ppermute(packed, "tm", [(t, t + 1) for t in range(rounds - 1)])
+    listed_next = pl.pallas_call(
+        spread_kernel,
+        out_shape=shape(2 * HALO, TILES, 8, LANES),
+        in_specs=[VMEM] * 2,
+        out_specs=VMEM,
+        compiler_params=PARAMS,
+        name="spread",
+    )(packed_next, listed)
 
     steps = [make_step(stage) for stage in range(4)]
     flag = (lax.axis_index("tm") == rounds - 1).astype(jnp.int32).reshape(1)
 
-    def slab(moved, listed_next=None, last=False):
+    def slab(moved, last=False):
         x, fixed, msg0, msg1, coef0, coef1 = steps[0](
-            ints, flag, *moved, *begun, rim, listed, mine, other
+            table, lists, fixes, flag, *moved, *begun, rim, listed, mine, other
         )
         got = exchange(msg0, msg1)
-        if listed_next is None and not last:
-            listed_next = following(msg0)
         x, fixed, msg0, msg1, late = steps[1](
-            ints, x, fixed, *got, rim, listed, coef0, coef1
+            table, lists, fixes, x, fixed, *got, rim, listed, coef0, coef1
         )
         got = exchange(msg0, msg1)
         if last:
-            (early,) = steps[3](ints, x, fixed, *got, rim, coef0, coef1)
+            (early,) = steps[3](table, lists, fixes, x, fixed, *got, rim, coef0, coef1)
             return early, late
-        return *steps[2](ints, x, fixed, *got, rim, listed_next, coef0, coef1), listed_next
+        return steps[2](table, lists, fixes, x, fixed, *got, rim, listed_next, coef0, coef1)
 
     def earlier(pairs):
         return [(t * count + d, (t - 1) * count + e) for t in range(1, rounds) for d, e in pairs]
@@ -577,17 +564,17 @@
     both = ("tm", "space")
     same = [(d, d) for d in range(count)]
 
-    def turn(step_index, carry):
-        msg0, msg1, early, listed_next = slab(*carry)
+    def turn(step_index, moved):
+        msg0, msg1, early = slab(moved)
         half = lax.ppermute(early, both, earlier(same))
         got0 = lax.ppermute(msg0, both, earlier(near))
         got1 = lax.ppermute(msg1, both, earlier(far))
         shared = lax.ppermute(half, "space", swap)
-        return (half, shared, got0, got1), listed_next
+        return (half, shared, got0, got1)
 
     moved = (start, start_other, got0[:MESSAGE], got1[:MESSAGE])
-    carry = turn(0, (moved, None))
-    moved, _ = lax.fori_loop(1, rounds - 1, turn, carry)
+    moved = turn(0, moved)
+    moved = lax.fori_loop(1, rounds - 1, turn, moved)
     early, late = slab(moved, last=True)
 
     shapes = shape_field.transpose(1, 0, 2)

time: 597 us -> 579 us (0.970)
  waiting for transfers between devices: 247 us -> 240 us
  local copies, waits for them, and re-layouts: 11.6 us -> 5.16 us
    ppermute x17, waiting for transfers between devices: 53.3 us -> 41.9 us  [exchange(): lax.ppermute(second, 'space', far)]
    unnamed x24 -> x14, local copies, waits for them, and re-layouts: 7.8 us -> 0.03 us
  transfers between devices with their start and end apart: 67 -> 67, of which waited for: 49 -> 50; matrix products, arithmetic and copies ran while one was open for 1% -> 1% of each run, Pallas kernels for 1% -> 3%
where the time goes in v6:
time: 579 us; the launch traced here: 576 us
  waiting for transfers between devices  240 us (41%)
  Pallas kernels  162 us (28%)
  starting transfers between devices  160 us (28%)
    ppermute x7, waiting for transfers between devices, turn(): half = lax.ppermute(early, both, earlier(same))  99.3 us
    ppermute x17, starting transfers between devices, exchange(): lax.ppermute(first, 'space', near)  72.7 us
    pallas_call x8, Pallas kernels, slab(): steps[0]  58.4 us
    pallas_call x8, Pallas kernels, slab(): steps[1](table, lists, fixes, x, fixed, *got, rim, listed, coef0, coef1)  51 us
    ppermute x17, waiting for transfers between devices, exchange(): lax.ppermute(first, 'space', near)  47.3 us
    ppermute x17, waiting for transfers between devices, exchange(): lax.ppermute(second, 'space', far)  41.9 us
    ppermute x7, waiting for transfers between devices, turn(): got0 = lax.ppermute(msg0, both, earlier(near))  41.1 us
    pallas_call x7, Pallas kernels, slab(): steps[2]  38.9 us
  transfers between devices with their start and end apart: 67, of which 50 were waited for; matrix products, arithmetic and copies ran while one was open for 1% of the time, Pallas kernels for 3%

profile of v6, /device:TPU:113, one launch (start us, length us, event | category | flops | bytes accessed | tf_op | source)
XLA Modules:
  0.0 575.8 jit_solution(2755933711117839108)
XLA Ops:
  9.0 6.3 %collective-permute-done.8 = s32[128,7]{0,1:T(8,128)S(1)} collective-permute-done((s32[128,7]{0,1:T(8,128)S(1)}, s32[128,7]{0,1:T(8,128)S(1)}, u32[]{:S(2)}, u32[]{:S(2)}) %collective-permute-start.8) | collective-permute-done | bytes 3616 | tf_op jit(solution)/shard_map/ppermute | solution.py:451
  38.5 7.2 %shard_map.122 = (f32[256,8,128]{2,1,0:T(8,128)S(1)}, f32[256,8,128]{2,1,0:T(8,128)S(1)}, f32[160,128]{1,0:T(8,128)S(1)}, f32[160,128]{1,0:T(8,128)S(1)}, f32[16...) custom-call(s32[1536]{0:T(1024)} %mul.50.table, s32[256]{0:T(256)} %reshape.64.lists, s32[192]{0:T(256)} %mul.57.fixes, ...), custom_call_target="tpu_custom_call" | custom-call | tf_op jit(solution)/shard_map/pallas_call | solution.py:548
  57.6 6.4 %shard_map.123 = (f32[256,8,128]{2,1,0:T(8,128)S(1)}, f32[256,8,128]{2,1,0:T(8,128)S(1)}, f32[160,128]{1,0:T(8,128)S(1)}, f32[160,128]{1,0:T(8,128)S(1)}, f32[5,128,128]{2,1,0:T(8,128)}) custom-call(s32[1536]{0:T(1024)} %mul.50.table, s32[256]{0:T(256)} %reshape.64.lists, s32[192]{0:T(256)} %mul.57.fixes, f32[256,8,128]{2,1,0:T(8,128)S(1)} %get-tuple-element.146.refs_0_, ...), custom_call_target="tpu_custom_call" | custom-call | tf_op jit(solution)/shard_map/pallas_call | solution.py:552
  83.3 10.2 %collective-permute-done.18 = f32[5,128,128]{2,1,0:T(8,128)} collective-permute-done((f32[5,128,128]{2,1,0:T(8,128)S(1)}, f32[5,128,128]{2,1,0:T(8,128)}, u32[]{:S(2)}, u32[]{:S(2)}) %collective-permute-start.18) | collective-permute-done | bytes 327712 | tf_op jit(solution)/shard_map/ppermute | solution.py:569
  102.8 412.5 %while.16 = (s32[]{:T(128)}, f32[5,128,128]{2,1,0:T(8,128)}, f32[5,128,128]{2,1,0:T(8,128)}, f32[160,128]{1,0:T(8,128)}, f32[160,128]{1,0:T(8,128)}, /*index=5*/...) while((s32[]{:T(128)}, f32[5,128,128]{2,1,0:T(8,128)}, ...), condition=%wide.region_7.8_spmd, body=%wide.region_6.7_spmd.sunk | while | flops 2 | bytes 9830921 | solution.py:577
  102.8 7.3 %eval_jaxpr.3 = (f32[256,8,128]{2,1,0:T(8,128)S(1)}, f32[256,8,128]{2,1,0:T(8,128)S(1)}, f32[160,128]{1,0:T(8,128)S(1)}, f32[160,128]{1,0:T(8,128)S(1)}, f32[16,...) custom-call(s32[1536]{0:T(1024)} %get-tuple-element.409.table, s32[256]{0:T(256)} %get-tuple-element.410.lists, ...), custom_call_target="tpu_custom_call" | custom-call | tf_op jit(solution)/shard_map/while/body/eval_jaxpr/pallas_call | solution.py:548
  110.1 6.5 %collective-permute-start = (f32[160,128]{1,0:T(8,128)S(1)}, f32[160,128]{1,0:T(8,128)S(1)}, u32[]{:S(2)}, u32[]{:S(2)}) collective-permute-start(f32[160,128]{1,0:T(8,128)S(1)} %get-tuple-element.355), channel_id=1, source_target_pairs={{1,2},{2,1},{3,4},{4,3},{5,6},{6,5},{7,8},{8,7},{9,10},{10,9},{11,... | collective-permute-start | bytes 245768 | tf_op jit(solution)/shard_map/while/body/eval_jaxpr/ppermute | solution.py:426
  123.9 6.5 %eval_jaxpr.4 = (f32[256,8,128]{2,1,0:T(8,128)S(1)}, f32[256,8,128]{2,1,0:T(8,128)S(1)}, f32[160,128]{1,0:T(8,128)S(1)}, f32[160,128]{1,0:T(8,128)S(1)}, f32[5,128,128]{2,1,0:T(8,128)}) custom-call(s32[1536]{0:T(1024)} %get-tuple-element.409.table, s32[256]{0:T(256)} %get-tuple-element.410.lists, s32[192]{0:T(256)} %get-tuple-element.411.fixes, ...), custom_call_target="tpu_custom_call" | custom-call | tf_op jit(solution)/shard_map/while/body/eval_jaxpr/pallas_call | solution.py:552
  147.5 15.7 %collective-permute-done.4 = f32[5,128,128]{2,1,0:T(8,128)} collective-permute-done((f32[5,128,128]{2,1,0:T(8,128)S(1)}, f32[5,128,128]{2,1,0:T(8,128)}, u32[]{:S(2)}, u32[]{:S(2)}) %collective-permute-start.4) | collective-permute-done | bytes 327712 | tf_op jit(solution)/shard_map/while/body/eval_jaxpr/ppermute | solution.py:569
  166.2 5.8 %collective-permute-done.6 = f32[160,128]{1,0:T(8,128)} collective-permute-done((f32[160,128]{1,0:T(8,128)S(1)}, f32[160,128]{1,0:T(8,128)}, u32[]{:S(2)}, u32[]{:S(2)}) %collective-permute-start.6) | collective-permute-done | bytes 81952 | tf_op jit(solution)/shard_map/while/body/eval_jaxpr/ppermute | solution.py:570
  172.0 7.3 %eval_jaxpr.3 = (f32[256,8,128]{2,1,0:T(8,128)S(1)}, f32[256,8,128]{2,1,0:T(8,128)S(1)}, f32[160,128]{1,0:T(8,128)S(1)}, f32[160,128]{1,0:T(8,128)S(1)}, f32[16,...) custom-call(s32[1536]{0:T(1024)} %get-tuple-element.409.table, s32[256]{0:T(256)} %get-tuple-element.410.lists, ...), custom_call_target="tpu_custom_call" | custom-call | tf_op jit(solution)/shard_map/while/body/eval_jaxpr/pallas_call | solution.py:548
  191.6 6.5 %eval_jaxpr.4 = (f32[256,8,128]{2,1,0:T(8,128)S(1)}, f32[256,8,128]{2,1,0:T(8,128)S(1)}, f32[160,128]{1,0:T(8,128)S(1)}, f32[160,128]{1,0:T(8,128)S(1)}, f32[5,128,128]{2,1,0:T(8,128)}) custom-call(s32[1536]{0:T(1024)} %get-tuple-element.409.table, s32[256]{0:T(256)} %get-tuple-element.410.lists, s32[192]{0:T(256)} %get-tuple-element.411.fixes, ...), custom_call_target="tpu_custom_call" | custom-call | tf_op jit(solution)/shard_map/while/body/eval_jaxpr/pallas_call | solution.py:552
  216.4 14.8 %collective-permute-done.4 = f32[5,128,128]{2,1,0:T(8,128)} collective-permute-done((f32[5,128,128]{2,1,0:T(8,128)S(1)}, f32[5,128,128]{2,1,0:T(8,128)}, u32[]{:S(2)}, u32[]{:S(2)}) %collective-permute-start.4) | collective-permute-done | bytes 327712 | tf_op jit(solution)/shard_map/while/body/eval_jaxpr/ppermute | solution.py:569
  234.8 5.9 %collective-permute-done.6 = f32[160,128]{1,0:T(8,128)} collective-permute-done((f32[160,128]{1,0:T(8,128)S(1)}, f32[160,128]{1,0:T(8,128)}, u32[]{:S(2)}, u32[]{:S(2)}) %collective-permute-start.6) | collective-permute-done | bytes 81952 | tf_op jit(solution)/shard_map/while/body/eval_jaxpr/ppermute | solution.py:570
  240.7 7.3 %eval_jaxpr.3 = (f32[256,8,128]{2,1,0:T(8,128)S(1)}, f32[256,8,128]{2,1,0:T(8,128)S(1)}, f32[160,128]{1,0:T(8,128)S(1)}, f32[160,128]{1,0:T(8,128)S(1)}, f32[16,...) custom-call(s32[1536]{0:T(1024)} %get-tuple-element.409.table, s32[256]{0:T(256)} %get-tuple-element.410.lists, ...), custom_call_target="tpu_custom_call" | custom-call | tf_op jit(solution)/shard_map/while/body/eval_jaxpr/pallas_call | solution.py:548
  260.2 6.5 %eval_jaxpr.4 = (f32[256,8,128]{2,1,0:T(8,128)S(1)}, f32[256,8,128]{2,1,0:T(8,128)S(1)}, f32[160,128]{1,0:T(8,128)S(1)}, f32[160,128]{1,0:T(8,128)S(1)}, f32[5,128,128]{2,1,0:T(8,128)}) custom-call(s32[1536]{0:T(1024)} %get-tuple-element.409.table, s32[256]{0:T(256)} %get-tuple-element.410.lists, s32[192]{0:T(256)} %get-tuple-element.411.fixes, ...), custom_call_target="tpu_custom_call" | custom-call | tf_op jit(solution)/shard_map/while/body/eval_jaxpr/pallas_call | solution.py:552
  285.1 14.7 %collective-permute-done.4 = f32[5,128,128]{2,1,0:T(8,128)} collective-permute-done((f32[5,128,128]{2,1,0:T(8,128)S(1)}, f32[5,128,128]{2,1,0:T(8,128)}, u32[]{:S(2)}, u32[]{:S(2)}) %collective-permute-start.4) | collective-permute-done | bytes 327712 | tf_op jit(solution)/shard_map/while/body/eval_jaxpr/ppermute | solution.py:569
  303.4 5.9 %collective-permute-done.6 = f32[160,128]{1,0:T(8,128)} collective-permute-done((f32[160,128]{1,0:T(8,128)S(1)}, f32[160,128]{1,0:T(8,128)}, u32[]{:S(2)}, u32[]{:S(2)}) %collective-permute-start.6) | collective-permute-done | bytes 81952 | tf_op jit(solution)/shard_map/while/body/eval_jaxpr/ppermute | solution.py:570
  309.4 7.3 %eval_jaxpr.3 = (f32[256,8,128]{2,1,0:T(8,128)S(1)}, f32[256,8,128]{2,1,0:T(8,128)S(1)}, f32[160,128]{1,0:T(8,128)S(1)}, f32[160,128]{1,0:T(8,128)S(1)}, f32[16,...) custom-call(s32[1536]{0:T(1024)} %get-tuple-element.409.table, s32[256]{0:T(256)} %get-tuple-element.410.lists, ...), custom_call_target="tpu_custom_call" | custom-call | tf_op jit(solution)/shard_map/while/body/eval_jaxpr/pallas_call | solution.py:548
  328.9 6.5 %eval_jaxpr.4 = (f32[256,8,128]{2,1,0:T(8,128)S(1)}, f32[256,8,128]{2,1,0:T(8,128)S(1)}, f32[160,128]{1,0:T(8,128)S(1)}, f32[160,128]{1,0:T(8,128)S(1)}, f32[5,128,128]{2,1,0:T(8,128)}) custom-call(s32[1536]{0:T(1024)} %get-tuple-element.409.table, s32[256]{0:T(256)} %get-tuple-element.410.lists, s32[192]{0:T(256)} %get-tuple-element.411.fixes, ...), custom_call_target="tpu_custom_call" | custom-call | tf_op jit(solution)/shard_map/while/body/eval_jaxpr/pallas_call | solution.py:552
  353.8 14.7 %collective-permute-done.4 = f32[5,128,128]{2,1,0:T(8,128)} collective-permute-done((f32[5,128,128]{2,1,0:T(8,128)S(1)}, f32[5,128,128]{2,1,0:T(8,128)}, u32[]{:S(2)}, u32[]{:S(2)}) %collective-permute-start.4) | collective-permute-done | bytes 327712 | tf_op jit(solution)/shard_map/while/body/eval_jaxpr/ppermute | solution.py:569
  372.1 5.9 %collective-permute-done.6 = f32[160,128]{1,0:T(8,128)} collective-permute-done((f32[160,128]{1,0:T(8,128)S(1)}, f32[160,128]{1,0:T(8,128)}, u32[]{:S(2)}, u32[]{:S(2)}) %collective-permute-start.6) | collective-permute-done | bytes 81952 | tf_op jit(solution)/shard_map/while/body/eval_jaxpr/ppermute | solution.py:570
  378.0 7.3 %eval_jaxpr.3 = (f32[256,8,128]{2,1,0:T(8,128)S(1)}, f32[256,8,128]{2,1,0:T(8,128)S(1)}, f32[160,128]{1,0:T(8,128)S(1)}, f32[160,128]{1,0:T(8,128)S(1)}, f32[16,...) custom-call(s32[1536]{0:T(1024)} %get-tuple-element.409.table, s32[256]{0:T(256)} %get-tuple-element.410.lists, ...), custom_call_target="tpu_custom_call" | custom-call | tf_op jit(solution)/shard_map/while/body/eval_jaxpr/pallas_call | solution.py:548
  397.5 6.5 %eval_jaxpr.4 = (f32[256,8,128]{2,1,0:T(8,128)S(1)}, f32[256,8,128]{2,1,0:T(8,128)S(1)}, f32[160,128]{1,0:T(8,128)S(1)}, f32[160,128]{1,0:T(8,128)S(1)}, f32[5,128,128]{2,1,0:T(8,128)}) custom-call(s32[1536]{0:T(1024)} %get-tuple-element.409.table, s32[256]{0:T(256)} %get-tuple-element.410.lists, s32[192]{0:T(256)} %get-tuple-element.411.fixes, ...), custom_call_target="tpu_custom_call" | custom-call | tf_op jit(solution)/shard_map/while/body/eval_jaxpr/pallas_call | solution.py:552
  422.4 14.7 %collective-permute-done.4 = f32[5,128,128]{2,1,0:T(8,128)} collective-permute-done((f32[5,128,128]{2,1,0:T(8,128)S(1)}, f32[5,128,128]{2,1,0:T(8,128)}, u32[]{:S(2)}, u32[]{:S(2)}) %collective-permute-start.4) | collective-permute-done | bytes 327712 | tf_op jit(solution)/shard_map/while/body/eval_jaxpr/ppermute | solution.py:569
  440.7 5.9 %collective-permute-done.6 = f32[160,128]{1,0:T(8,128)} collective-permute-done((f32[160,128]{1,0:T(8,128)S(1)}, f32[160,128]{1,0:T(8,128)}, u32[]{:S(2)}, u32[]{:S(2)}) %collective-permute-start.6) | collective-permute-done | bytes 81952 | tf_op jit(solution)/shard_map/while/body/eval_jaxpr/ppermute | solution.py:570
  446.6 7.3 %eval_jaxpr.3 = (f32[256,8,128]{2,1,0:T(8,128)S(1)}, f32[256,8,128]{2,1,0:T(8,128)S(1)}, f32[160,128]{1,0:T(8,128)S(1)}, f32[160,128]{1,0:T(8,128)S(1)}, f32[16,...) custom-call(s32[1536]{0:T(1024)} %get-tuple-element.409.table, s32[256]{0:T(256)} %get-tuple-element.410.lists, ...), custom_call_target="tpu_custom_call" | custom-call | tf_op jit(solution)/shard_map/while/body/eval_jaxpr/pallas_call | solution.py:548
  466.1 6.5 %eval_jaxpr.4 = (f32[256,8,128]{2,1,0:T(8,128)S(1)}, f32[256,8,128]{2,1,0:T(8,128)S(1)}, f32[160,128]{1,0:T(8,128)S(1)}, f32[160,128]{1,0:T(8,128)S(1)}, f32[5,128,128]{2,1,0:T(8,128)}) custom-call(s32[1536]{0:T(1024)} %get-tuple-element.409.table, s32[256]{0:T(256)} %get-tuple-element.410.lists, s32[192]{0:T(256)} %get-tuple-element.411.fixes, ...), custom_call_target="tpu_custom_call" | custom-call | tf_op jit(solution)/shard_map/while/body/eval_jaxpr/pallas_call | solution.py:552
  491.0 14.7 %collective-permute-done.4 = f32[5,128,128]{2,1,0:T(8,128)} collective-permute-done((f32[5,128,128]{2,1,0:T(8,128)S(1)}, f32[5,128,128]{2,1,0:T(8,128)}, u32[]{:S(2)}, u32[]{:S(2)}) %collective-permute-start.4) | collective-permute-done | bytes 327712 | tf_op jit(solution)/shard_map/while/body/eval_jaxpr/ppermute | solution.py:569
  509.3 5.9 %collective-permute-done.6 = f32[160,128]{1,0:T(8,128)} collective-permute-done((f32[160,128]{1,0:T(8,128)S(1)}, f32[160,128]{1,0:T(8,128)}, u32[]{:S(2)}, u32[]{:S(2)}) %collective-permute-start.6) | collective-permute-done | bytes 81952 | tf_op jit(solution)/shard_map/while/body/eval_jaxpr/ppermute | solution.py:570
  515.3 7.3 %shard_map.125 = (f32[256,8,128]{2,1,0:T(8,128)S(1)}, f32[256,8,128]{2,1,0:T(8,128)S(1)}, f32[160,128]{1,0:T(8,128)S(1)}, f32[160,128]{1,0:T(8,128)S(1)}, f32[16...) custom-call(s32[1536]{0:T(1024)} %mul.50.table, s32[256]{0:T(256)} %reshape.64.lists, s32[192]{0:T(256)} %mul.57.fixes, ...), custom_call_target="tpu_custom_call" | custom-call | tf_op jit(solution)/shard_map/pallas_call | solution.py:548
  559.1 11.1 %all-to-all-start = ((f32[8,1,128]{2,1,0:T(1,128)}), f32[8,1,128]{2,1,0:T(1,128)S(1)}, u32[]{:S(2)}, u32[]{:S(2)}) async-start(f32[8,1,128]{2,1,0:T(1,128)} %broadcast_in_dim.103), calls=%async_computation | async-start | bytes 8192 | tf_op jit(solution)/shard_map/all_to_all | solution.py:586
  (207 shorter events, 311.1 us)
Async XLA Ops:
  7.5 9.7 %collective-permute-start.10 = (f32[16,65,8,128]{3,2,1,0:T(8,128)}, f32[16,65,8,128]{3,2,1,0:T(8,128)}, u32[]{:S(2)}, u32[]{:S(2)}) collective-permute-start(f32[16,65,8,128]{3,2,1,0:T(8,128)} %prep.1.mine.refs_11_), channel_id=1, source_target_pairs={{0,1},{1,0},{2,3},{3,2},{4,5},{5,4},{6,7},{7,6},{8,9},{9,8},{10,11... | collective-permute-start | bytes 12779528 | tf_op jit(solution)/shard_map/ppermute | solution.py:447
  8.5 10.2 %collective-permute-start.9 = (f32[5,128,128]{2,1,0:T(8,128)S(1)}, f32[5,128,128]{2,1,0:T(8,128)}, u32[]{:S(2)}, u32[]{:S(2)}) collective-permute-start(f32[5,128,128]{2,1,0:T(8,128)S(1)} %multiply_bitcast_fusion.mine.refs_1_.refs_5_), channel_id=1, source_target_pairs={{0,1},{1,0},{2,3},{3,2},{4,5},{5,4},{6,7},{7,6},{8,9},{9,8},{10,11... | collective-permute-start | bytes 983048 | tf_op jit(solution)/shard_map/ppermute | solution.py:497
  20.2 10.4 %collective-permute-start.11 = (f32[352,128]{1,0:T(8,128)S(1)}, f32[352,128]{1,0:T(8,128)S(1)}, u32[]{:S(2)}, u32[]{:S(2)}) collective-permute-start(f32[352,128]{1,0:T(8,128)S(1)} %get-tuple-element.142), channel_id=1, source_target_pairs={{1,2},{2,1},{3,4},{4,3},{5,6},{6,5},{7,8},{8,7},{9,10},{10,9},{11,... | collective-permute-start | bytes 540680 | tf_op jit(solution)/shard_map/ppermute | solution.py:426
  25.0 9.7 %collective-permute-start.12 = (f32[352,128]{1,0:T(8,128)S(1)}, f32[352,128]{1,0:T(8,128)}, u32[]{:S(2)}, u32[]{:S(2)}) collective-permute-start(f32[352,128]{1,0:T(8,128)S(1)} %get-tuple-element.143), channel_id=1, source_target_pairs={{0,3},{2,5},{3,0},{4,7},{5,2},{6,9},{7,4},{8,11},{9,6},{10,13},{11... | collective-permute-start | bytes 540680 | tf_op jit(solution)/shard_map/ppermute | solution.py:426
  30.6 39.8 %collective-permute-start.17 = (f32[32,40,128]{2,1,0:T(8,128)S(1)}, f32[32,40,128]{2,1,0:T(8,128)S(1)}, u32[]{:S(2)}, u32[]{:S(2)}) collective-permute-start(f32[32,40,128]{2,1,0:T(8,128)S(1)} %get-tuple-element.157), channel_id=1, source_target_pairs={{0,32},{32,64},{64,96},{96,128},{128,160},{160,192},{192,224},{1,3... | collective-permute-start | bytes 1966088 | tf_op jit(solution)/shard_map/ppermute | solution.py:534
  45.7 9.4 %collective-permute-start.13 = (f32[160,128]{1,0:T(8,128)S(1)}, f32[160,128]{1,0:T(8,128)S(1)}, u32[]{:S(2)}, u32[]{:S(2)}) collective-permute-start(f32[160,128]{1,0:T(8,128)S(1)} %get-tuple-element.148), channel_id=1, source_target_pairs={{1,2},{2,1},{3,4},{4,3},{5,6},{6,5},{7,8},{8,7},{9,10},{10,9},{11,... | collective-permute-start | bytes 245768 | tf_op jit(solution)/shard_map/ppermute | solution.py:426
  63.9 9.4 %collective-permute-start.15 = (f32[160,128]{1,0:T(8,128)S(1)}, f32[160,128]{1,0:T(8,128)S(1)}, u32[]{:S(2)}, u32[]{:S(2)}) collective-permute-start(f32[160,128]{1,0:T(8,128)S(1)} %get-tuple-element.154), channel_id=1, source_target_pairs={{1,2},{2,1},{3,4},{4,3},{5,6},{6,5},{7,8},{8,7},{9,10},{10,9},{11,... | collective-permute-start | bytes 245768 | tf_op jit(solution)/shard_map/ppermute | solution.py:426
  82.0 11.5 %collective-permute-start.18 = (f32[5,128,128]{2,1,0:T(8,128)S(1)}, f32[5,128,128]{2,1,0:T(8,128)}, u32[]{:S(2)}, u32[]{:S(2)}) collective-permute-start(f32[5,128,128]{2,1,0:T(8,128)S(1)} %get-tuple-element.158), channel_id=1, source_target_pairs={{32,0},{33,1},{34,2},{35,3},{36,4},{37,5},{38,6},{39,7},{40,8},{41... | collective-permute-start | bytes 983048 | tf_op jit(solution)/shard_map/ppermute | solution.py:569
  110.1 9.4 %collective-permute-start = (f32[160,128]{1,0:T(8,128)S(1)}, f32[160,128]{1,0:T(8,128)S(1)}, u32[]{:S(2)}, u32[]{:S(2)}) collective-permute-start(f32[160,128]{1,0:T(8,128)S(1)} %get-tuple-element.355), channel_id=1, source_target_pairs={{1,2},{2,1},{3,4},{4,3},{5,6},{6,5},{7,8},{8,7},{9,10},{10,9},{11,... | collective-permute-start | bytes 245768 | tf_op jit(solution)/shard_map/while/body/eval_jaxpr/ppermute | solution.py:426
  130.4 9.4 %collective-permute-start.2 = (f32[160,128]{1,0:T(8,128)S(1)}, f32[160,128]{1,0:T(8,128)S(1)}, u32[]{:S(2)}, u32[]{:S(2)}) collective-permute-start(f32[160,128]{1,0:T(8,128)S(1)} %get-tuple-element.361), channel_id=1, source_target_pairs={{1,2},{2,1},{3,4},{4,3},{5,6},{6,5},{7,8},{8,7},{9,10},{10,9},{11,... | collective-permute-start | bytes 245768 | tf_op jit(solution)/shard_map/while/body/eval_jaxpr/ppermute | solution.py:426
  146.2 17.0 %collective-permute-start.4 = (f32[5,128,128]{2,1,0:T(8,128)S(1)}, f32[5,128,128]{2,1,0:T(8,128)}, u32[]{:S(2)}, u32[]{:S(2)}) collective-permute-start(f32[5,128,128]{2,1,0:T(8,128)S(1)} %get-tuple-element.363), channel_id=1, source_target_pairs={{32,0},{33,1},{34,2},{35,3},{36,4},{37,5},{38,6},{39,7},{40,8},{41... | collective-permute-start | bytes 983048 | tf_op jit(solution)/shard_map/while/body/eval_jaxpr/ppermute | solution.py:569
  179.3 9.4 %collective-permute-start = (f32[160,128]{1,0:T(8,128)S(1)}, f32[160,128]{1,0:T(8,128)S(1)}, u32[]{:S(2)}, u32[]{:S(2)}) collective-permute-start(f32[160,128]{1,0:T(8,128)S(1)} %get-tuple-element.355), channel_id=1, source_target_pairs={{1,2},{2,1},{3,4},{4,3},{5,6},{6,5},{7,8},{8,7},{9,10},{10,9},{11,... | collective-permute-start | bytes 245768 | tf_op jit(solution)/shard_map/while/body/eval_jaxpr/ppermute | solution.py:426
  198.1 9.4 %collective-permute-start.2 = (f32[160,128]{1,0:T(8,128)S(1)}, f32[160,128]{1,0:T(8,128)S(1)}, u32[]{:S(2)}, u32[]{:S(2)}) collective-permute-start(f32[160,128]{1,0:T(8,128)S(1)} %get-tuple-element.361), channel_id=1, source_target_pairs={{1,2},{2,1},{3,4},{4,3},{5,6},{6,5},{7,8},{8,7},{9,10},{10,9},{11,... | collective-permute-start | bytes 245768 | tf_op jit(solution)/shard_map/while/body/eval_jaxpr/ppermute | solution.py:426
  215.1 16.1 %collective-permute-start.4 = (f32[5,128,128]{2,1,0:T(8,128)S(1)}, f32[5,128,128]{2,1,0:T(8,128)}, u32[]{:S(2)}, u32[]{:S(2)}) collective-permute-start(f32[5,128,128]{2,1,0:T(8,128)S(1)} %get-tuple-element.363), channel_id=1, source_target_pairs={{32,0},{33,1},{34,2},{35,3},{36,4},{37,5},{38,6},{39,7},{40,8},{41... | collective-permute-start | bytes 983048 | tf_op jit(solution)/shard_map/while/body/eval_jaxpr/ppermute | solution.py:569
  231.1 9.6 %collective-permute-start.5 = (f32[5,128,128]{2,1,0:T(8,128)}, f32[5,128,128]{2,1,0:T(8,128)}, u32[]{:S(2)}, u32[]{:S(2)}) collective-permute-start(f32[5,128,128]{2,1,0:T(8,128)} %collective-permute-done.4), channel_id=1, source_target_pairs={{0,1},{1,0},{2,3},{3,2},{4,5},{5,4},{6,7},{7,6},{8,9},{9,8},{10,11... | collective-permute-start | bytes 983048 | tf_op jit(solution)/shard_map/while/body/eval_jaxpr/ppermute | solution.py:572
  248.1 9.4 %collective-permute-start = (f32[160,128]{1,0:T(8,128)S(1)}, f32[160,128]{1,0:T(8,128)S(1)}, u32[]{:S(2)}, u32[]{:S(2)}) collective-permute-start(f32[160,128]{1,0:T(8,128)S(1)} %get-tuple-element.355), channel_id=1, source_target_pairs={{1,2},{2,1},{3,4},{4,3},{5,6},{6,5},{7,8},{8,7},{9,10},{10,9},{11,... | collective-permute-start | bytes 245768 | tf_op jit(solution)/shard_map/while/body/eval_jaxpr/ppermute | solution.py:426
  266.7 9.4 %collective-permute-start.2 = (f32[160,128]{1,0:T(8,128)S(1)}, f32[160,128]{1,0:T(8,128)S(1)}, u32[]{:S(2)}, u32[]{:S(2)}) collective-permute-start(f32[160,128]{1,0:T(8,128)S(1)} %get-tuple-element.361), channel_id=1, source_target_pairs={{1,2},{2,1},{3,4},{4,3},{5,6},{6,5},{7,8},{8,7},{9,10},{10,9},{11,... | collective-permute-start | bytes 245768 | tf_op jit(solution)/shard_map/while/body/eval_jaxpr/ppermute | solution.py:426
  283.8 16.0 %collective-permute-start.4 = (f32[5,128,128]{2,1,0:T(8,128)S(1)}, f32[5,128,128]{2,1,0:T(8,128)}, u32[]{:S(2)}, u32[]{:S(2)}) collective-permute-start(f32[5,128,128]{2,1,0:T(8,128)S(1)} %get-tuple-element.363), channel_id=1, source_target_pairs={{32,0},{33,1},{34,2},{35,3},{36,4},{37,5},{38,6},{39,7},{40,8},{41... | collective-permute-start | bytes 983048 | tf_op jit(solution)/shard_map/while/body/eval_jaxpr/ppermute | solution.py:569
  299.8 9.6 %collective-permute-start.5 = (f32[5,128,128]{2,1,0:T(8,128)}, f32[5,128,128]{2,1,0:T(8,128)}, u32[]{:S(2)}, u32[]{:S(2)}) collective-permute-start(f32[5,128,128]{2,1,0:T(8,128)} %collective-permute-done.4), channel_id=1, source_target_pairs={{0,1},{1,0},{2,3},{3,2},{4,5},{5,4},{6,7},{7,6},{8,9},{9,8},{10,11... | collective-permute-start | bytes 983048 | tf_op jit(solution)/shard_map/while/body/eval_jaxpr/ppermute | solution.py:572
  316.7 9.4 %collective-permute-start = (f32[160,128]{1,0:T(8,128)S(1)}, f32[160,128]{1,0:T(8,128)S(1)}, u32[]{:S(2)}, u32[]{:S(2)}) collective-permute-start(f32[160,128]{1,0:T(8,128)S(1)} %get-tuple-element.355), channel_id=1, source_target_pairs={{1,2},{2,1},{3,4},{4,3},{5,6},{6,5},{7,8},{8,7},{9,10},{10,9},{11,... | collective-permute-start | bytes 245768 | tf_op jit(solution)/shard_map/while/body/eval_jaxpr/ppermute | solution.py:426
  335.4 9.4 %collective-permute-start.2 = (f32[160,128]{1,0:T(8,128)S(1)}, f32[160,128]{1,0:T(8,128)S(1)}, u32[]{:S(2)}, u32[]{:S(2)}) collective-permute-start(f32[160,128]{1,0:T(8,128)S(1)} %get-tuple-element.361), channel_id=1, source_target_pairs={{1,2},{2,1},{3,4},{4,3},{5,6},{6,5},{7,8},{8,7},{9,10},{10,9},{11,... | collective-permute-start | bytes 245768 | tf_op jit(solution)/shard_map/while/body/eval_jaxpr/ppermute | solution.py:426
  352.5 16.0 %collective-permute-start.4 = (f32[5,128,128]{2,1,0:T(8,128)S(1)}, f32[5,128,128]{2,1,0:T(8,128)}, u32[]{:S(2)}, u32[]{:S(2)}) collective-permute-start(f32[5,128,128]{2,1,0:T(8,128)S(1)} %get-tuple-element.363), channel_id=1, source_target_pairs={{32,0},{33,1},{34,2},{35,3},{36,4},{37,5},{38,6},{39,7},{40,8},{41... | collective-permute-start | bytes 983048 | tf_op jit(solution)/shard_map/while/body/eval_jaxpr/ppermute | solution.py:569
  368.4 9.6 %collective-permute-start.5 = (f32[5,128,128]{2,1,0:T(8,128)}, f32[5,128,128]{2,1,0:T(8,128)}, u32[]{:S(2)}, u32[]{:S(2)}) collective-permute-start(f32[5,128,128]{2,1,0:T(8,128)} %collective-permute-done.4), channel_id=1, source_target_pairs={{0,1},{1,0},{2,3},{3,2},{4,5},{5,4},{6,7},{7,6},{8,9},{9,8},{10,11... | collective-permute-start | bytes 983048 | tf_op jit(solution)/shard_map/while/body/eval_jaxpr/ppermute | solution.py:572
  385.3 9.4 %collective-permute-start = (f32[160,128]{1,0:T(8,128)S(1)}, f32[160,128]{1,0:T(8,128)S(1)}, u32[]{:S(2)}, u32[]{:S(2)}) collective-permute-start(f32[160,128]{1,0:T(8,128)S(1)} %get-tuple-element.355), channel_id=1, source_target_pairs={{1,2},{2,1},{3,4},{4,3},{5,6},{6,5},{7,8},{8,7},{9,10},{10,9},{11,... | collective-permute-start | bytes 245768 | tf_op jit(solution)/shard_map/while/body/eval_jaxpr/ppermute | solution.py:426
  421.1 16.0 %collective-permute-start.4 = (f32[5,128,128]{2,1,0:T(8,128)S(1)}, f32[5,128,128]{2,1,0:T(8,128)}, u32[]{:S(2)}, u32[]{:S(2)}) collective-permute-start(f32[5,128,128]{2,1,0:T(8,128)S(1)} %get-tuple-element.363), channel_id=1, source_target_pairs={{32,0},{33,1},{34,2},{35,3},{36,4},{37,5},{38,6},{39,7},{40,8},{41... | collective-permute-start | bytes 983048 | tf_op jit(solution)/shard_map/while/body/eval_jaxpr/ppermute | solution.py:569
  437.1 9.6 %collective-permute-start.5 = (f32[5,128,128]{2,1,0:T(8,128)}, f32[5,128,128]{2,1,0:T(8,128)}, u32[]{:S(2)}, u32[]{:S(2)}) collective-permute-start(f32[5,128,128]{2,1,0:T(8,128)} %collective-permute-done.4), channel_id=1, source_target_pairs={{0,1},{1,0},{2,3},{3,2},{4,5},{5,4},{6,7},{7,6},{8,9},{9,8},{10,11... | collective-permute-start | bytes 983048 | tf_op jit(solution)/shard_map/while/body/eval_jaxpr/ppermute | solution.py:572
  454.0 9.4 %collective-permute-start = (f32[160,128]{1,0:T(8,128)S(1)}, f32[160,128]{1,0:T(8,128)S(1)}, u32[]{:S(2)}, u32[]{:S(2)}) collective-permute-start(f32[160,128]{1,0:T(8,128)S(1)} %get-tuple-element.355), channel_id=1, source_target_pairs={{1,2},{2,1},{3,4},{4,3},{5,6},{6,5},{7,8},{8,7},{9,10},{10,9},{11,... | collective-permute-start | bytes 245768 | tf_op jit(solution)/shard_map/while/body/eval_jaxpr/ppermute | solution.py:426
  489.7 16.0 %collective-permute-start.4 = (f32[5,128,128]{2,1,0:T(8,128)S(1)}, f32[5,128,128]{2,1,0:T(8,128)}, u32[]{:S(2)}, u32[]{:S(2)}) collective-permute-start(f32[5,128,128]{2,1,0:T(8,128)S(1)} %get-tuple-element.363), channel_id=1, source_target_pairs={{32,0},{33,1},{34,2},{35,3},{36,4},{37,5},{38,6},{39,7},{40,8},{41... | collective-permute-start | bytes 983048 | tf_op jit(solution)/shard_map/while/body/eval_jaxpr/ppermute | solution.py:569
  505.7 9.6 %collective-permute-start.5 = (f32[5,128,128]{2,1,0:T(8,128)}, f32[5,128,128]{2,1,0:T(8,128)}, u32[]{:S(2)}, u32[]{:S(2)}) collective-permute-start(f32[5,128,128]{2,1,0:T(8,128)} %collective-permute-done.4), channel_id=1, source_target_pairs={{0,1},{1,0},{2,3},{3,2},{4,5},{5,4},{6,7},{7,6},{8,9},{9,8},{10,11... | collective-permute-start | bytes 983048 | tf_op jit(solution)/shard_map/while/body/eval_jaxpr/ppermute | solution.py:572
  522.6 9.4 %collective-permute-start.22 = (f32[160,128]{1,0:T(8,128)S(1)}, f32[160,128]{1,0:T(8,128)S(1)}, u32[]{:S(2)}, u32[]{:S(2)}) collective-permute-start(f32[160,128]{1,0:T(8,128)S(1)} %get-tuple-element.167), channel_id=1, source_target_pairs={{1,2},{2,1},{3,4},{4,3},{5,6},{6,5},{7,8},{8,7},{9,10},{10,9},{11,... | collective-permute-start | bytes 245768 | tf_op jit(solution)/shard_map/ppermute | solution.py:426
  540.5 9.4 %collective-permute-start.24 = (f32[160,128]{1,0:T(8,128)S(1)}, f32[160,128]{1,0:T(8,128)S(1)}, u32[]{:S(2)}, u32[]{:S(2)}) collective-permute-start(f32[160,128]{1,0:T(8,128)S(1)} %get-tuple-element.173), channel_id=1, source_target_pairs={{1,2},{2,1},{3,4},{4,3},{5,6},{6,5},{7,8},{8,7},{9,10},{10,9},{11,... | collective-permute-start | bytes 245768 | tf_op jit(solution)/shard_map/ppermute | solution.py:426
  559.1 16.2 %all-to-all-start = ((f32[8,1,128]{2,1,0:T(1,128)}), f32[8,1,128]{2,1,0:T(1,128)S(1)}, u32[]{:S(2)}, u32[]{:S(2)}) async-start(f32[8,1,128]{2,1,0:T(1,128)} %broadcast_in_dim.103), calls=%async_computation | async-start | bytes 8192 | tf_op jit(solution)/shard_map/all_to_all | solution.py:586
  (48 other events, 447.8 us)
